TPU v7x, 256 devices: a whole 4x4x8 slice. The times are simulated.
256 devices in a mesh: gx: 8 (over x, core), gy: 8 (over z), gz: 4 (over y).
Axes of the slice: x: 4, y: 4, z: 8, core: 2. Of those that a mesh axis runs over, the one named last changes fastest.
Arguments:
- fields: float32 [1, 256, 256, 512], P(None, 'gx', 'gy', 'gz'), may hold values from -13 to 13
- exponents: int32 [5], replicated, may hold values from -5 to -1
Outputs:
- coefficients: float32 [1, 256, 256, 512], P(None, 'gx', 'gy', 'gz')
- statistics: float32 [2, 1, 5], replicated
All inputs are finite; a program needn't handle non-finite values.
Results may differ from a plain program's by a relative error of at most 0.0003.
Values sent between devices are 32-bit elements; how exact they have to be, the bound alone decides.
No kernel may reach another device: no remote copies, remote signals or barrier semaphores. Data moves between devices by JAX's collectives and lax.ppermute only.
A program may use at most 64 MiB of HBM per device.

v0:
```python
import jax
import jax.numpy as jnp
from jax import lax
from jax.sharding import Mesh
from jax.sharding import PartitionSpec as P

FINE = 3
COARSE = 2
GX = ("gx_0", "gx_1")
GX_GY_GZ = ("gx_0", "gx_1", "gy", "gz")


def shifted(block, axis, distance):
    devices = range(lax.axis_size(axis))
    route = [((i - distance) % len(devices), i) for i in devices]
    return lax.ppermute(block, axis, route)


def over_axes(x, axes):
    for axis in axes:
        x = lax.psum(x, axis)
    return x


def split_pair(values, axis_dim):
    length = values.shape[axis_dim]
    even_part = lax.slice_in_dim(values, 0, length, 2, axis_dim)
    odd_part = lax.slice_in_dim(values, 1, length, 2, axis_dim)
    return (even_part, odd_part)


def finish(values, even_part, detail, before_rim, axis_dim):
    half_length = detail.shape[axis_dim]
    behind = jnp.concatenate(
        (before_rim, lax.slice_in_dim(detail, 0, half_length - 1, 1, axis_dim)), axis_dim
    )
    smooth = even_part + 0.25 * (behind + detail)
    return jnp.stack((smooth, detail), axis_dim + 1).reshape(values.shape)


def lift_shifts(values, axis_dim, fetch_ahead, fetch_behind):
    even_part, odd_part = split_pair(values, axis_dim)
    half_length = even_part.shape[axis_dim]
    first_even = lax.slice_in_dim(even_part, 0, 1, 1, axis_dim)
    after_rim = fetch_ahead(first_even)
    ahead_even = jnp.concatenate(
        (lax.slice_in_dim(even_part, 1, half_length, 1, axis_dim), after_rim), axis_dim
    )
    detail = odd_part - 0.5 * (even_part + ahead_even)
    before_rim = fetch_behind(lax.slice_in_dim(detail, half_length - 1, half_length, 1, axis_dim))
    return finish(values, even_part, detail, before_rim, axis_dim)


def detail_mask(shape):
    parity_flags = [jnp.arange(shape[index_dim]) % 2 == 0 for index_dim in (1, 2, 3)]
    smooth_cells = (
        parity_flags[0][:, None, None]
        & parity_flags[1][None, :, None]
        & parity_flags[2][None, None, :]
    )
    return jnp.where(smooth_cells, 0.0, 1.0).astype(jnp.float32)[None]


def shrink(values, exponent):
    thresh = jnp.exp2(exponent.astype(jnp.float32))
    return jnp.sign(values) * jnp.maximum(jnp.abs(values) - thresh, 0.0)


def shards(fields, exponents):
    lifters = (
        lambda values: lift_shifts(
            values,
            1,
            lambda boundary: shifted(boundary, GX, -1),
            lambda boundary: shifted(boundary, GX, 1),
        ),
        lambda values: lift_shifts(
            values,
            2,
            lambda boundary: shifted(boundary, "gy", -1),
            lambda boundary: shifted(boundary, "gy", 1),
        ),
        lambda values: lift_shifts(
            values,
            3,
            lambda boundary: shifted(boundary, "gz", -1),
            lambda boundary: shifted(boundary, "gz", 1),
        ),
    )
    grid_x = lax.axis_size(GX)
    grid_y = lax.axis_size("gy")
    grid_z = lax.axis_size("gz")
    cell_total = fields.shape[1] * fields.shape[2] * fields.shape[3] * grid_x * grid_y * grid_z
    sharded_levels = FINE + COARSE
    current = fields
    layers = []
    energies = []
    retained = []
    for layer_index in range(sharded_levels):
        for lifter in lifters:
            current = lifter(current)
        masking = detail_mask(current.shape)
        shrunk = shrink(current, exponents[layer_index])
        level_count = 7.0 * cell_total / 8 ** (layer_index + 1)
        local_energy = jnp.sum(current * current * masking, axis=(1, 2, 3))
        local_kept = jnp.sum(jnp.abs(shrunk) * masking, axis=(1, 2, 3))
        summed_energy, summed_kept = (
            over_axes(local_energy, GX_GY_GZ),
            over_axes(local_kept, GX_GY_GZ),
        )
        energies.append(summed_energy / level_count)
        retained.append(summed_kept / level_count)
        layers.append(shrunk)
        current = current[:, ::2, ::2, ::2]
    result = current
    for shrunk in reversed(layers):
        result = shrunk.at[:, ::2, ::2, ::2].set(result)
    statistics = jnp.stack((jnp.stack(energies, 1), jnp.stack(retained, 1)))
    return (result, statistics)


def solution(mesh):
    torus = Mesh(
        mesh.devices.reshape(4, 2, mesh.shape["gy"], mesh.shape["gz"]), ("gx_0", "gx_1", "gy", "gz")
    )
    placed = (P(None, GX, "gy", "gz"), P())
    return jax.shard_map(
        shards,
        mesh=torus,
        in_specs=placed,
        out_specs=(P(None, GX, "gy", "gz"), P()),
        check_vma=False,
    )
```

profile of v0, /device:TPU:1, one launch (start us, length us, event | category | flops | bytes accessed | tf_op | source)
XLA Modules:
  0.0 307.6 jit_solution(9396979299132331808)
XLA Ops:
  1.7 3.2 %collective-permute-start = (f32[1,1,32,128]{3,2,1,0:T(8,128)S(1)}, f32[1,1,32,128]{3,2,1,0:T(8,128)S(1)}, u32[]{:S(2)}, u32[]{:S(2)}) collective-permute-start(f32[1,1,32,128]{3,2,1,0:T(8,128)S(1)} %slice.393), channel_id=1, source_target_pairs={{32,0},{64,32},{96,64},{128,96},{160,128},{192,160},{224,192},{0,2... | collective-permute-start | bytes 49160 | tf_op jit(solution)/shard_map/ppermute | solution.py:16
  10.1 5.6 %collective-permute-start.2 = (f32[1,32,1,128]{3,2,1,0:T(1,128)S(1)}, f32[1,32,1,128]{3,2,1,0:T(1,128)S(1)}, u32[]{:S(2)}, u32[]{:S(2)}) collective-permute-start(f32[1,32,1,128]{3,2,1,0:T(1,128)S(1)} %slice.397), channel_id=1, source_target_pairs={{4,0},{8,4},{12,8},{16,12},{20,16},{24,20},{28,24},{0,28},{5,1},{9... | collective-permute-start | bytes 49160 | tf_op jit(solution)/shard_map/ppermute | solution.py:16
  17.4 3.4 %collective-permute-done.3 = f32[1,32,1,128]{3,2,1,0:T(1,128)S(1)} collective-permute-done((f32[1,32,1,128]{3,2,1,0:T(1,128)S(1)}, f32[1,32,1,128]{3,2,1,0:T(1,128)S(1)}, u32[]{:S(2)}, u32[]{:S(2)}) %collective-permute-start.3) | collective-permute-done | bytes 16416 | tf_op jit(solution)/shard_map/ppermute | solution.py:16
  21.1 10.7 %slice.293 = f32[1,32,32,64]{3,1,2,0:T(8,128)S(1)} slice(f32[1,32,32,128]{3,1,2,0:T(8,128)S(1)} %bitcast.129), slice={[0:1:1], [0:32:1], [0:32:1], [0:128:2]} | slice | bytes 524288 | tf_op jit(solution)/shard_map/slice | solution.py:27
  31.8 2.8 collective-permute-start.4
  34.6 10.8 %slice.294 = f32[1,32,32,64]{3,1,2,0:T(8,128)S(1)} slice(f32[1,32,32,128]{3,1,2,0:T(8,128)S(1)} %bitcast.130), slice={[0:1:1], [0:32:1], [0:32:1], [1:128:2]} | slice | bytes 524288 | tf_op jit(solution)/shard_map/slice | solution.py:28
  47.0 8.5 %collective-permute-done.5 = f32[1,32,32,1]{3,1,2,0:T(8,128)S(1)} collective-permute-done((f32[1,32,32,1]{3,1,2,0:T(8,128)S(1)}, f32[1,32,32,1]{3,1,2,0:T(8,128)S(1)}, u32[]{:S(2)}, u32[]{:S(2)}) %collective-permute-start.5) | collective-permute-done | bytes 4128 | tf_op jit(solution)/shard_map/ppermute | solution.py:16
  58.9 6.9 %slice.300 = f32[1,16,16,64]{2,1,3,0:T(8,128)S(1)} slice(f32[1,32,32,128]{2,1,3,0:T(8,128)S(1)} %bitcast.126), slice={[0:1:1], [0:32:2], [0:32:2], [0:128:2]} | slice | bytes 131072 | tf_op jit(solution)/shard_map/slice | solution.py:114
  66.3 7.2 %collective-permute-start.6 = (f32[1,1,16,64]{2,1,3,0:T(1,128)S(1)}, f32[1,1,16,64]{2,1,3,0:T(1,128)S(1)}, u32[]{:S(2)}, u32[]{:S(2)}) collective-permute-start(f32[1,1,16,64]{2,1,3,0:T(1,128)S(1)} %slice.405), channel_id=1, source_target_pairs={{32,0},{64,32},{96,64},{128,96},{160,128},{192,160},{224,192},{0,2... | collective-permute-start | bytes 12296 | tf_op jit(solution)/shard_map/ppermute | solution.py:16
  79.4 3.7 %collective-permute-done.9 = f32[1,16,1,64]{3,2,1,0:T(1,128)S(1)} collective-permute-done((f32[1,16,1,64]{3,2,1,0:T(1,128)S(1)}, f32[1,16,1,64]{3,2,1,0:T(1,128)S(1)}, u32[]{:S(2)}, u32[]{:S(2)}) %collective-permute-start.9) | collective-permute-done | bytes 4128 | tf_op jit(solution)/shard_map/ppermute | solution.py:16
  85.9 2.6 collective-permute-done.10
  89.5 4.3 %collective-permute-done.11 = f32[1,16,16,1]{3,1,2,0:T(8,128)S(1)} collective-permute-done((f32[1,16,16,1]{3,1,2,0:T(8,128)S(1)}, f32[1,16,16,1]{3,1,2,0:T(8,128)S(1)}, u32[]{:S(2)}, u32[]{:S(2)}) %collective-permute-start.11) | collective-permute-done | bytes 1056 | tf_op jit(solution)/shard_map/ppermute | solution.py:16
  95.3 2.7 slice.320
  98.1 7.9 %collective-permute-start.12 = (f32[1,1,8,32]{2,1,3,0:T(1,128)S(1)}, f32[1,1,8,32]{2,1,3,0:T(1,128)S(1)}, u32[]{:S(2)}, u32[]{:S(2)}) collective-permute-start(f32[1,1,8,32]{2,1,3,0:T(1,128)S(1)} %slice.417), channel_id=1, source_target_pairs={{32,0},{64,32},{96,64},{128,96},{160,128},{192,160},{224,192},{0,2... | collective-permute-start | bytes 3080 | tf_op jit(solution)/shard_map/ppermute | solution.py:16
  112.3 2.8 collective-permute-done.15
  119.1 3.2 %collective-permute-done.17 = f32[1,8,8,1]{3,1,2,0:T(8,128)S(1)} collective-permute-done((f32[1,8,8,1]{3,1,2,0:T(8,128)S(1)}, f32[1,8,8,1]{3,1,2,0:T(8,128)S(1)}, u32[]{:S(2)}, u32[]{:S(2)}) %collective-permute-start.17) | collective-permute-done | bytes 288 | tf_op jit(solution)/shard_map/ppermute | solution.py:16
  123.8 8.0 %collective-permute-start.18 = (f32[1,1,4,16]{3,2,1,0:T(4,128)S(1)}, f32[1,1,4,16]{3,2,1,0:T(4,128)S(1)}, u32[]{:S(2)}, u32[]{:S(2)}) collective-permute-start(f32[1,1,4,16]{3,2,1,0:T(4,128)S(1)} %get-tuple-element.64), channel_id=1, source_target_pairs={{32,0},{64,32},{96,64},{128,96},{160,128},{192,160},{224,192},{0,2... | collective-permute-start | bytes 776 | tf_op jit(solution)/shard_map/ppermute | solution.py:16
  137.9 3.7 %collective-permute-done.21 = f32[1,4,1,16]{3,2,1,0:T(1,128)S(1)} collective-permute-done((f32[1,4,1,16]{3,2,1,0:T(1,128)S(1)}, f32[1,4,1,16]{3,2,1,0:T(1,128)S(1)}, u32[]{:S(2)}, u32[]{:S(2)}) %collective-permute-start.21) | collective-permute-done | bytes 288 | tf_op jit(solution)/shard_map/ppermute | solution.py:16
  142.2 2.4 collective-permute-done.22
  144.9 3.6 %collective-permute-done.23 = f32[1,4,4,1]{3,2,1,0:T(4,128)S(1)} collective-permute-done((f32[1,4,4,1]{3,2,1,0:T(4,128)S(1)}, f32[1,4,4,1]{3,2,1,0:T(4,128)S(1)}, u32[]{:S(2)}, u32[]{:S(2)}) %collective-permute-start.23) | collective-permute-done | bytes 96 | tf_op jit(solution)/shard_map/ppermute | solution.py:16
  149.6 7.4 %collective-permute-start.24 = (f32[1,1,2,8]{2,3,1,0:T(8,128)S(1)}, f32[1,1,2,8]{2,3,1,0:T(8,128)S(1)}, u32[]{:S(2)}, u32[]{:S(2)}) collective-permute-start(f32[1,1,2,8]{2,3,1,0:T(8,128)S(1)} %slice.440), channel_id=1, source_target_pairs={{32,0},{64,32},{96,64},{128,96},{160,128},{192,160},{224,192},{0,2... | collective-permute-start | bytes 200 | tf_op jit(solution)/shard_map/ppermute | solution.py:16
  161.9 3.6 %collective-permute-done.27 = f32[1,2,1,8]{3,2,1,0:T(1,128)S(1)} collective-permute-done((f32[1,2,1,8]{3,2,1,0:T(1,128)S(1)}, f32[1,2,1,8]{3,2,1,0:T(1,128)S(1)}, u32[]{:S(2)}, u32[]{:S(2)}) %collective-permute-start.27) | collective-permute-done | bytes 96 | tf_op jit(solution)/shard_map/ppermute | solution.py:16
  165.8 2.4 collective-permute-done.28
  168.4 3.6 %collective-permute-done.29 = f32[1,2,2,1]{3,2,1,0:T(2,128)S(1)} collective-permute-done((f32[1,2,2,1]{3,2,1,0:T(2,128)S(1)}, f32[1,2,2,1]{3,2,1,0:T(2,128)S(1)}, u32[]{:S(2)}, u32[]{:S(2)}) %collective-permute-start.29) | collective-permute-done | bytes 48 | tf_op jit(solution)/shard_map/ppermute | solution.py:16
  173.9 2.5 scatter_fusion.1
  176.5 15.1 %scatter_fusion.2 = f32[8,8,32]{2,1,0:T(8,128)S(1)} fusion(f32[8,8,32]{2,1,0:T(8,128)S(1)} %multiply_bitcast_fusion, s32[256]{0:T(256)S(1)} %reshape.1208, f32[256]{0:T(256)S(1)} %reshape.1210), kind=kCustom, calls=%fused_computation.2 | custom fusion | bytes 6144 | tf_op jit(solution)/shard_map/scatter | solution.py:117
  191.7 9.8 %all-reduce.3 = (f32[1]{0:T(128)}, f32[1]{0:T(128)}, f32[1]{0:T(128)}, f32[1]{0:T(128)}, f32[1]{0:T(128)}, /*index=5*/f32[1]{0:T(128)}, f32[1]{0:T(128)}, f32[1]{0:T(128)}, f32[1]{0:T(128)}, f32[1]{0:T(128)}) all-reduce(f32[1]{0:T(128)} %bitcast.68, f32[1]{0:T(128)} %bitcast.70, ...), channel_id=1, replica_groups=mesh['gx_0'=4,'gx_1'=2,'gy'=8,'gz'=4] {'gx_0'}, use_global_device_ids=true, to_apply=%region_31.32 | all-reduce | flops 10 | bytes 80 | tf_op jit(solution)/shard_map/psum | solution.py:21
  201.5 9.5 %all-reduce.4 = (f32[1]{0:T(128)}, f32[1]{0:T(128)}, f32[1]{0:T(128)}, f32[1]{0:T(128)}, f32[1]{0:T(128)}, /*index=5*/f32[1]{0:T(128)}, f32[1]{0:T(128)}, f32[1]{0:T(128)}, f32[1]{0:T(128)}, f32[1]{0:T(128)}) all-reduce(f32[1]{0:T(128)} %get-tuple-element.32, ...), channel_id=1, replica_groups=mesh['gx_0'=4,'gx_1'=2,'gy'=8,'gz'=4] {'gx_1'}, use_global_device_ids=true, to_apply=%region_32.33 | all-reduce | flops 10 | bytes 80 | tf_op jit(solution)/shard_map/psum | solution.py:21
  210.9 13.4 %all-reduce.1 = (f32[1]{0:T(128)}, f32[1]{0:T(128)}, f32[1]{0:T(128)}, f32[1]{0:T(128)}, f32[1]{0:T(128)}, /*index=5*/f32[1]{0:T(128)}, f32[1]{0:T(128)}, f32[1]{0:T(128)}, f32[1]{0:T(128)}, f32[1]{0:T(128)}) all-reduce(f32[1]{0:T(128)} %get-tuple-element.42, ...), channel_id=1, replica_groups=mesh['gx_0'=4,'gx_1'=2,'gy'=8,'gz'=4] {'gy'}, use_global_device_ids=true, to_apply=%region_33.34 | all-reduce | flops 10 | bytes 80 | tf_op jit(solution)/shard_map/psum | solution.py:21
  224.4 6.8 %all-reduce.2 = (f32[1]{0:T(128)}, f32[1]{0:T(128)}, f32[1]{0:T(128)}, f32[1]{0:T(128)}, f32[1]{0:T(128)}, /*index=5*/f32[1]{0:T(128)}, f32[1]{0:T(128)}, f32[1]{0:T(128)}, f32[1]{0:T(128)}, f32[1]{0:T(128)}) all-reduce(f32[1]{0:T(128)} %get-tuple-element.12, ...), channel_id=1, replica_groups=mesh['gx_0'=4,'gx_1'=2,'gy'=8,'gz'=4] {'gz'}, use_global_device_ids=true, to_apply=%region_34.35 | all-reduce | flops 10 | bytes 80 | tf_op jit(solution)/shard_map/psum | solution.py:21
  238.2 8.1 %scatter_fusion.3 = f32[16384]{0:T(1024)S(1)} fusion(f32[16384]{0:T(1024)S(1)} %reshape.1216, s32[2048]{0:T(1024)S(1)} %reshape.1218, f32[2048]{0:T(1024)S(1)} %reshape.1220), kind=kCustom, calls=%fused_computation.3 | custom fusion | bytes 32768 | tf_op jit(solution)/shard_map/scatter | solution.py:117
  246.3 60.5 %scatter_fusion.4 = f32[131072]{0:T(1024)S(1)} fusion(f32[131072]{0:T(1024)S(1)} %bitcast.122, s32[16384]{0:T(1024)S(1)} %reshape.1228, f32[16384]{0:T(1024)S(1)} %scatter_fusion.3), kind=kCustom, calls=%fused_computation.4 | custom fusion | bytes 262144
  (238 shorter events, 49.3 us)
Async XLA Ops:
  0.6 7.2 %copy-start.3 = (s32[3]{0:T(128)S(1)}, s32[3]{0:T(128)}, u32[]{:S(2)}) copy-start(s32[3]{0:T(128)} %constant.207) | copy-start | bytes 40
  0.6 7.6 %copy-start.1 = (f32[1,32,32,128]{3,2,1,0:T(8,128)S(1)}, f32[1,32,32,128]{3,2,1,0:T(8,128)}, u32[]{:S(2)}) copy-start(f32[1,32,32,128]{3,2,1,0:T(8,128)} %param.2) | copy-start | bytes 1572868
  1.7 6.5 %collective-permute-start = (f32[1,1,32,128]{3,2,1,0:T(8,128)S(1)}, f32[1,1,32,128]{3,2,1,0:T(8,128)S(1)}, u32[]{:S(2)}, u32[]{:S(2)}) collective-permute-start(f32[1,1,32,128]{3,2,1,0:T(8,128)S(1)} %slice.393), channel_id=1, source_target_pairs={{32,0},{64,32},{96,64},{128,96},{160,128},{192,160},{224,192},{0,2... | collective-permute-start | bytes 49160 | tf_op jit(solution)/shard_map/ppermute | solution.py:16
  8.3 1.2 collective-permute-start.1
  10.1 6.5 %collective-permute-start.2 = (f32[1,32,1,128]{3,2,1,0:T(1,128)S(1)}, f32[1,32,1,128]{3,2,1,0:T(1,128)S(1)}, u32[]{:S(2)}, u32[]{:S(2)}) collective-permute-start(f32[1,32,1,128]{3,2,1,0:T(1,128)S(1)} %slice.397), channel_id=1, source_target_pairs={{4,0},{8,4},{12,8},{16,12},{20,16},{24,20},{28,24},{0,28},{5,1},{9... | collective-permute-start | bytes 49160 | tf_op jit(solution)/shard_map/ppermute | solution.py:16
  16.7 4.1 %collective-permute-start.3 = (f32[1,32,1,128]{3,2,1,0:T(1,128)S(1)}, f32[1,32,1,128]{3,2,1,0:T(1,128)S(1)}, u32[]{:S(2)}, u32[]{:S(2)}) collective-permute-start(f32[1,32,1,128]{3,2,1,0:T(1,128)S(1)} %slice.398), channel_id=1, source_target_pairs={{28,0},{0,4},{4,8},{8,12},{12,16},{16,20},{20,24},{24,28},{29,1},{... | collective-permute-start | bytes 49160 | tf_op jit(solution)/shard_map/ppermute | solution.py:16
  31.8 13.9 %collective-permute-start.4 = (f32[1,32,32,1]{3,1,2,0:T(8,128)S(1)}, f32[1,32,32,1]{3,1,2,0:T(8,128)S(1)}, u32[]{:S(2)}, u32[]{:S(2)}) collective-permute-start(f32[1,32,32,1]{3,1,2,0:T(8,128)S(1)} %bitcast.128), channel_id=1, source_target_pairs={{1,0},{2,1},{3,2},{0,3},{5,4},{6,5},{7,6},{4,7},{9,8},{10,9},{11,1... | collective-permute-start | bytes 12296 | tf_op jit(solution)/shard_map/ppermute | solution.py:16
  46.1 9.3 %collective-permute-start.5 = (f32[1,32,32,1]{3,1,2,0:T(8,128)S(1)}, f32[1,32,32,1]{3,1,2,0:T(8,128)S(1)}, u32[]{:S(2)}, u32[]{:S(2)}) collective-permute-start(f32[1,32,32,1]{3,1,2,0:T(8,128)S(1)} %slice.402), channel_id=1, source_target_pairs={{3,0},{0,1},{1,2},{2,3},{7,4},{4,5},{5,6},{6,7},{11,8},{8,9},{9,10... | collective-permute-start | bytes 12296 | tf_op jit(solution)/shard_map/ppermute | solution.py:16
  66.3 8.1 %collective-permute-start.6 = (f32[1,1,16,64]{2,1,3,0:T(1,128)S(1)}, f32[1,1,16,64]{2,1,3,0:T(1,128)S(1)}, u32[]{:S(2)}, u32[]{:S(2)}) collective-permute-start(f32[1,1,16,64]{2,1,3,0:T(1,128)S(1)} %slice.405), channel_id=1, source_target_pairs={{32,0},{64,32},{96,64},{128,96},{160,128},{192,160},{224,192},{0,2... | collective-permute-start | bytes 12296 | tf_op jit(solution)/shard_map/ppermute | solution.py:16
  74.5 1.3 collective-permute-start.7
  76.2 3.1 collective-permute-start.8
  79.3 3.8 %collective-permute-start.9 = (f32[1,16,1,64]{3,2,1,0:T(1,128)S(1)}, f32[1,16,1,64]{3,2,1,0:T(1,128)S(1)}, u32[]{:S(2)}, u32[]{:S(2)}) collective-permute-start(f32[1,16,1,64]{3,2,1,0:T(1,128)S(1)} %slice.410), channel_id=1, source_target_pairs={{28,0},{0,4},{4,8},{8,12},{12,16},{16,20},{20,24},{24,28},{29,1},{... | collective-permute-start | bytes 12296 | tf_op jit(solution)/shard_map/ppermute | solution.py:16
  84.4 4.1 %collective-permute-start.10 = (f32[1,16,16,1]{3,1,2,0:T(8,128)S(1)}, f32[1,16,16,1]{3,1,2,0:T(8,128)S(1)}, u32[]{:S(2)}, u32[]{:S(2)}) collective-permute-start(f32[1,16,16,1]{3,1,2,0:T(8,128)S(1)} %bitcast.140), channel_id=1, source_target_pairs={{1,0},{2,1},{3,2},{0,3},{5,4},{6,5},{7,6},{4,7},{9,8},{10,9},{11,1... | collective-permute-start | bytes 3080 | tf_op jit(solution)/shard_map/ppermute | solution.py:16
  88.7 5.1 %collective-permute-start.11 = (f32[1,16,16,1]{3,1,2,0:T(8,128)S(1)}, f32[1,16,16,1]{3,1,2,0:T(8,128)S(1)}, u32[]{:S(2)}, u32[]{:S(2)}) collective-permute-start(f32[1,16,16,1]{3,1,2,0:T(8,128)S(1)} %slice.414), channel_id=1, source_target_pairs={{3,0},{0,1},{1,2},{2,3},{7,4},{4,5},{5,6},{6,7},{11,8},{8,9},{9,10... | collective-permute-start | bytes 3080 | tf_op jit(solution)/shard_map/ppermute | solution.py:16
  98.1 8.8 %collective-permute-start.12 = (f32[1,1,8,32]{2,1,3,0:T(1,128)S(1)}, f32[1,1,8,32]{2,1,3,0:T(1,128)S(1)}, u32[]{:S(2)}, u32[]{:S(2)}) collective-permute-start(f32[1,1,8,32]{2,1,3,0:T(1,128)S(1)} %slice.417), channel_id=1, source_target_pairs={{32,0},{64,32},{96,64},{128,96},{160,128},{192,160},{224,192},{0,2... | collective-permute-start | bytes 3080 | tf_op jit(solution)/shard_map/ppermute | solution.py:16
  107.0 1.3 collective-permute-start.13
  108.5 2.8 collective-permute-start.14
  111.3 3.7 %collective-permute-start.15 = (f32[1,8,1,32]{3,2,1,0:T(1,128)S(1)}, f32[1,8,1,32]{3,2,1,0:T(1,128)S(1)}, u32[]{:S(2)}, u32[]{:S(2)}) collective-permute-start(f32[1,8,1,32]{3,2,1,0:T(1,128)S(1)} %slice.422), channel_id=1, source_target_pairs={{28,0},{0,4},{4,8},{8,12},{12,16},{16,20},{20,24},{24,28},{29,1},{... | collective-permute-start | bytes 3080 | tf_op jit(solution)/shard_map/ppermute | solution.py:16
  115.3 2.8 collective-permute-start.16
  118.3 4.0 %collective-permute-start.17 = (f32[1,8,8,1]{3,1,2,0:T(8,128)S(1)}, f32[1,8,8,1]{3,1,2,0:T(8,128)S(1)}, u32[]{:S(2)}, u32[]{:S(2)}) collective-permute-start(f32[1,8,8,1]{3,1,2,0:T(8,128)S(1)} %slice.426), channel_id=1, source_target_pairs={{3,0},{0,1},{1,2},{2,3},{7,4},{4,5},{5,6},{6,7},{11,8},{8,9},{9,10... | collective-permute-start | bytes 776 | tf_op jit(solution)/shard_map/ppermute | solution.py:16
  123.8 10.0 %collective-permute-start.18 = (f32[1,1,4,16]{3,2,1,0:T(4,128)S(1)}, f32[1,1,4,16]{3,2,1,0:T(4,128)S(1)}, u32[]{:S(2)}, u32[]{:S(2)}) collective-permute-start(f32[1,1,4,16]{3,2,1,0:T(4,128)S(1)} %get-tuple-element.64), channel_id=1, source_target_pairs={{32,0},{64,32},{96,64},{128,96},{160,128},{192,160},{224,192},{0,2... | collective-permute-start | bytes 776 | tf_op jit(solution)/shard_map/ppermute | solution.py:16
  133.8 1.2 collective-permute-start.19
  135.1 2.6 collective-permute-start.20
  137.7 3.9 %collective-permute-start.21 = (f32[1,4,1,16]{3,2,1,0:T(1,128)S(1)}, f32[1,4,1,16]{3,2,1,0:T(1,128)S(1)}, u32[]{:S(2)}, u32[]{:S(2)}) collective-permute-start(f32[1,4,1,16]{3,2,1,0:T(1,128)S(1)} %get-tuple-element.57), channel_id=1, source_target_pairs={{28,0},{0,4},{4,8},{8,12},{12,16},{16,20},{20,24},{24,28},{29,1},{... | collective-permute-start | bytes 776 | tf_op jit(solution)/shard_map/ppermute | solution.py:16
  141.9 2.8 collective-permute-start.22
  144.8 3.7 %collective-permute-start.23 = (f32[1,4,4,1]{3,2,1,0:T(4,128)S(1)}, f32[1,4,4,1]{3,2,1,0:T(4,128)S(1)}, u32[]{:S(2)}, u32[]{:S(2)}) collective-permute-start(f32[1,4,4,1]{3,2,1,0:T(4,128)S(1)} %slice.438), channel_id=1, source_target_pairs={{3,0},{0,1},{1,2},{2,3},{7,4},{4,5},{5,6},{6,7},{11,8},{8,9},{9,10... | collective-permute-start | bytes 200 | tf_op jit(solution)/shard_map/ppermute | solution.py:16
  149.6 8.2 %collective-permute-start.24 = (f32[1,1,2,8]{2,3,1,0:T(8,128)S(1)}, f32[1,1,2,8]{2,3,1,0:T(8,128)S(1)}, u32[]{:S(2)}, u32[]{:S(2)}) collective-permute-start(f32[1,1,2,8]{2,3,1,0:T(8,128)S(1)} %slice.440), channel_id=1, source_target_pairs={{32,0},{64,32},{96,64},{128,96},{160,128},{192,160},{224,192},{0,2... | collective-permute-start | bytes 200 | tf_op jit(solution)/shard_map/ppermute | solution.py:16
  157.8 1.2 collective-permute-start.25
  159.1 2.8 collective-permute-start.26
  161.9 3.6 %collective-permute-start.27 = (f32[1,2,1,8]{3,2,1,0:T(1,128)S(1)}, f32[1,2,1,8]{3,2,1,0:T(1,128)S(1)}, u32[]{:S(2)}, u32[]{:S(2)}) collective-permute-start(f32[1,2,1,8]{3,2,1,0:T(1,128)S(1)} %slice_subtract_fusion.1), channel_id=1, source_target_pairs={{28,0},{0,4},{4,8},{8,12},{12,16},{16,20},{20,24},{24,28},{29,1},{... | collective-permute-start | bytes 200 | tf_op jit(solution)/shard_map/ppermute | solution.py:16
  165.8 2.4 collective-permute-start.28
  168.4 3.7 %collective-permute-start.29 = (f32[1,2,2,1]{3,2,1,0:T(2,128)S(1)}, f32[1,2,2,1]{3,2,1,0:T(2,128)S(1)}, u32[]{:S(2)}, u32[]{:S(2)}) collective-permute-start(f32[1,2,2,1]{3,2,1,0:T(2,128)S(1)} %slice.446), channel_id=1, source_target_pairs={{3,0},{0,1},{1,2},{2,3},{7,4},{4,5},{5,6},{6,7},{11,8},{8,9},{9,10... | collective-permute-start | bytes 56 | tf_op jit(solution)/shard_map/ppermute | solution.py:16
  (2 other events, 8.0 us)
where the time goes:
time: 313 us; the launch traced here: 308 us
  local copies, waits for them, and re-layouts  134 us (43%)
  waiting for transfers between devices  61.3 us (20%)
  starting transfers between devices  50.7 us (16%)
  blocking collectives  39.5 us (13%)
  between operations  11.3 us (4%)
  other arithmetic  10.7 us (3%)
    unnamed x12, local copies, waits for them, and re-layouts  61.6 us
    ppermute x30, waiting for transfers between devices, shifted(): return lax.ppermute(block, axis, route)  61.3 us
    ppermute x30, starting transfers between devices, shifted(): return lax.ppermute(block, axis, route)  50.7 us
    psum x4, blocking collectives, over_axes(): x = lax.psum(x, axis)  39.5 us
    scatter x7, local copies, waits for them, and re-layouts, shards(): result = shrunk.at[:, ::2, ::2, ::2].set(result)  26.6 us
    slice x15, local copies, waits for them, and re-layouts, split_pair(): even_part = lax.slice_in_dim(values, 0, length, 2, axis_dim)  14.4 us
    slice x11, local copies, waits for them, and re-layouts, split_pair(): odd_part = lax.slice_in_dim(values, 1, length, 2, axis_dim)  13.4 us
    slice x5, local copies, waits for them, and re-layouts, shards(): current = current[:, ::2, ::2, ::2]  10.3 us
  transfers between devices with their start and end apart: 30, of which 27 were waited for; matrix products, arithmetic and copies ran while one was open for 7% of the time, Pallas kernels for 0%

commit v1 on v0

v1 whole, which is shorter than its diff:
```python
import functools

import jax
import jax.numpy as jnp
import numpy as np
from jax import lax
from jax.experimental import pallas as pl
from jax.experimental.pallas import tpu as pltpu
from jax.sharding import PartitionSpec as P

NEAR = 4
LEVELS = 5
LANES = 128
SIDE = 32
EXT = 2 * NEAR
PITCH = SIDE + EXT
F32 = jnp.float32


def cascade(cells, ahead, behind):
    details, firsts = [], []
    for level in range(NEAR):
        half = len(cells) // 2
        following = cells[2::2] + [ahead[level]]
        detail = [cells[2 * k + 1] - 0.5 * (cells[2 * k] + following[k]) for k in range(half)]
        details.append(detail[-1])
        firsts.append(cells[0])
        before = [behind[level]] + detail[:-1]
        cells = [cells[2 * k] + 0.25 * (before[k] + detail[k]) for k in range(half)]
    return details, firsts


def end_weights(length):
    none = [np.zeros(length)] * NEAR
    details, firsts = cascade(list(np.eye(length)), none, none)
    return np.stack(details + firsts)


def seam_weights():
    zero = [np.zeros(1)] * NEAR
    flat = [np.zeros(1)] * SIDE
    alpha = np.zeros((NEAR, NEAR))
    beta = np.zeros((NEAR, NEAR))
    for j in range(NEAR):
        unit = [np.ones(1) * (k == j) for k in range(NEAR)]
        alpha[:, j] = [d[0] for d in cascade(flat, unit, zero)[0]]
        beta[:, j] = [f[0] for f in cascade(flat, zero, unit)[1]]
    lasts, firsts = [], []
    for level in range(NEAR):
        first = np.eye(EXT)[NEAR + level]
        for j in range(level):
            first = first + beta[level, j] * lasts[j]
        firsts.append(first)
        last = np.eye(EXT)[level]
        for j in range(level + 1):
            last = last + alpha[level, j] * firsts[j]
        lasts.append(last)
    return np.stack(lasts), np.stack(firsts)


W = end_weights(SIDE)
WZ = end_weights(LANES)
LAST, FIRST = seam_weights()
GROUP = LANES // EXT


def constant_tables():
    tables = np.zeros((7, LANES, LANES), np.float32)
    left = np.zeros((EXT, EXT))
    right = np.zeros((EXT, EXT))
    left[:, :NEAR] = LAST.T
    right[:, NEAR:] = FIRST.T
    tables[0] = np.tile(WZ.T, (1, GROUP))
    tables[1] = np.kron(np.eye(GROUP), left)
    tables[2] = np.kron(np.eye(GROUP), right)
    for half in range(2):
        tables[3 + half, :, : EXT * EXT] = np.kron(W[:, half * GROUP : (half + 1) * GROUP].T, np.eye(EXT))
    tables[5, : EXT * EXT, : EXT * EXT] = np.kron(left, np.eye(EXT))
    tables[6, : EXT * EXT, : EXT * EXT] = np.kron(right, np.eye(EXT))
    return tables


def dot(a, b):
    return jnp.dot(a, b, precision=lax.Precision.HIGHEST, preferred_element_type=F32)


def lanes_of(rows):
    return lax.broadcasted_iota(jnp.int32, (rows, LANES), 1)


def rows_of(rows):
    return lax.broadcasted_iota(jnp.int32, (rows, LANES), 0)


def roll(v, shift):
    return pltpu.roll(v, shift % LANES, 1)


def weighted(rows, load):
    sums = [None] * EXT
    for i in range(SIDE):
        block = load(i)
        for g in range(EXT):
            if W[g, i] != 0.0:
                term = float(W[g, i]) * block
                sums[g] = term if sums[g] is None else sums[g] + term
    return sums


def mix(weights, blocks):
    total = None
    for w, block in zip(weights, blocks):
        if w != 0.0:
            term = float(w) * block
            total = term if total is None else total + term
    return total


def ends_kernel(f, table, pz, fx, fy):
    lane = lanes_of(SIDE)
    packed = [jnp.zeros((SIDE, LANES), F32)] * 2
    for x in range(SIDE):
        out = dot(f[pl.ds(x * SIDE, SIDE), :], table[...])
        packed[x // GROUP] = jnp.where(lane // EXT == x % GROUP, out, packed[x // GROUP])
    for half in range(2):
        pz[pl.ds(half * SIDE, SIDE), :] = packed[half]
    for c in range(SIDE // 8):
        for g, block in enumerate(weighted(8, lambda x: f[pl.ds(x * SIDE + 8 * c, 8), :])):
            fx[pl.ds(g * SIDE + 8 * c, 8), :] = block
    for c in range(SIDE // 8):
        for g, block in enumerate(weighted(8, lambda y: f[pl.ds(8 * c * SIDE + y, 8, stride=SIDE), :])):
            fy[pl.ds(g * SIDE + 8 * c, 8), :] = block


def depth_kernel(pz, before, after, fx, tables, ez, up, down):
    slot = lanes_of(SIDE) % EXT
    fxe = None
    for half in range(2):
        rows = pl.ds(half * SIDE, SIDE)
        own = pz[rows, :]
        full = dot(jnp.where(slot < NEAR, before[rows, :], own), tables[1]) + dot(
            jnp.where(slot < NEAR, own, after[rows, :]), tables[2]
        )
        ez[rows, :] = full
        part = dot(full, tables[3 + half])
        fxe = part if fxe is None else fxe + part
    for g in range(NEAR):
        up[pl.ds(g * SIDE, SIDE), :] = fx[pl.ds(g * SIDE, SIDE), :]
        down[pl.ds(g * SIDE, SIDE), :] = fx[pl.ds((NEAR + g) * SIDE, SIDE), :]
    up[pl.ds(NEAR * SIDE, SIDE), :] = fxe
    down[pl.ds(NEAR * SIDE, SIDE), :] = fxe


def width_kernel(up, down, before, after, fy, ez, wy, tables, xe, xee, yup, ydown):
    for c in range(SIDE // 8):
        rows = [pl.ds(g * SIDE + 8 * c, 8) for g in range(NEAR)]
        own_last = [up[r, :] for r in rows]
        own_first = [down[r, :] for r in rows]
        seam_before = [before[r, :] for r in rows] + own_first
        seam_after = own_last + [after[r, :] for r in rows]
        for level in range(NEAR):
            xe[pl.ds(level * SIDE + 8 * c, 8), :] = mix(LAST[level], seam_before)
            xe[pl.ds((NEAR + level) * SIDE + 8 * c, 8), :] = mix(FIRST[level], seam_after)
    slot = lanes_of(SIDE) // EXT
    rows = pl.ds(NEAR * SIDE, SIDE)
    own = up[rows, :]
    corner = dot(jnp.where(slot < NEAR, before[rows, :], own), tables[5]) + dot(
        jnp.where(slot < NEAR, own, after[rows, :]), tables[6]
    )
    xee[...] = corner
    sums = weighted(EXT, lambda y: xe[pl.ds(y, EXT, stride=SIDE), :])
    for g in range(EXT):
        target = yup if g < NEAR else ydown
        base = (g % NEAR) * PITCH
        target[pl.ds(base, SIDE), :] = fy[pl.ds(g * SIDE, SIDE), :]
        target[pl.ds(base + SIDE, EXT), :] = sums[g]
    for i, block in enumerate((ez[pl.ds(0, SIDE), :], ez[pl.ds(SIDE, SIDE), :], corner)):
        part = dot(wy[...], block)
        yup[pl.ds(NEAR * PITCH + i * EXT, EXT), :] = part
        ydown[pl.ds(NEAR * PITCH + i * EXT, EXT), :] = part


def lift_chunk(ref, at, level, masked):
    step = 1 << level
    pairs = SIDE // (2 * step)
    masked = masked and level > 0
    behind = ref[at(SIDE + level), :]
    even = ref[at(0), :]
    for k in range(pairs):
        odd = ref[at(step * (2 * k + 1)), :]
        ahead = ref[at(step * (2 * k + 2)), :] if k < pairs - 1 else ref[at(SIDE + NEAR + level), :]
        detail = odd - 0.5 * (even + ahead)
        smooth = even + 0.25 * (behind + detail)
        if masked:
            live = (lanes_of(odd.shape[0]) & (step - 1)) == 0
            detail, smooth = jnp.where(live, detail, odd), jnp.where(live, smooth, even)
        ref[at(step * (2 * k + 1)), :] = detail
        ref[at(2 * step * k), :] = smooth
        behind, even = detail, ahead


def chunks(level):
    step = 1 << level
    count = SIDE // step
    own = [(8 * step * c, min(8, count), step) for c in range(max(1, count // 8))]
    return own + ([(SIDE, EXT, 1)] if level < NEAR else [])


def levels_kernel(f, ez, xe, xee, yup, ydown, before, after, th, coef, send, v, q):
    for x in range(SIDE):
        v[pl.ds(x * PITCH, SIDE), :] = f[pl.ds(x * SIDE, SIDE), :]
    for g in range(EXT):
        v[pl.ds((SIDE + g) * PITCH, SIDE), :] = xe[pl.ds(g * SIDE, SIDE), :]
    for c in range(PITCH // 8):
        rows = [pl.ds(g * PITCH + 8 * c, 8) for g in range(NEAR)]
        seam_before = [before[r, :] for r in rows] + [ydown[r, :] for r in rows]
        seam_after = [yup[r, :] for r in rows] + [after[r, :] for r in rows]
        for level in range(NEAR):
            v[pl.ds(8 * c * PITCH + SIDE + level, 8, stride=PITCH), :] = mix(LAST[level], seam_before)
            v[pl.ds(8 * c * PITCH + SIDE + NEAR + level, 8, stride=PITCH), :] = mix(FIRST[level], seam_after)
    row8 = rows_of(EXT)
    for i in range(3):
        first = NEAR * PITCH + i * EXT
        own = [yup[pl.ds(first + j, 1), :] for j in range(EXT)]
        seam_before = [before[pl.ds(first + j, 1), :] for j in range(NEAR)] + own[NEAR:]
        seam_after = own[:NEAR] + [after[pl.ds(first + NEAR + j, 1), :] for j in range(NEAR)]
        extra = jnp.zeros((EXT, LANES), F32)
        for level in range(NEAR):
            extra = jnp.where(row8 == level, mix(LAST[level], seam_before), extra)
            extra = jnp.where(row8 == NEAR + level, mix(FIRST[level], seam_after), extra)
        block = ez[pl.ds(i * SIDE, SIDE), :] if i < 2 else xee[...]
        for j in range(GROUP if i < 2 else EXT):
            x = i * GROUP + j
            q[pl.ds(x * PITCH, SIDE), :] = roll(block, -EXT * j)
            q[pl.ds(x * PITCH + SIDE, EXT), :] = roll(extra, -EXT * j)

    for level in range(NEAR):
        step = 1 << level
        for ref in (v, q):
            for first, count, stride in chunks(level):
                lift_chunk(ref, lambda i: pl.ds(i * PITCH + first, count, stride=stride), level, ref is v)
            for first, count, stride in chunks(level):
                lift_chunk(ref, lambda i: pl.ds(first * PITCH + i, count, stride=stride * PITCH), level, ref is v)
        planes = list(range(0, SIDE, step)) + (list(range(SIDE, PITCH)) if level < NEAR - 1 else [])
        for x in planes:
            for first, count, stride in chunks(level):
                if first == SIDE and level == NEAR - 1:
                    continue
                at = pl.ds(x * PITCH + first, count, stride=stride)
                lane = lanes_of(count)
                cells, ends = v[at, :], q[at, :]
                ahead = jnp.where(lane == 0, roll(ends, -(NEAR + level)), cells)
                detail = cells - 0.5 * (roll(cells, step) + roll(ahead, -step))
                behind = jnp.where(lane == LANES - step, roll(ends, -step - level), detail)
                smooth = cells + 0.25 * (roll(behind, step) + roll(detail, -step))
                place = lane & (2 * step - 1)
                v[at, :] = jnp.where(place == 0, smooth, jnp.where(place == step, detail, cells))

    energy = [jnp.zeros((8, LANES), F32)] * NEAR
    kept = [jnp.zeros((8, LANES), F32)] * NEAR
    for c in range(SIDE // 8):
        bits = (rows_of(8) + 8 * c) | lanes_of(8)
        own = [(bits & ((2 << level) - 1)) == (1 << level) for level in range(NEAR)]
        rest = [(bits & ((1 << level) - 1)) == 0 for level in range(NEAR)]
        bounds = []
        for depth in range(NEAR + 1):
            bound = jnp.broadcast_to(th[pl.ds(min(depth, NEAR - 1), 1), :], (8, LANES))
            for level in range(min(depth, NEAR - 1) - 1, -1, -1):
                bound = jnp.where(own[level], th[pl.ds(level, 1), :], bound)
            bounds.append(bound)
        squares = [None] * (NEAR + 1)
        sizes = [None] * (NEAR + 1)
        for x in range(SIDE):
            depth = NEAR if x == 0 else min(NEAR, (x & -x).bit_length() - 1)
            cells = v[pl.ds(x * PITCH + 8 * c, 8), :]
            shrunk = cells - jnp.minimum(jnp.maximum(cells, -bounds[depth]), bounds[depth])
            coef[pl.ds(x * SIDE + 8 * c, 8), :] = shrunk
            square, size = cells * cells, jnp.abs(shrunk)
            squares[depth] = square if squares[depth] is None else squares[depth] + square
            sizes[depth] = size if sizes[depth] is None else sizes[depth] + size
        for sums, target in ((squares, energy), (sizes, kept)):
            for level in range(NEAR):
                deeper = functools.reduce(lambda a, b: a + b, sums[level + 1 :])
                part = jnp.where(rest[level], sums[level], 0.0) + jnp.where(own[level], deeper, 0.0)
                target[level] = target[level] + part

    lane8 = lanes_of(8)
    corners = [v[pl.ds(a * 16 * PITCH + b * 16, 1), :] for a in range(2) for b in range(2)]
    block = jnp.zeros((8, LANES), F32)
    for i, corner in enumerate(corners):
        block = jnp.where(row8 == i, corner, block)
    source, target = rows_of(LANES), lanes_of(LANES)
    pick = jnp.where((source == 16 * (target % 8)) & (target < 32), 1.0, 0.0).astype(F32)
    block = jnp.where(lane8 // 8 == row8, dot(block, pick), 0.0)
    for i, part in enumerate(energy + kept):
        block = jnp.where((lane8 == 32 + i) & (row8 == 0), jnp.sum(part), block)
    send[...] = jnp.broadcast_to(jnp.sum(block, axis=0, keepdims=True), send.shape)


def last_kernel(got, spot, coef, th, out, stats, grid, *, sizes, counts):
    nx, ny, nz = sizes
    plane = ny * nz
    lane, row = lanes_of(plane), rows_of(plane)
    turn = pl.program_id(0)

    @pl.when(turn == 0)
    def _():
        v = [got[pl.ds(i * plane, plane), :] for i in range(nx)]
        sums = functools.reduce(lambda a, b: a + b, v)
        sums = jnp.sum(sums, axis=0, keepdims=True)

        def down(a, shift):
            return pltpu.roll(a, shift % plane, 0)

        odd = (lane & 16) != 0
        d = [v[i] - 0.5 * roll(v[i] + v[(i + 1) % nx], 16) for i in range(nx)]
        v = [jnp.where(odd, d[i], v[i] + 0.25 * roll(d[i] + d[i - 1], -16)) for i in range(nx)]
        odd = (lane & 8) != 0
        d = [a - 0.5 * roll(a + down(a, -nz), 8) for a in v]
        v = [jnp.where(odd, b, a + 0.25 * roll(b + down(b, nz), -8)) for a, b in zip(v, d)]
        odd = (lane & 1) != 0
        top, low = (lane & 7) == 7, (lane & 7) == 0
        far = row % nz == nz - 1
        near = row % nz == 0
        result = []
        for a in v:
            following = jnp.where(far, down(a, nz - 1), down(a, -1))
            d = a - 0.5 * (roll(a, 1) + jnp.where(top, roll(following, 7), roll(a, -1)))
            previous = jnp.where(near, down(d, 1 - nz), down(d, 1))
            s = a + 0.25 * (jnp.where(low, roll(previous, -7), roll(d, 1)) + roll(d, -1))
            result.append(jnp.where(odd, d, s))
        bound = th[pl.ds(LEVELS - 1, 1), :]
        detail = (lane < 32) & ((lane & 25) != 0)
        energy = kept = None
        for i, a in enumerate(result):
            shrunk = a - jnp.minimum(jnp.maximum(a, -bound), bound)
            grid[pl.ds(i * plane, plane), :] = jnp.where(detail, shrunk, a)
            square, size = jnp.where(detail, a * a, 0.0), jnp.where(detail, jnp.abs(shrunk), 0.0)
            energy = square if energy is None else energy + square
            kept = size if kept is None else kept + size
        lane1 = lanes_of(1)
        for i, (part, base) in enumerate(((energy, 32), (kept, 36))):
            totals = jnp.where(lane1 == NEAR, jnp.sum(part), roll(sums, -base))
            scale = jnp.zeros((1, LANES), F32)
            for level in range(LEVELS):
                scale = jnp.where(lane1 == level, 1.0 / counts[level], scale)
            stats[i] = (totals * scale)[:, :LEVELS]

    own = grid[pl.ds(spot[0], 1), :]
    row8, lane8 = rows_of(8), lanes_of(8)
    block = jnp.where((lane8 < 32) & (lane8 // 8 == 2 * turn + row8) & (row8 < 2), own, 0.0)
    source, target = rows_of(LANES), lanes_of(LANES)
    pick = jnp.where((target == 16 * (source % 8)) & (source < 32), 1.0, 0.0).astype(F32)
    block = dot(block, pick)
    out[...] = coef[...]
    start = (lane8[:1] % 16) == 0
    for b in range(2):
        at = pl.ds(16 * b, 1)
        out[at, :] = jnp.where(start, block[b : b + 1, :], coef[at, :])


def shape(*dims):
    return jax.ShapeDtypeStruct(dims, F32)


def shards(fields, exponents):
    sizes = tuple(lax.axis_size(a) for a in ("gx", "gy", "gz"))
    devices = sizes[0] * sizes[1] * sizes[2]
    cells = fields.size * devices
    counts = [7.0 * cells / 8 ** (level + 1) for level in range(LEVELS)]
    f = fields.reshape(SIDE * SIDE, LANES)
    th = jnp.broadcast_to(jnp.pad(jnp.exp2(exponents.astype(F32)), (0, 3))[:, None], (8, LANES))
    tables = jnp.asarray(constant_tables())
    wy = jnp.asarray(W.astype(np.float32))

    def swap(up, down, axis):
        n = lax.axis_size(axis)
        before = lax.ppermute(up, axis, [(i, (i + 1) % n) for i in range(n)])
        after = lax.ppermute(down, axis, [((i + 1) % n, i) for i in range(n)])
        return before, after

    pz, fx, fy = pl.pallas_call(
        ends_kernel,
        out_shape=(shape(2 * SIDE, LANES), shape(EXT * SIDE, LANES), shape(EXT * SIDE, LANES)),
        name="ends",
    )(f, tables[0])
    before, after = swap(pz, pz, "gz")
    message = shape((NEAR + 1) * SIDE, LANES)
    ez, up, down = pl.pallas_call(
        depth_kernel, out_shape=(shape(2 * SIDE, LANES), message, message), name="depth"
    )(pz, before, after, fx, tables)
    before, after = swap(up, down, "gx")
    message = shape(NEAR * PITCH + 3 * EXT, LANES)
    xe, xee, yup, ydown = pl.pallas_call(
        width_kernel,
        out_shape=(shape(EXT * SIDE, LANES), shape(SIDE, LANES), message, message),
        name="width",
    )(up, down, before, after, fy, ez, wy, tables)
    before, after = swap(yup, ydown, "gy")
    coef, send = pl.pallas_call(
        levels_kernel,
        out_shape=(shape(SIDE * SIDE, LANES), shape(devices, LANES)),
        scratch_shapes=[pltpu.VMEM((PITCH * PITCH, LANES), F32)] * 2,
        name="levels",
    )(f, ez, xe, xee, yup, ydown, before, after, th)
    got = lax.all_to_all(send.reshape(devices, 1, LANES), ("gx", "gy", "gz"), 0, 0).reshape(devices, LANES)
    spot = lax.axis_index(("gx", "gy", "gz")).astype(jnp.int32).reshape(1)
    whole = lambda *dims: pl.BlockSpec(dims, lambda i: (0,) * len(dims))
    out, stats = pl.pallas_call(
        functools.partial(last_kernel, sizes=sizes, counts=counts),
        grid=(2,),
        in_specs=[
            whole(devices, LANES),
            pl.BlockSpec(memory_space=pltpu.SMEM),
            pl.BlockSpec((SIDE, LANES), lambda i: (16 * i, 0)),
            whole(8, LANES),
        ],
        out_specs=[pl.BlockSpec((SIDE, LANES), lambda i: (16 * i, 0)), whole(2, 1, LEVELS)],
        out_shape=(shape(SIDE * SIDE, LANES), shape(2, 1, LEVELS)),
        scratch_shapes=[pltpu.VMEM((devices, LANES), F32)],
        input_output_aliases={2: 0},
        name="last",
    )(got, spot, coef, th)
    return out.reshape(fields.shape), stats


def solution(mesh):
    placed = (P(None, "gx", "gy", "gz"), P())
    return jax.shard_map(shards, mesh=mesh, in_specs=placed, out_specs=placed, check_vma=False)
```

time: 313 us -> 95.2 us (0.30); the launches traced: 308 us -> 95 us
  local copies, waits for them, and re-layouts: 134 us -> 2.59 us
  Pallas kernels: 0 us -> 46.4 us
  waiting for transfers between devices: 61.3 us -> 21.3 us
  blocking collectives: 39.5 us -> 0 us
  starting transfers between devices: 50.7 us -> 24 us
  other arithmetic: 10.7 us -> 0.01 us
  between operations: 11.3 us -> 0.66 us
    unnamed x12 -> x16, local copies, waits for them, and re-layouts: 61.6 us -> 1.92 us
    ppermute x30 -> x6, waiting for transfers between devices: 61.3 us -> 8.66 us  [the longest x3 6.07 us: swap(): before = lax.ppermute(up, axis, [(i, (i + 1) % n) for i in range(n)])]
    pallas_call x0 -> x5, Pallas kernels: none -> 46.4 us  [the longest x1 35.2 us: shards(): pl.pallas_call(levels_kernel, out_shape=(shape(SIDE * SIDE, LANES), shape...]
    slice x65 -> x0, local copies, waits for them, and re-layouts: 40 us -> none  [the longest x15 14.4 us: split_pair(): even_part = lax.slice_in_dim(values, 0, length, 2, axis_dim)]
    psum x4 -> x0, blocking collectives: 39.5 us -> none  [over_axes(): x = lax.psum(x, axis)]
    ppermute x30 -> x6, starting transfers between devices: 50.7 us -> 12.4 us  [the longest x3 6.67 us: swap(): before = lax.ppermute(up, axis, [(i, (i + 1) % n) for i in range(n)])]
    scatter x7 -> x0, local copies, waits for them, and re-layouts: 26.6 us -> none  [shards(): result = shrunk.at[:, ::2, ::2, ::2].set(result)]
    all_to_all x0 -> x1, waiting for transfers between devices: none -> 12.6 us  [shards(): lax.all_to_all(send.reshape(devices, 1, LANES), ('gx', 'gy', 'gz'), 0, 0)]
  transfers between devices with their start and end apart: 30 -> 7, of which waited for: 27 -> 5; matrix products, arithmetic and copies ran while one was open for 7% -> 0% of each run, Pallas kernels for 0% -> 0%
where the time goes in v1:
time: 95.2 us; the launch traced here: 95 us
  Pallas kernels  46.4 us (49%)
  starting transfers between devices  24 us (25%)
  waiting for transfers between devices  21.3 us (22%)
  local copies, waits for them, and re-layouts  2.59 us (3%)
    pallas_call x1, Pallas kernels, shards(): pl.pallas_call(levels_kernel, out_shape=(shape(SIDE * SIDE, LANES), shape...  35.2 us
    all_to_all x1, waiting for transfers between devices, shards(): lax.all_to_all(send.reshape(devices, 1, LANES), ('gx', 'gy', 'gz'), 0, 0)  12.6 us
    all_to_all x1, starting transfers between devices, shards(): lax.all_to_all(send.reshape(devices, 1, LANES), ('gx', 'gy', 'gz'), 0, 0)  11.6 us
    ppermute x3, starting transfers between devices, swap(): before = lax.ppermute(up, axis, [(i, (i + 1) % n) for i in range(n)])  6.67 us
    ppermute x3, waiting for transfers between devices, swap(): before = lax.ppermute(up, axis, [(i, (i + 1) % n) for i in range(n)])  6.07 us
    ppermute x3, starting transfers between devices, swap(): after = lax.ppermute(down, axis, [((i + 1) % n, i) for i in range(n)])  5.74 us
    pallas_call x1, Pallas kernels, shards(): pl.pallas_call(ends_kernel, out_shape=(shape(2 * SIDE, LANES), shape(EXT...  3.72 us
    pallas_call x1, Pallas kernels, shards(): pl.pallas_call(functools.partial(last_kernel, sizes=sizes, counts=counts)...  2.6 us
  transfers between devices with their start and end apart: 7, of which 5 were waited for; matrix products, arithmetic and copies ran while one was open for 0% of the time, Pallas kernels for 0%

profile of v1, /device:TPU:1, one launch (start us, length us, event | category | flops | bytes accessed | tf_op | source)
XLA Modules:
  0.0 95.0 jit_solution(8557850951614707371)
XLA Ops:
  0.6 3.7 %ends.1 = (f32[64,128]{1,0:T(8,128)}, f32[256,128]{1,0:T(8,128)}, f32[256,128]{1,0:T(8,128)}) custom-call(f32[1024,128]{1,0:T(8,128)} %bitcast.7, f32[128,128]{1,0:T(8,128)} %constant.31.table), custom_call_target="tpu_custom_call" | custom-call | tf_op jit(solution)/shard_map/ends/pallas_call | solution.py:382
  4.3 2.1 %collective-permute-start = (f32[64,128]{1,0:T(8,128)}, f32[64,128]{1,0:T(8,128)S(1)}, u32[]{:S(2)}, u32[]{:S(2)}) collective-permute-start(f32[64,128]{1,0:T(8,128)} %get-tuple-element.16.pz), channel_id=1, source_target_pairs={{0,1},{1,2},{2,3},{3,0},{4,5},{5,6},{6,7},{7,4},{8,9},{9,10},{10,1... | collective-permute-start | bytes 98312 | tf_op jit(solution)/shard_map/ppermute | solution.py:378
  6.5 1.4 %collective-permute-start.1 = (f32[64,128]{1,0:T(8,128)}, f32[64,128]{1,0:T(8,128)S(1)}, u32[]{:S(2)}, u32[]{:S(2)}) collective-permute-start(f32[64,128]{1,0:T(8,128)} %get-tuple-element.16.pz), channel_id=1, source_target_pairs={{1,0},{2,1},{3,2},{0,3},{5,4},{6,5},{7,6},{4,7},{9,8},{10,9},{11,1... | collective-permute-start | bytes 98312 | tf_op jit(solution)/shard_map/ppermute | solution.py:379
  7.9 1.5 %collective-permute-done.before = f32[64,128]{1,0:T(8,128)S(1)} collective-permute-done((f32[64,128]{1,0:T(8,128)}, f32[64,128]{1,0:T(8,128)S(1)}, u32[]{:S(2)}, u32[]{:S(2)}) %collective-permute-start) | collective-permute-done | bytes 32800 | tf_op jit(solution)/shard_map/ppermute | solution.py:378
  9.4 0.0 copy-start.5
  9.4 0.0 collective-permute-done.1.after
  9.4 0.0 copy-start.6
  9.4 0.6 copy-done.5
  10.0 0.0 copy-done.6
  10.0 2.5 %depth.1 = (f32[64,128]{1,0:T(8,128)}, f32[160,128]{1,0:T(8,128)}, f32[160,128]{1,0:T(8,128)}) custom-call(f32[64,128]{1,0:T(8,128)} %get-tuple-element.16.pz, f32[64,128]{1,0:T(8,128)} %copy-done.5, f32[64,128]{1,0:T(8,128)} %copy-done.6, f32[256,128]{1,0:T(8,128)} %get-tuple-element.17.fx, f32[7,128,128]{2,1,0:T(8,128)} %constant.26.clone.tables), custom_call_target="tpu_custom_call" | custom-call | tf_op jit(solution)/shard_map/depth/pallas_call | solution.py:389
  12.6 3.2 %collective-permute-start.2 = (f32[160,128]{1,0:T(8,128)}, f32[160,128]{1,0:T(8,128)S(1)}, u32[]{:S(2)}, u32[]{:S(2)}) collective-permute-start(f32[160,128]{1,0:T(8,128)} %get-tuple-element.19.up), channel_id=1, source_target_pairs={{0,32},{32,64},{64,96},{96,128},{128,160},{160,192},{192,224},{224... | collective-permute-start | bytes 245768 | tf_op jit(solution)/shard_map/ppermute | solution.py:378
  15.8 0.3 collective-permute-start.3
  16.1 1.5 %collective-permute-done.2.before = f32[160,128]{1,0:T(8,128)S(1)} collective-permute-done((f32[160,128]{1,0:T(8,128)}, f32[160,128]{1,0:T(8,128)S(1)}, u32[]{:S(2)}, u32[]{:S(2)}) %collective-permute-start.2) | collective-permute-done | bytes 81952 | tf_op jit(solution)/shard_map/ppermute | solution.py:378
  17.6 0.0 copy-start.3
  17.6 2.6 %collective-permute-done.3.after = f32[160,128]{1,0:T(8,128)S(1)} collective-permute-done((f32[160,128]{1,0:T(8,128)}, f32[160,128]{1,0:T(8,128)S(1)}, u32[]{:S(2)}, u32[]{:S(2)}) %collective-permute-start.3) | collective-permute-done | bytes 81952 | tf_op jit(solution)/shard_map/ppermute | solution.py:379
  20.2 0.0 copy-start.4
  20.2 0.0 copy-done.3
  20.2 0.6 copy-done.4
  20.8 2.4 %width.1 = (f32[256,128]{1,0:T(8,128)}, f32[32,128]{1,0:T(8,128)}, f32[184,128]{1,0:T(8,128)}, f32[184,128]{1,0:T(8,128)}) custom-call(f32[160,128]{1,0:T(8,128)} %get-tuple-element.19.up, f32[160,128]{1,0:T(8,128)} %get-tuple-element.20.down, f32[160,128]{1,0:T(8,128)} %copy-done.3, f32[160,128]{1,0:T(8,128)} %copy-done.4, ...), custom_call_target="tpu_custom_call" | custom-call | tf_op jit(solution)/shard_map/width/pallas_call | solution.py:394
  23.2 1.4 %collective-permute-start.4 = (f32[184,128]{1,0:T(8,128)}, f32[184,128]{1,0:T(8,128)S(1)}, u32[]{:S(2)}, u32[]{:S(2)}) collective-permute-start(f32[184,128]{1,0:T(8,128)} %get-tuple-element.24.yup), channel_id=1, source_target_pairs={{0,4},{4,8},{8,12},{12,16},{16,20},{20,24},{24,28},{28,0},{1,5},{5... | collective-permute-start | bytes 282632 | tf_op jit(solution)/shard_map/ppermute | solution.py:378
  24.5 4.0 %collective-permute-start.5 = (f32[184,128]{1,0:T(8,128)}, f32[184,128]{1,0:T(8,128)S(1)}, u32[]{:S(2)}, u32[]{:S(2)}) collective-permute-start(f32[184,128]{1,0:T(8,128)} %get-tuple-element.25.ydown), channel_id=1, source_target_pairs={{4,0},{8,4},{12,8},{16,12},{20,16},{24,20},{28,24},{0,28},{5,1},{9... | collective-permute-start | bytes 282632 | tf_op jit(solution)/shard_map/ppermute | solution.py:379
  28.6 0.0 copy-done.7
  28.6 3.0 %collective-permute-done.4.before = f32[184,128]{1,0:T(8,128)S(1)} collective-permute-done((f32[184,128]{1,0:T(8,128)}, f32[184,128]{1,0:T(8,128)S(1)}, u32[]{:S(2)}, u32[]{:S(2)}) %collective-permute-start.4) | collective-permute-done | bytes 94240 | tf_op jit(solution)/shard_map/ppermute | solution.py:378
  31.6 0.0 collective-permute-done.5.after
  31.6 0.7 broadcast_in_dim.2.th
  32.3 0.0 copy-done.1
  32.3 0.0 copy-done.2
  32.3 35.2 %levels.1 = (f32[1024,128]{1,0:T(8,128)}, f32[256,128]{1,0:T(8,128)}) custom-call(f32[1024,128]{1,0:T(8,128)} %bitcast.8, f32[64,128]{1,0:T(8,128)} %get-tuple-element.18.ez, f32[256,128]{1,0:T(8,128)} %get-tuple-element.22.xe, f32[32,128]{1,0:T(8,128)} %get-tuple-element.23.xee, f32[184,128]{1,0:T(8,128)} %get-tuple-element.24.yup, ...), custom_call_target="tpu_custom_call" | custom-call | tf_op jit(solution)/shard_map/levels/pallas_call | solution.py:400
  67.5 11.6 %all-to-all-start = ((f32[256,1,128]{2,1,0:T(1,128)}), f32[256,1,128]{2,1,0:T(1,128)S(1)}, u32[]{:S(2)}, u32[]{:S(2)}) async-start(f32[256,1,128]{2,1,0:T(1,128)} %bitcast.11), calls=%async_computation | async-start | bytes 262144 | tf_op jit(solution)/shard_map/all_to_all | solution.py:406
  79.1 12.6 %all-to-all-done = f32[256,1,128]{2,1,0:T(1,128)S(1)} async-done(((f32[256,1,128]{2,1,0:T(1,128)}), f32[256,1,128]{2,1,0:T(1,128)S(1)}, u32[]{:S(2)}, u32[]{:S(2)}) %all-to-all-start) | async-done | bytes 131104 | tf_op jit(solution)/shard_map/all_to_all | solution.py:406
  91.7 0.6 copy-done
  92.4 2.6 %last.1 = (f32[1024,128]{1,0:T(8,128)}, f32[2,1,5]{2,1,0:T(1,128)}) custom-call(f32[256,128]{1,0:T(8,128)} %bitcast.10, s32[1]{0:T(128)} %bitcast.4.spot, f32[1024,128]{1,0:T(8,128)} %get-tuple-element.27.coef, f32[8,128]{1,0:T(8,128)} %broadcast_in_dim.2.th), custom_call_target="tpu_custom_call", output_to_operand_aliasing={{0}: (2, {})} | custom-call | tf_op jit(solution)/shard_map/last/pallas_call | solution.py:409
  (6 shorter events, 0.0 us)
Async XLA Ops:
  4.3 5.1 %collective-permute-start = (f32[64,128]{1,0:T(8,128)}, f32[64,128]{1,0:T(8,128)S(1)}, u32[]{:S(2)}, u32[]{:S(2)}) collective-permute-start(f32[64,128]{1,0:T(8,128)} %get-tuple-element.16.pz), channel_id=1, source_target_pairs={{0,1},{1,2},{2,3},{3,0},{4,5},{5,6},{6,7},{7,4},{8,9},{9,10},{10,1... | collective-permute-start | bytes 98312 | tf_op jit(solution)/shard_map/ppermute | solution.py:378
  6.5 3.0 %collective-permute-start.1 = (f32[64,128]{1,0:T(8,128)}, f32[64,128]{1,0:T(8,128)S(1)}, u32[]{:S(2)}, u32[]{:S(2)}) collective-permute-start(f32[64,128]{1,0:T(8,128)} %get-tuple-element.16.pz), channel_id=1, source_target_pairs={{1,0},{2,1},{3,2},{0,3},{5,4},{6,5},{7,6},{4,7},{9,8},{10,9},{11,1... | collective-permute-start | bytes 98312 | tf_op jit(solution)/shard_map/ppermute | solution.py:379
  9.4 0.6 copy-start.5
  9.4 0.6 copy-start.6
  12.6 5.0 %collective-permute-start.2 = (f32[160,128]{1,0:T(8,128)}, f32[160,128]{1,0:T(8,128)S(1)}, u32[]{:S(2)}, u32[]{:S(2)}) collective-permute-start(f32[160,128]{1,0:T(8,128)} %get-tuple-element.19.up), channel_id=1, source_target_pairs={{0,32},{32,64},{64,96},{96,128},{128,160},{160,192},{192,224},{224... | collective-permute-start | bytes 245768 | tf_op jit(solution)/shard_map/ppermute | solution.py:378
  15.8 4.4 %collective-permute-start.3 = (f32[160,128]{1,0:T(8,128)}, f32[160,128]{1,0:T(8,128)S(1)}, u32[]{:S(2)}, u32[]{:S(2)}) collective-permute-start(f32[160,128]{1,0:T(8,128)} %get-tuple-element.20.down), channel_id=1, source_target_pairs={{32,0},{64,32},{96,64},{128,96},{160,128},{192,160},{224,192},{0,2... | collective-permute-start | bytes 245768 | tf_op jit(solution)/shard_map/ppermute | solution.py:379
  17.6 2.6 %copy-start.3 = (f32[160,128]{1,0:T(8,128)}, f32[160,128]{1,0:T(8,128)S(1)}, u32[]{:S(2)}) copy-start(f32[160,128]{1,0:T(8,128)S(1)} %collective-permute-done.2.before) | copy-start | bytes 245764
  20.2 0.7 copy-start.4
  23.2 5.4 %copy-start.7 = (s32[5]{0:T(128)S(1)}, s32[5]{0:T(128)}, u32[]{:S(2)}) copy-start(s32[5]{0:T(128)} %param.5) | copy-start | bytes 64
  23.2 8.4 %collective-permute-start.4 = (f32[184,128]{1,0:T(8,128)}, f32[184,128]{1,0:T(8,128)S(1)}, u32[]{:S(2)}, u32[]{:S(2)}) collective-permute-start(f32[184,128]{1,0:T(8,128)} %get-tuple-element.24.yup), channel_id=1, source_target_pairs={{0,4},{4,8},{8,12},{12,16},{16,20},{20,24},{24,28},{28,0},{1,5},{5... | collective-permute-start | bytes 282632 | tf_op jit(solution)/shard_map/ppermute | solution.py:378
  24.5 7.1 %collective-permute-start.5 = (f32[184,128]{1,0:T(8,128)}, f32[184,128]{1,0:T(8,128)S(1)}, u32[]{:S(2)}, u32[]{:S(2)}) collective-permute-start(f32[184,128]{1,0:T(8,128)} %get-tuple-element.25.ydown), channel_id=1, source_target_pairs={{4,0},{8,4},{12,8},{16,12},{20,16},{24,20},{28,24},{0,28},{5,1},{9... | collective-permute-start | bytes 282632 | tf_op jit(solution)/shard_map/ppermute | solution.py:379
  31.6 0.7 copy-start.1
  31.6 0.7 copy-start.2
  67.5 24.2 %all-to-all-start = ((f32[256,1,128]{2,1,0:T(1,128)}), f32[256,1,128]{2,1,0:T(1,128)S(1)}, u32[]{:S(2)}, u32[]{:S(2)}) async-start(f32[256,1,128]{2,1,0:T(1,128)} %bitcast.11), calls=%async_computation | async-start | bytes 262144 | tf_op jit(solution)/shard_map/all_to_all | solution.py:406
  91.7 0.6 copy-start

commit v2 on v1

--- a/solution.py
+++ b/solution.py
@@ -65,11 +65,15 @@
 
 
 def constant_tables():
-    tables = np.zeros((7, LANES, LANES), np.float32)
+    tables = np.zeros((9, LANES, LANES), np.float32)
     left = np.zeros((EXT, EXT))
     right = np.zeros((EXT, EXT))
     left[:, :NEAR] = LAST.T
     right[:, NEAR:] = FIRST.T
+    spread = np.zeros((2, EXT, EXT))
+    for level in range(NEAR):
+        spread[0, level, EXT - (1 << level)] = 1.0
+        spread[1, NEAR + level, EXT - (1 << level)] = 1.0
     tables[0] = np.tile(WZ.T, (1, GROUP))
     tables[1] = np.kron(np.eye(GROUP), left)
     tables[2] = np.kron(np.eye(GROUP), right)
@@ -77,6 +81,8 @@
         tables[3 + half, :, : EXT * EXT] = np.kron(W[:, half * GROUP : (half + 1) * GROUP].T, np.eye(EXT))
     tables[5, : EXT * EXT, : EXT * EXT] = np.kron(left, np.eye(EXT))
     tables[6, : EXT * EXT, : EXT * EXT] = np.kron(right, np.eye(EXT))
+    tables[7] = np.kron(np.eye(GROUP), spread[0])
+    tables[8] = np.kron(np.eye(GROUP), spread[1])
     return tables
 
 
@@ -206,7 +212,45 @@
     return own + ([(SIDE, EXT, 1)] if level < NEAR else [])
 
 
-def levels_kernel(f, ez, xe, xee, yup, ydown, before, after, th, coef, send, v, q):
+def lift_lanes(level, v, qa, qb, t, d):
+    step = 1 << level
+    own = SIDE // step
+    parts = [c for c in chunks(level) if c[0] < SIDE or level < NEAR - 1]
+    total = own + (EXT if level < NEAR - 1 else 0)
+
+    def sweep(work):
+        def body(half, carry):
+            for k in range(total // 2):
+                j = half * (total // 2) + k
+                x = j if step == 1 else jnp.where(j < own, j * step, j + (SIDE - own))
+                for first, count, stride in parts:
+                    work(pl.ds(x * PITCH + first, count, stride=stride), lanes_of(count))
+            return carry
+
+        lax.fori_loop(0, 2, body, 0)
+
+    def left(at, lane):
+        t[at, :] = roll(v[at, :], step)
+
+    def detail(at, lane):
+        cells = v[at, :]
+        ahead = jnp.where(lane == LANES - step, qb[at, :], roll(cells, -step))
+        d[at, :] = cells - 0.5 * (t[at, :] + ahead)
+
+    def behind(at, lane):
+        t[at, :] = roll(jnp.where(lane == LANES - step, qa[at, :], d[at, :]), step)
+
+    def smooth(at, lane):
+        cells, mid = v[at, :], d[at, :]
+        even = cells + 0.25 * (t[at, :] + roll(mid, -step))
+        place = lane & (2 * step - 1)
+        v[at, :] = jnp.where(place == 0, even, jnp.where(place == step, mid, cells))
+
+    for work in (left, detail, behind, smooth):
+        sweep(work)
+
+
+def levels_kernel(f, ez, xe, xee, yup, ydown, before, after, th, tables, coef, send, v, qa, qb, t, d):
     for x in range(SIDE):
         v[pl.ds(x * PITCH, SIDE), :] = f[pl.ds(x * SIDE, SIDE), :]
     for g in range(EXT):
@@ -229,32 +273,21 @@
             extra = jnp.where(row8 == level, mix(LAST[level], seam_before), extra)
             extra = jnp.where(row8 == NEAR + level, mix(FIRST[level], seam_after), extra)
         block = ez[pl.ds(i * SIDE, SIDE), :] if i < 2 else xee[...]
+        parts = [(dot(block, tables[7 + k]), dot(extra, tables[7 + k])) for k in range(2)]
         for j in range(GROUP if i < 2 else EXT):
             x = i * GROUP + j
-            q[pl.ds(x * PITCH, SIDE), :] = roll(block, -EXT * j)
-            q[pl.ds(x * PITCH + SIDE, EXT), :] = roll(extra, -EXT * j)
+            for ref, (main, rest) in zip((qa, qb), parts):
+                ref[pl.ds(x * PITCH, SIDE), :] = roll(main, -EXT * (j + 1))
+                ref[pl.ds(x * PITCH + SIDE, EXT), :] = roll(rest, -EXT * (j + 1))
 
     for level in range(NEAR):
         step = 1 << level
-        for ref in (v, q):
+        for ref in (v, qa, qb):
             for first, count, stride in chunks(level):
                 lift_chunk(ref, lambda i: pl.ds(i * PITCH + first, count, stride=stride), level, ref is v)
             for first, count, stride in chunks(level):
                 lift_chunk(ref, lambda i: pl.ds(first * PITCH + i, count, stride=stride * PITCH), level, ref is v)
-        planes = list(range(0, SIDE, step)) + (list(range(SIDE, PITCH)) if level < NEAR - 1 else [])
-        for x in planes:
-            for first, count, stride in chunks(level):
-                if first == SIDE and level == NEAR - 1:
-                    continue
-                at = pl.ds(x * PITCH + first, count, stride=stride)
-                lane = lanes_of(count)
-                cells, ends = v[at, :], q[at, :]
-                ahead = jnp.where(lane == 0, roll(ends, -(NEAR + level)), cells)
-                detail = cells - 0.5 * (roll(cells, step) + roll(ahead, -step))
-                behind = jnp.where(lane == LANES - step, roll(ends, -step - level), detail)
-                smooth = cells + 0.25 * (roll(behind, step) + roll(detail, -step))
-                place = lane & (2 * step - 1)
-                v[at, :] = jnp.where(place == 0, smooth, jnp.where(place == step, detail, cells))
+        lift_lanes(level, v, qa, qb, t, d)
 
     energy = [jnp.zeros((8, LANES), F32)] * NEAR
     kept = [jnp.zeros((8, LANES), F32)] * NEAR
@@ -379,30 +412,41 @@
         after = lax.ppermute(down, axis, [((i + 1) % n, i) for i in range(n)])
         return before, after
 
-    pz, fx, fy = pl.pallas_call(
-        ends_kernel,
-        out_shape=(shape(2 * SIDE, LANES), shape(EXT * SIDE, LANES), shape(EXT * SIDE, LANES)),
-        name="ends",
-    )(f, tables[0])
+    here = pl.BlockSpec(memory_space=pltpu.VMEM)
+
+    def pinned(a):
+        return pltpu.with_memory_space_constraint(a, pltpu.VMEM)
+
+    def local(kernel, name, outs, *args, scratch=()):
+        args = [pinned(a) for a in args]
+        return pl.pallas_call(
+            kernel,
+            in_specs=[here] * len(args),
+            out_specs=[here] * len(outs),
+            out_shape=[pltpu.VMEM((rows, LANES), F32) for rows in outs],
+            scratch_shapes=[pltpu.VMEM((rows, LANES), F32) for rows in scratch],
+            name=name,
+        )(*args)
+
+    pz, fx, fy = local(ends_kernel, "ends", (2 * SIDE, EXT * SIDE, EXT * SIDE), f, tables[0])
     before, after = swap(pz, pz, "gz")
-    message = shape((NEAR + 1) * SIDE, LANES)
-    ez, up, down = pl.pallas_call(
-        depth_kernel, out_shape=(shape(2 * SIDE, LANES), message, message), name="depth"
-    )(pz, before, after, fx, tables)
+    message = (NEAR + 1) * SIDE
+    ez, up, down = local(
+        depth_kernel, "depth", (2 * SIDE, message, message), pz, before, after, fx, tables
+    )
     before, after = swap(up, down, "gx")
-    message = shape(NEAR * PITCH + 3 * EXT, LANES)
-    xe, xee, yup, ydown = pl.pallas_call(
-        width_kernel,
-        out_shape=(shape(EXT * SIDE, LANES), shape(SIDE, LANES), message, message),
-        name="width",
-    )(up, down, before, after, fy, ez, wy, tables)
+    message = NEAR * PITCH + 3 * EXT
+    xe, xee, yup, ydown = local(
+        width_kernel, "width", (EXT * SIDE, SIDE, message, message), up, down, before, after, fy, ez, wy, tables
+    )
     before, after = swap(yup, ydown, "gy")
-    coef, send = pl.pallas_call(
+    coef, send = local(
         levels_kernel,
-        out_shape=(shape(SIDE * SIDE, LANES), shape(devices, LANES)),
-        scratch_shapes=[pltpu.VMEM((PITCH * PITCH, LANES), F32)] * 2,
-        name="levels",
-    )(f, ez, xe, xee, yup, ydown, before, after, th)
+        "levels",
+        (SIDE * SIDE, devices),
+        *(f, ez, xe, xee, yup, ydown, before, after, th, tables),
+        scratch=[PITCH * PITCH] * 5,
+    )
     got = lax.all_to_all(send.reshape(devices, 1, LANES), ("gx", "gy", "gz"), 0, 0).reshape(devices, LANES)
     spot = lax.axis_index(("gx", "gy", "gz")).astype(jnp.int32).reshape(1)
     whole = lambda *dims: pl.BlockSpec(dims, lambda i: (0,) * len(dims))
@@ -410,17 +454,17 @@
         functools.partial(last_kernel, sizes=sizes, counts=counts),
         grid=(2,),
         in_specs=[
-            whole(devices, LANES),
+            here,
             pl.BlockSpec(memory_space=pltpu.SMEM),
             pl.BlockSpec((SIDE, LANES), lambda i: (16 * i, 0)),
-            whole(8, LANES),
+            here,
         ],
         out_specs=[pl.BlockSpec((SIDE, LANES), lambda i: (16 * i, 0)), whole(2, 1, LEVELS)],
         out_shape=(shape(SIDE * SIDE, LANES), shape(2, 1, LEVELS)),
         scratch_shapes=[pltpu.VMEM((devices, LANES), F32)],
         input_output_aliases={2: 0},
         name="last",
-    )(got, spot, coef, th)
+    )(pinned(got), spot, coef, pinned(th))
     return out.reshape(fields.shape), stats
 
 

time: 95.2 us -> 59.5 us (0.62)
  Pallas kernels: 46.4 us -> 11.2 us
    pallas_call x4, Pallas kernels: 43.8 us -> 9.7 us  [local(): pl.pallas_call(kernel, in_specs=[here] * len(args), out_specs=[here] * le...]
    pallas_call x1, Pallas kernels: 2.6 us -> 1.49 us  [shards(): pl.pallas_call(functools.partial(last_kernel, sizes=sizes, counts=counts)...]
    unnamed x16 -> x13, local copies, waits for them, and re-layouts: 1.92 us -> 2.75 us
where the time goes in v2:
time: 59.5 us; the launch traced here: 59.4 us
  starting transfers between devices  24.1 us (41%)
  waiting for transfers between devices  20.6 us (35%)
  Pallas kernels  11.2 us (19%)
  local copies, waits for them, and re-layouts  2.82 us (5%)
  between operations  0.68 us (1%)
    all_to_all x1, waiting for transfers between devices, shards(): lax.all_to_all(send.reshape(devices, 1, LANES), ('gx', 'gy', 'gz'), 0, 0)  12.5 us
    all_to_all x1, starting transfers between devices, shards(): lax.all_to_all(send.reshape(devices, 1, LANES), ('gx', 'gy', 'gz'), 0, 0)  11.5 us
    pallas_call x4, Pallas kernels, local(): pl.pallas_call(kernel, in_specs=[here] * len(args), out_specs=[here] * le...  9.7 us
    ppermute x3, starting transfers between devices, swap(): before = lax.ppermute(up, axis, [(i, (i + 1) % n) for i in range(n)])  6.76 us
    ppermute x3, starting transfers between devices, swap(): after = lax.ppermute(down, axis, [((i + 1) % n, i) for i in range(n)])  5.78 us
    ppermute x3, waiting for transfers between devices, swap(): before = lax.ppermute(up, axis, [(i, (i + 1) % n) for i in range(n)])  5.33 us
    unnamed x13, local copies, waits for them, and re-layouts  2.75 us
    ppermute x3, waiting for transfers between devices, swap(): after = lax.ppermute(down, axis, [((i + 1) % n, i) for i in range(n)])  2.7 us
  transfers between devices with their start and end apart: 7, of which 5 were waited for; matrix products, arithmetic and copies ran while one was open for 0% of the time, Pallas kernels for 0%

profile of v2, /device:TPU:1, one launch (start us, length us, event | category | flops | bytes accessed | tf_op | source)
XLA Modules:
  0.0 59.4 jit_solution(12179585895495741090)
XLA Ops:
  0.6 0.0 copy-start
  0.6 0.0 copy-start.1
  0.7 1.1 %copy-done.1 = f32[1,32,32,128]{3,2,1,0:T(8,128)S(1)} copy-done((f32[1,32,32,128]{3,2,1,0:T(8,128)S(1)}, f32[1,32,32,128]{3,2,1,0:T(8,128)}, u32[]{:S(2)}) %copy-start.1) | copy-done | bytes 524312
  1.7 0.0 copy-start.3
  1.7 0.8 %copy-done.3 = f32[128,128]{1,0:T(8,128)S(1)} copy-done((f32[128,128]{1,0:T(8,128)S(1)}, f32[128,128]{1,0:T(8,128)}, u32[]{:S(2)}) %copy-start.3) | copy-done | bytes 65560
  2.6 2.0 %ends.1 = (f32[64,128]{1,0:T(8,128)S(1)}, f32[256,128]{1,0:T(8,128)S(1)}, f32[256,128]{1,0:T(8,128)S(1)}) custom-call(f32[1024,128]{1,0:T(8,128)S(1)} %bitcast.8, f32[128,128]{1,0:T(8,128)S(1)} %copy-done.3), custom_call_target="tpu_custom_call" | custom-call | tf_op jit(solution)/shard_map/ends/pallas_call | solution.py:422
  4.6 2.2 %collective-permute-start = (f32[64,128]{1,0:T(8,128)S(1)}, f32[64,128]{1,0:T(8,128)S(1)}, u32[]{:S(2)}, u32[]{:S(2)}) collective-permute-start(f32[64,128]{1,0:T(8,128)S(1)} %get-tuple-element.16.pz), channel_id=1, source_target_pairs={{0,1},{1,2},{2,3},{3,0},{4,5},{5,6},{6,7},{7,4},{8,9},{9,10},{10,1... | collective-permute-start | bytes 98312 | tf_op jit(solution)/shard_map/ppermute | solution.py:411
  6.8 1.5 %collective-permute-start.1 = (f32[64,128]{1,0:T(8,128)S(1)}, f32[64,128]{1,0:T(8,128)S(1)}, u32[]{:S(2)}, u32[]{:S(2)}) collective-permute-start(f32[64,128]{1,0:T(8,128)S(1)} %get-tuple-element.16.pz), channel_id=1, source_target_pairs={{1,0},{2,1},{3,2},{0,3},{5,4},{6,5},{7,6},{4,7},{9,8},{10,9},{11,1... | collective-permute-start | bytes 98312 | tf_op jit(solution)/shard_map/ppermute | solution.py:412
  8.3 1.2 %collective-permute-done.before = f32[64,128]{1,0:T(8,128)S(1)} collective-permute-done((f32[64,128]{1,0:T(8,128)S(1)}, f32[64,128]{1,0:T(8,128)S(1)}, u32[]{:S(2)}, u32[]{:S(2)}) %collective-permute-start) | collective-permute-done | bytes 32800 | tf_op jit(solution)/shard_map/ppermute | solution.py:411
  9.5 0.0 collective-permute-done.1.after
  9.6 0.0 copy-done
  9.6 0.7 %depth.1 = (f32[64,128]{1,0:T(8,128)S(1)}, f32[160,128]{1,0:T(8,128)S(1)}, f32[160,128]{1,0:T(8,128)S(1)}) custom-call(f32[64,128]{1,0:T(8,128)S(1)} %get-tuple-element.16.pz, f32[64,128]{1,0:T(8,128)S(1)} %collective-permute-done.before, f32[64,128]{1,0:T(8,128)S(1)} %collective-permute-done.1.after, f32[256,128]{1,0:T(8,128)S(1)} %get-tuple-element.17.fx, ...), custom_call_target="tpu_custom_call" | custom-call | tf_op jit(solution)/shard_map/depth/pallas_call | solution.py:422
  10.3 0.0 copy-start.4
  10.3 3.2 %collective-permute-start.2 = (f32[160,128]{1,0:T(8,128)S(1)}, f32[160,128]{1,0:T(8,128)S(1)}, u32[]{:S(2)}, u32[]{:S(2)}) collective-permute-start(f32[160,128]{1,0:T(8,128)S(1)} %get-tuple-element.19.up), channel_id=1, source_target_pairs={{0,32},{32,64},{64,96},{96,128},{128,160},{160,192},{192,224},{224... | collective-permute-start | bytes 245768 | tf_op jit(solution)/shard_map/ppermute | solution.py:411
  13.5 0.3 collective-permute-start.3
  13.8 1.2 %collective-permute-done.2.before = f32[160,128]{1,0:T(8,128)S(1)} collective-permute-done((f32[160,128]{1,0:T(8,128)S(1)}, f32[160,128]{1,0:T(8,128)S(1)}, u32[]{:S(2)}, u32[]{:S(2)}) %collective-permute-start.2) | collective-permute-done | bytes 81952 | tf_op jit(solution)/shard_map/ppermute | solution.py:411
  15.0 2.7 %collective-permute-done.3.after = f32[160,128]{1,0:T(8,128)S(1)} collective-permute-done((f32[160,128]{1,0:T(8,128)S(1)}, f32[160,128]{1,0:T(8,128)S(1)}, u32[]{:S(2)}, u32[]{:S(2)}) %collective-permute-start.3) | collective-permute-done | bytes 81952 | tf_op jit(solution)/shard_map/ppermute | solution.py:412
  17.7 0.0 copy-done.4
  17.7 0.0 copy-start.2
  17.7 0.4 width.1
  18.1 1.4 %collective-permute-start.4 = (f32[184,128]{1,0:T(8,128)S(1)}, f32[184,128]{1,0:T(8,128)S(1)}, u32[]{:S(2)}, u32[]{:S(2)}) collective-permute-start(f32[184,128]{1,0:T(8,128)S(1)} %get-tuple-element.24.yup), channel_id=1, source_target_pairs={{0,4},{4,8},{8,12},{12,16},{16,20},{20,24},{24,28},{28,0},{1,5},{5... | collective-permute-start | bytes 282632 | tf_op jit(solution)/shard_map/ppermute | solution.py:411
  19.4 4.0 %collective-permute-start.5 = (f32[184,128]{1,0:T(8,128)S(1)}, f32[184,128]{1,0:T(8,128)S(1)}, u32[]{:S(2)}, u32[]{:S(2)}) collective-permute-start(f32[184,128]{1,0:T(8,128)S(1)} %get-tuple-element.25.ydown), channel_id=1, source_target_pairs={{4,0},{8,4},{12,8},{16,12},{20,16},{24,20},{28,24},{0,28},{5,1},{9... | collective-permute-start | bytes 282632 | tf_op jit(solution)/shard_map/ppermute | solution.py:412
  23.4 0.0 copy-done.5
  23.5 2.9 %collective-permute-done.4.before = f32[184,128]{1,0:T(8,128)S(1)} collective-permute-done((f32[184,128]{1,0:T(8,128)S(1)}, f32[184,128]{1,0:T(8,128)S(1)}, u32[]{:S(2)}, u32[]{:S(2)}) %collective-permute-start.4) | collective-permute-done | bytes 94240 | tf_op jit(solution)/shard_map/ppermute | solution.py:411
  26.3 0.0 collective-permute-done.5.after
  26.3 0.1 broadcast_in_dim.2.th
  26.4 0.0 copy-done.2
  26.4 6.5 %levels.1 = (f32[1024,128]{1,0:T(8,128)S(1)}, f32[256,128]{1,0:T(8,128)}) custom-call(f32[1024,128]{1,0:T(8,128)S(1)} %bitcast.9, f32[64,128]{1,0:T(8,128)S(1)} %get-tuple-element.18.ez, f32[256,128]{1,0:T(8,128)S(1)} %get-tuple-element.22.xe, f32[32,128]{1,0:T(8,128)S(1)} %get-tuple-element.23.xee, f32[184,128]{1,0:T(8,128)S(1)} %get-tuple-element.24.yup, ...), custom_call_target="tpu_custom_call" | custom-call | tf_op jit(solution)/shard_map/levels/pallas_call | solution.py:422
  33.0 11.5 %all-to-all-start = ((f32[256,1,128]{2,1,0:T(1,128)}), f32[256,1,128]{2,1,0:T(1,128)S(1)}, u32[]{:S(2)}, u32[]{:S(2)}) async-start(f32[256,1,128]{2,1,0:T(1,128)} %bitcast.2), calls=%async_computation | async-start | bytes 262144 | tf_op jit(solution)/shard_map/all_to_all | solution.py:450
  44.5 12.5 %all-to-all-done = f32[256,1,128]{2,1,0:T(1,128)S(1)} async-done(((f32[256,1,128]{2,1,0:T(1,128)}), f32[256,1,128]{2,1,0:T(1,128)S(1)}, u32[]{:S(2)}, u32[]{:S(2)}) %all-to-all-start) | async-done | bytes 131104 | tf_op jit(solution)/shard_map/all_to_all | solution.py:450
  57.1 1.5 %last.1 = (f32[1024,128]{1,0:T(8,128)S(1)}, f32[2,1,5]{2,1,0:T(1,128)}) custom-call(f32[256,128]{1,0:T(8,128)S(1)} %bitcast.10, s32[1]{0:T(128)} %bitcast.4.spot, f32[1024,128]{1,0:T(8,128)S(1)} %get-tuple-element.27.coef, f32[8,128]{1,0:T(8,128)S(1)} %broadcast_in_dim.2.th), custom_call_target="tpu_custom_call", output_to_operand_aliasing={{0}: (2, {})} | custom-call | tf_op jit(solution)/shard_map/last/pallas_call | solution.py:453
  58.6 0.8 %copy.9 = f32[1,32,32,128]{3,2,1,0:T(8,128)} copy(f32[1,32,32,128]{3,2,1,0:T(8,128)S(1)} %bitcast.7) | data formatting | bytes 1048576
  (3 shorter events, 0.0 us)
Async XLA Ops:
  0.6 8.9 %copy-start = (f32[9,128,128]{2,1,0:T(8,128)S(1)}, f32[9,128,128]{2,1,0:T(8,128)}, u32[]{:S(2)}) copy-start(f32[9,128,128]{2,1,0:T(8,128)} %constant.26.clone.tables) | copy-start | bytes 1769476
  0.6 1.1 %copy-start.1 = (f32[1,32,32,128]{3,2,1,0:T(8,128)S(1)}, f32[1,32,32,128]{3,2,1,0:T(8,128)}, u32[]{:S(2)}) copy-start(f32[1,32,32,128]{3,2,1,0:T(8,128)} %param.4) | copy-start | bytes 1572868
  1.7 0.8 %copy-start.3 = (f32[128,128]{1,0:T(8,128)S(1)}, f32[128,128]{1,0:T(8,128)}, u32[]{:S(2)}) copy-start(f32[128,128]{1,0:T(8,128)} %constant.31.table) | copy-start | bytes 196612
  4.6 4.9 %collective-permute-start = (f32[64,128]{1,0:T(8,128)S(1)}, f32[64,128]{1,0:T(8,128)S(1)}, u32[]{:S(2)}, u32[]{:S(2)}) collective-permute-start(f32[64,128]{1,0:T(8,128)S(1)} %get-tuple-element.16.pz), channel_id=1, source_target_pairs={{0,1},{1,2},{2,3},{3,0},{4,5},{5,6},{6,7},{7,4},{8,9},{9,10},{10,1... | collective-permute-start | bytes 98312 | tf_op jit(solution)/shard_map/ppermute | solution.py:411
  6.8 2.8 %collective-permute-start.1 = (f32[64,128]{1,0:T(8,128)S(1)}, f32[64,128]{1,0:T(8,128)S(1)}, u32[]{:S(2)}, u32[]{:S(2)}) collective-permute-start(f32[64,128]{1,0:T(8,128)S(1)} %get-tuple-element.16.pz), channel_id=1, source_target_pairs={{1,0},{2,1},{3,2},{0,3},{5,4},{6,5},{7,6},{4,7},{9,8},{10,9},{11,1... | collective-permute-start | bytes 98312 | tf_op jit(solution)/shard_map/ppermute | solution.py:412
  10.3 7.4 %copy-start.4 = (f32[8,32]{1,0:T(8,128)S(1)}, f32[8,32]{1,0:T(8,128)}, u32[]{:S(2)}) copy-start(f32[8,32]{1,0:T(8,128)} %constant.27.clone.wy) | copy-start | bytes 3076
  10.3 4.7 %collective-permute-start.2 = (f32[160,128]{1,0:T(8,128)S(1)}, f32[160,128]{1,0:T(8,128)S(1)}, u32[]{:S(2)}, u32[]{:S(2)}) collective-permute-start(f32[160,128]{1,0:T(8,128)S(1)} %get-tuple-element.19.up), channel_id=1, source_target_pairs={{0,32},{32,64},{64,96},{96,128},{128,160},{160,192},{192,224},{224... | collective-permute-start | bytes 245768 | tf_op jit(solution)/shard_map/ppermute | solution.py:411
  13.5 4.2 %collective-permute-start.3 = (f32[160,128]{1,0:T(8,128)S(1)}, f32[160,128]{1,0:T(8,128)S(1)}, u32[]{:S(2)}, u32[]{:S(2)}) collective-permute-start(f32[160,128]{1,0:T(8,128)S(1)} %get-tuple-element.20.down), channel_id=1, source_target_pairs={{32,0},{64,32},{96,64},{128,96},{160,128},{192,160},{224,192},{0,2... | collective-permute-start | bytes 245768 | tf_op jit(solution)/shard_map/ppermute | solution.py:412
  17.7 8.7 %copy-start.2 = (f32[1,32,32,128]{3,2,1,0:T(8,128)S(1)}, f32[1,32,32,128]{3,2,1,0:T(8,128)}, u32[]{:S(2)}) copy-start(f32[1,32,32,128]{3,2,1,0:T(8,128)} %param.4) | copy-start | bytes 1572868
  18.1 5.4 %copy-start.5 = (s32[5]{0:T(128)S(1)}, s32[5]{0:T(128)}, u32[]{:S(2)}) copy-start(s32[5]{0:T(128)} %param.5) | copy-start | bytes 64
  18.1 8.3 %collective-permute-start.4 = (f32[184,128]{1,0:T(8,128)S(1)}, f32[184,128]{1,0:T(8,128)S(1)}, u32[]{:S(2)}, u32[]{:S(2)}) collective-permute-start(f32[184,128]{1,0:T(8,128)S(1)} %get-tuple-element.24.yup), channel_id=1, source_target_pairs={{0,4},{4,8},{8,12},{12,16},{16,20},{20,24},{24,28},{28,0},{1,5},{5... | collective-permute-start | bytes 282632 | tf_op jit(solution)/shard_map/ppermute | solution.py:411
  19.4 6.9 %collective-permute-start.5 = (f32[184,128]{1,0:T(8,128)S(1)}, f32[184,128]{1,0:T(8,128)S(1)}, u32[]{:S(2)}, u32[]{:S(2)}) collective-permute-start(f32[184,128]{1,0:T(8,128)S(1)} %get-tuple-element.25.ydown), channel_id=1, source_target_pairs={{4,0},{8,4},{12,8},{16,12},{20,16},{24,20},{28,24},{0,28},{5,1},{9... | collective-permute-start | bytes 282632 | tf_op jit(solution)/shard_map/ppermute | solution.py:412
  33.0 24.1 %all-to-all-start = ((f32[256,1,128]{2,1,0:T(1,128)}), f32[256,1,128]{2,1,0:T(1,128)S(1)}, u32[]{:S(2)}, u32[]{:S(2)}) async-start(f32[256,1,128]{2,1,0:T(1,128)} %bitcast.2), calls=%async_computation | async-start | bytes 262144 | tf_op jit(solution)/shard_map/all_to_all | solution.py:450

commit v3 on v2

--- a/solution.py
+++ b/solution.py
@@ -122,14 +122,18 @@
     return total
 
 
-def ends_kernel(f, table, pz, fx, fy):
-    lane = lanes_of(SIDE)
-    packed = [jnp.zeros((SIDE, LANES), F32)] * 2
-    for x in range(SIDE):
-        out = dot(f[pl.ds(x * SIDE, SIDE), :], table[...])
-        packed[x // GROUP] = jnp.where(lane // EXT == x % GROUP, out, packed[x // GROUP])
-    for half in range(2):
-        pz[pl.ds(half * SIDE, SIDE), :] = packed[half]
+def ends_kernel(f, table, pz):
+    turn = pl.program_id(0)
+    rows = pl.ds(turn // 2 * SIDE, SIDE)
+    group = lanes_of(SIDE) // EXT
+    packed = jnp.where(turn % 2 == 0, jnp.zeros((SIDE, LANES), F32), pz[rows, :])
+    for j in range(GROUP // 2):
+        out = dot(f[pl.ds(j * SIDE, SIDE), :], table[...])
+        packed = jnp.where(group == turn % 2 * (GROUP // 2) + j, out, packed)
+    pz[rows, :] = packed
+
+
+def faces_kernel(f, fx, fy):
     for c in range(SIDE // 8):
         for g, block in enumerate(weighted(8, lambda x: f[pl.ds(x * SIDE + 8 * c, 8), :])):
             fx[pl.ds(g * SIDE + 8 * c, 8), :] = block
@@ -212,49 +216,60 @@
     return own + ([(SIDE, EXT, 1)] if level < NEAR else [])
 
 
-def lift_lanes(level, v, qa, qb, t, d):
+def lift_lanes(level, go, v, qa, qb, d):
     step = 1 << level
-    own = SIDE // step
-    parts = [c for c in chunks(level) if c[0] < SIDE or level < NEAR - 1]
-    total = own + (EXT if level < NEAR - 1 else 0)
-
-    def sweep(work):
-        def body(half, carry):
-            for k in range(total // 2):
-                j = half * (total // 2) + k
-                x = j if step == 1 else jnp.where(j < own, j * step, j + (SIDE - own))
-                for first, count, stride in parts:
-                    work(pl.ds(x * PITCH + first, count, stride=stride), lanes_of(count))
-            return carry
-
-        lax.fori_loop(0, 2, body, 0)
-
-    def left(at, lane):
-        t[at, :] = roll(v[at, :], step)
-
-    def detail(at, lane):
-        cells = v[at, :]
-        ahead = jnp.where(lane == LANES - step, qb[at, :], roll(cells, -step))
-        d[at, :] = cells - 0.5 * (t[at, :] + ahead)
-
-    def behind(at, lane):
-        t[at, :] = roll(jnp.where(lane == LANES - step, qa[at, :], d[at, :]), step)
-
-    def smooth(at, lane):
-        cells, mid = v[at, :], d[at, :]
-        even = cells + 0.25 * (t[at, :] + roll(mid, -step))
-        place = lane & (2 * step - 1)
-        v[at, :] = jnp.where(place == 0, even, jnp.where(place == step, mid, cells))
-
-    for work in (left, detail, behind, smooth):
-        sweep(work)
-
-
-def levels_kernel(f, ez, xe, xee, yup, ydown, before, after, th, tables, coef, send, v, qa, qb, t, d):
+    rows = [
+        (pl.ds(x * PITCH + first, count, stride=stride), count)
+        for x in list(range(0, SIDE, step)) + (list(range(SIDE, PITCH)) if level < NEAR - 1 else [])
+        for first, count, stride in chunks(level)
+        if first < SIDE or level < NEAR - 1
+    ]
+
+    @pl.when(go)
+    def _():
+        for at, count in rows:
+            cells = v[at, :]
+            odd = roll(cells, -step)
+            ahead = roll(jnp.where(lanes_of(count) == LANES - step, qb[at, :], odd), -step)
+            d[at, :] = odd - 0.5 * (cells + ahead)
+
+    @pl.when(go)
+    def _():
+        for at, count in rows:
+            lane = lanes_of(count)
+            cells, mid = v[at, :], d[at, :]
+            odd = roll(mid, step)
+            behind = roll(jnp.where(lane == LANES - step, qa[at, :], odd), step)
+            even = cells + 0.25 * (mid + behind)
+            place = lane & (2 * step - 1)
+            v[at, :] = jnp.where(place == 0, even, jnp.where(place == step, odd, cells))
+
+
+def lift_width(ref, level, masked, pieces):
+    for first, count, stride in pieces:
+        lift_chunk(ref, lambda i: pl.ds(i * PITCH + first, count, stride=stride), level, masked)
+
+
+def prepare_kernel(f, ez, xe, xee, tables, v, qa, qb):
     for x in range(SIDE):
         v[pl.ds(x * PITCH, SIDE), :] = f[pl.ds(x * SIDE, SIDE), :]
     for g in range(EXT):
         v[pl.ds((SIDE + g) * PITCH, SIDE), :] = xe[pl.ds(g * SIDE, SIDE), :]
+    for i in range(3):
+        block = ez[pl.ds(i * SIDE, SIDE), :] if i < 2 else xee[...]
+        parts = [dot(block, tables[7 + k]) for k in range(2)]
+        for j in range(GROUP if i < 2 else EXT):
+            for ref, part in zip((qa, qb), parts):
+                ref[pl.ds((i * GROUP + j) * PITCH, SIDE), :] = roll(part, -EXT * (j + 1))
+    for ref in (v, qa, qb):
+        lift_width(ref, 0, False, chunks(0)[:-1])
+
+
+def levels_kernel(
+    spot, yup, ydown, before, after, th, tables, v_in, qa_in, qb_in, coef, send, v, qa, qb, d
+):
+    del v_in, qa_in, qb_in
+    go = spot[0] >= 0
     for c in range(PITCH // 8):
         rows = [pl.ds(g * PITCH + 8 * c, 8) for g in range(NEAR)]
         seam_before = [before[r, :] for r in rows] + [ydown[r, :] for r in rows]
@@ -272,22 +287,22 @@
         for level in range(NEAR):
             extra = jnp.where(row8 == level, mix(LAST[level], seam_before), extra)
             extra = jnp.where(row8 == NEAR + level, mix(FIRST[level], seam_after), extra)
-        block = ez[pl.ds(i * SIDE, SIDE), :] if i < 2 else xee[...]
-        parts = [(dot(block, tables[7 + k]), dot(extra, tables[7 + k])) for k in range(2)]
+        parts = [dot(extra, tables[7 + k]) for k in range(2)]
         for j in range(GROUP if i < 2 else EXT):
-            x = i * GROUP + j
-            for ref, (main, rest) in zip((qa, qb), parts):
-                ref[pl.ds(x * PITCH, SIDE), :] = roll(main, -EXT * (j + 1))
-                ref[pl.ds(x * PITCH + SIDE, EXT), :] = roll(rest, -EXT * (j + 1))
+            for ref, part in zip((qa, qb), parts):
+                ref[pl.ds((i * GROUP + j) * PITCH + SIDE, EXT), :] = roll(part, -EXT * (j + 1))
 
     for level in range(NEAR):
-        step = 1 << level
         for ref in (v, qa, qb):
+            lift_width(ref, level, ref is v, chunks(level)[-1:] if level == 0 else chunks(level))
             for first, count, stride in chunks(level):
-                lift_chunk(ref, lambda i: pl.ds(i * PITCH + first, count, stride=stride), level, ref is v)
-            for first, count, stride in chunks(level):
-                lift_chunk(ref, lambda i: pl.ds(first * PITCH + i, count, stride=stride * PITCH), level, ref is v)
-        lift_lanes(level, v, qa, qb, t, d)
+                lift_chunk(
+                    ref,
+                    lambda i: pl.ds(first * PITCH + i, count, stride=stride * PITCH),
+                    level,
+                    ref is v,
+                )
+        lift_lanes(level, go, v, qa, qb, d)
 
     energy = [jnp.zeros((8, LANES), F32)] * NEAR
     kept = [jnp.zeros((8, LANES), F32)] * NEAR
@@ -417,19 +432,31 @@
     def pinned(a):
         return pltpu.with_memory_space_constraint(a, pltpu.VMEM)
 
-    def local(kernel, name, outs, *args, scratch=()):
+    def local(kernel, name, outs, *args, scalars=(), scratch=(), aliases={}):
         args = [pinned(a) for a in args]
         return pl.pallas_call(
             kernel,
-            in_specs=[here] * len(args),
+            in_specs=[pl.BlockSpec(memory_space=pltpu.SMEM)] * len(scalars) + [here] * len(args),
             out_specs=[here] * len(outs),
             out_shape=[pltpu.VMEM((rows, LANES), F32) for rows in outs],
             scratch_shapes=[pltpu.VMEM((rows, LANES), F32) for rows in scratch],
+            input_output_aliases=aliases,
+            compiler_params=pltpu.CompilerParams(vmem_limit_bytes=8 << 20),
             name=name,
-        )(*args)
-
-    pz, fx, fy = local(ends_kernel, "ends", (2 * SIDE, EXT * SIDE, EXT * SIDE), f, tables[0])
+        )(*scalars, *args)
+
+    spot = lax.axis_index(("gx", "gy", "gz")).astype(jnp.int32).reshape(1)
+    whole = lambda *dims: pl.BlockSpec(dims, lambda i: (0,) * len(dims))
+    pz = pl.pallas_call(
+        ends_kernel,
+        grid=(4,),
+        in_specs=[pl.BlockSpec((SIDE * SIDE // 4, LANES), lambda i: (i, 0)), whole(LANES, LANES)],
+        out_specs=here,
+        out_shape=pltpu.VMEM((2 * SIDE, LANES), F32),
+        name="ends",
+    )(f, tables[0])
     before, after = swap(pz, pz, "gz")
+    fx, fy = local(faces_kernel, "faces", (EXT * SIDE, EXT * SIDE), f)
     message = (NEAR + 1) * SIDE
     ez, up, down = local(
         depth_kernel, "depth", (2 * SIDE, message, message), pz, before, after, fx, tables
@@ -440,16 +467,19 @@
         width_kernel, "width", (EXT * SIDE, SIDE, message, message), up, down, before, after, fy, ez, wy, tables
     )
     before, after = swap(yup, ydown, "gy")
-    coef, send = local(
+    block = PITCH * PITCH
+    v, qa, qb = local(prepare_kernel, "prepare", (block,) * 3, f, ez, xe, xee, tables)
+    coef, send, *_ = local(
         levels_kernel,
         "levels",
-        (SIDE * SIDE, devices),
-        *(f, ez, xe, xee, yup, ydown, before, after, th, tables),
-        scratch=[PITCH * PITCH] * 5,
+        (SIDE * SIDE, devices, block, block, block),
+        *(yup, ydown, before, after, th, tables, v, qa, qb),
+        scalars=(spot,),
+        scratch=(block,),
+        aliases={7: 2, 8: 3, 9: 4},
     )
+    send, spot, th = lax.optimization_barrier((send, spot, th))
     got = lax.all_to_all(send.reshape(devices, 1, LANES), ("gx", "gy", "gz"), 0, 0).reshape(devices, LANES)
-    spot = lax.axis_index(("gx", "gy", "gz")).astype(jnp.int32).reshape(1)
-    whole = lambda *dims: pl.BlockSpec(dims, lambda i: (0,) * len(dims))
     out, stats = pl.pallas_call(
         functools.partial(last_kernel, sizes=sizes, counts=counts),
         grid=(2,),

time: 59.5 us -> 56.6 us (0.951)
  blocking collectives: 0 us -> 21.6 us
  waiting for transfers between devices: 20.6 us -> 8.59 us
  starting transfers between devices: 24.1 us -> 12.4 us
  local copies, waits for them, and re-layouts: 2.82 us -> 1.93 us
    all_to_all x0 -> x1, blocking collectives: none -> 21.6 us  [shards(): lax.all_to_all(send.reshape(devices, 1, LANES), ('gx', 'gy', 'gz'), 0, 0)]
    all_to_all x1 -> x0, waiting for transfers between devices: 12.5 us -> none  [shards(): lax.all_to_all(send.reshape(devices, 1, LANES), ('gx', 'gy', 'gz'), 0, 0)]
    all_to_all x1 -> x0, starting transfers between devices: 11.5 us -> none  [shards(): lax.all_to_all(send.reshape(devices, 1, LANES), ('gx', 'gy', 'gz'), 0, 0)]
    ppermute x3, starting transfers between devices: 6.76 us -> 4.87 us  [swap(): before = lax.ppermute(up, axis, [(i, (i + 1) % n) for i in range(n)])]
    ppermute x3, starting transfers between devices: 5.78 us -> 7.56 us  [swap(): after = lax.ppermute(down, axis, [((i + 1) % n, i) for i in range(n)])]
    unnamed x13 -> x11, local copies, waits for them, and re-layouts: 2.75 us -> 1.85 us
    ppermute x3, waiting for transfers between devices: 5.33 us -> 6.21 us  [swap(): before = lax.ppermute(up, axis, [(i, (i + 1) % n) for i in range(n)])]
    pallas_call x4 -> x6, Pallas kernels: 9.7 us -> 9.63 us  [the longest x5 6.18 us: local(): pl.pallas_call(kernel, in_specs=[pl.BlockSpec(memory_space=pltpu.SMEM)] *...]
  transfers between devices with their start and end apart: 7 -> 6, of which waited for: 5 -> 4; matrix products, arithmetic and copies ran while one was open for 0% -> 0% of each run, Pallas kernels for 0% -> 2%
where the time goes in v3:
time: 56.6 us; the launch traced here: 56.4 us
  blocking collectives  21.6 us (38%)
  starting transfers between devices  12.4 us (22%)
  Pallas kernels  11.1 us (20%)
  waiting for transfers between devices  8.59 us (15%)
  local copies, waits for them, and re-layouts  1.93 us (3%)
  between operations  0.68 us (1%)
    all_to_all x1, blocking collectives, shards(): lax.all_to_all(send.reshape(devices, 1, LANES), ('gx', 'gy', 'gz'), 0, 0)  21.6 us
    ppermute x3, starting transfers between devices, swap(): after = lax.ppermute(down, axis, [((i + 1) % n, i) for i in range(n)])  7.56 us
    ppermute x3, waiting for transfers between devices, swap(): before = lax.ppermute(up, axis, [(i, (i + 1) % n) for i in range(n)])  6.21 us
    pallas_call x5, Pallas kernels, local(): pl.pallas_call(kernel, in_specs=[pl.BlockSpec(memory_space=pltpu.SMEM)] *...  6.18 us
    ppermute x3, starting transfers between devices, swap(): before = lax.ppermute(up, axis, [(i, (i + 1) % n) for i in range(n)])  4.87 us
    pallas_call x1, Pallas kernels, shards(): pl.pallas_call(ends_kernel, grid=(4,), in_specs=[pl.BlockSpec((SIDE * SID...  3.46 us
    ppermute x3, waiting for transfers between devices, swap(): after = lax.ppermute(down, axis, [((i + 1) % n, i) for i in range(n)])  2.39 us
    unnamed x11, local copies, waits for them, and re-layouts  1.85 us
  transfers between devices with their start and end apart: 6, of which 4 were waited for; matrix products, arithmetic and copies ran while one was open for 0% of the time, Pallas kernels for 2%

profile of v3, /device:TPU:1, one launch (start us, length us, event | category | flops | bytes accessed | tf_op | source)
XLA Modules:
  0.0 56.4 jit_solution(17164414900273304266)
XLA Ops:
  0.6 0.0 copy-start
  0.6 3.5 %ends.1.pz = f32[64,128]{1,0:T(8,128)S(1)} custom-call(f32[1024,128]{1,0:T(8,128)} %bitcast.8, f32[128,128]{1,0:T(8,128)} %constant.31.table), custom_call_target="tpu_custom_call" | custom-call | tf_op jit(solution)/shard_map/ends/pallas_call | solution.py:450
  4.1 3.6 %collective-permute-start.1 = (f32[64,128]{1,0:T(8,128)S(1)}, f32[64,128]{1,0:T(8,128)S(1)}, u32[]{:S(2)}, u32[]{:S(2)}) collective-permute-start(f32[64,128]{1,0:T(8,128)S(1)} %ends.1.pz), channel_id=1, source_target_pairs={{1,0},{2,1},{3,2},{0,3},{5,4},{6,5},{7,6},{4,7},{9,8},{10,9},{11,1... | collective-permute-start | bytes 98312 | tf_op jit(solution)/shard_map/ppermute | solution.py:427
  7.7 0.0 collective-permute-start
  7.7 0.0 copy-start.1
  7.7 1.0 %copy-done.1 = f32[1,32,32,128]{3,2,1,0:T(8,128)S(1)} copy-done((f32[1,32,32,128]{3,2,1,0:T(8,128)S(1)}, f32[1,32,32,128]{3,2,1,0:T(8,128)}, u32[]{:S(2)}) %copy-start.1) | copy-done | bytes 524312
  8.7 0.4 faces.1
  9.1 0.0 collective-permute-done.1.after
  9.1 2.5 %collective-permute-done.before = f32[64,128]{1,0:T(8,128)S(1)} collective-permute-done((f32[64,128]{1,0:T(8,128)S(1)}, f32[64,128]{1,0:T(8,128)S(1)}, u32[]{:S(2)}, u32[]{:S(2)}) %collective-permute-start) | collective-permute-done | bytes 32800 | tf_op jit(solution)/shard_map/ppermute | solution.py:426
  11.6 0.0 copy-done
  11.6 0.7 %depth.1 = (f32[64,128]{1,0:T(8,128)S(1)}, f32[160,128]{1,0:T(8,128)S(1)}, f32[160,128]{1,0:T(8,128)S(1)}) custom-call(f32[64,128]{1,0:T(8,128)S(1)} %ends.1.pz, f32[64,128]{1,0:T(8,128)S(1)} %collective-permute-done.before, f32[64,128]{1,0:T(8,128)S(1)} %collective-permute-done.1.after, f32[256,128]{1,0:T(8,128)S(1)} %get-tuple-element.21.fx, ...), custom_call_target="tpu_custom_call" | custom-call | tf_op jit(solution)/shard_map/depth/pallas_call | solution.py:437
  12.4 0.0 copy-start.3
  12.4 3.2 %collective-permute-start.2 = (f32[160,128]{1,0:T(8,128)S(1)}, f32[160,128]{1,0:T(8,128)S(1)}, u32[]{:S(2)}, u32[]{:S(2)}) collective-permute-start(f32[160,128]{1,0:T(8,128)S(1)} %get-tuple-element.22.up), channel_id=1, source_target_pairs={{0,32},{32,64},{64,96},{96,128},{128,160},{160,192},{192,224},{224... | collective-permute-start | bytes 245768 | tf_op jit(solution)/shard_map/ppermute | solution.py:426
  15.6 0.0 collective-permute-start.3
  15.6 1.5 %collective-permute-done.2.before = f32[160,128]{1,0:T(8,128)S(1)} collective-permute-done((f32[160,128]{1,0:T(8,128)S(1)}, f32[160,128]{1,0:T(8,128)S(1)}, u32[]{:S(2)}, u32[]{:S(2)}) %collective-permute-start.2) | collective-permute-done | bytes 81952 | tf_op jit(solution)/shard_map/ppermute | solution.py:426
  17.1 2.4 %collective-permute-done.3.after = f32[160,128]{1,0:T(8,128)S(1)} collective-permute-done((f32[160,128]{1,0:T(8,128)S(1)}, f32[160,128]{1,0:T(8,128)S(1)}, u32[]{:S(2)}, u32[]{:S(2)}) %collective-permute-start.3) | collective-permute-done | bytes 81952 | tf_op jit(solution)/shard_map/ppermute | solution.py:427
  19.5 0.0 copy-done.3
  19.5 0.0 copy-start.2
  19.5 0.4 width.1
  19.9 0.0 copy-start.4
  19.9 1.7 %collective-permute-start.4 = (f32[184,128]{1,0:T(8,128)S(1)}, f32[184,128]{1,0:T(8,128)S(1)}, u32[]{:S(2)}, u32[]{:S(2)}) collective-permute-start(f32[184,128]{1,0:T(8,128)S(1)} %get-tuple-element.26.yup), channel_id=1, source_target_pairs={{0,4},{4,8},{8,12},{12,16},{16,20},{20,24},{24,28},{28,0},{1,5},{5... | collective-permute-start | bytes 282632 | tf_op jit(solution)/shard_map/ppermute | solution.py:426
  21.5 4.0 %collective-permute-start.5 = (f32[184,128]{1,0:T(8,128)S(1)}, f32[184,128]{1,0:T(8,128)S(1)}, u32[]{:S(2)}, u32[]{:S(2)}) collective-permute-start(f32[184,128]{1,0:T(8,128)S(1)} %get-tuple-element.27.ydown), channel_id=1, source_target_pairs={{4,0},{8,4},{12,8},{16,12},{20,16},{24,20},{28,24},{0,28},{5,1},{9... | collective-permute-start | bytes 282632 | tf_op jit(solution)/shard_map/ppermute | solution.py:427
  25.5 0.0 copy-done.4
  25.5 0.0 copy-done.2
  25.5 0.6 %prepare.1 = (f32[1600,128]{1,0:T(8,128)S(1)}, f32[1600,128]{1,0:T(8,128)S(1)}, f32[1600,128]{1,0:T(8,128)S(1)}) custom-call(f32[1024,128]{1,0:T(8,128)S(1)} %bitcast.10, f32[64,128]{1,0:T(8,128)S(1)} %get-tuple-element.25.ez, f32[256,128]{1,0:T(8,128)S(1)} %get-tuple-element.28.xe, f32[32,128]{1,0:T(8,128)S(1)} %get-tuple-element.29.xee, ...), custom_call_target="tpu_custom_call" | custom-call | tf_op jit(solution)/shard_map/prepare/pallas_call | solution.py:437
  26.2 2.2 %collective-permute-done.4.before = f32[184,128]{1,0:T(8,128)S(1)} collective-permute-done((f32[184,128]{1,0:T(8,128)S(1)}, f32[184,128]{1,0:T(8,128)S(1)}, u32[]{:S(2)}, u32[]{:S(2)}) %collective-permute-start.4) | collective-permute-done | bytes 94240 | tf_op jit(solution)/shard_map/ppermute | solution.py:426
  28.4 0.0 collective-permute-done.5.after
  28.4 0.1 broadcast_in_dim.2.th
  28.5 4.0 %levels.1 = (f32[1024,128]{1,0:T(8,128)S(1)}, f32[256,128]{1,0:T(8,128)S(1)}, f32[1600,128]{1,0:T(8,128)S(1)}, f32[1600,128]{1,0:T(8,128)S(1)}, f32[1600,128]{1,0:T(8,128)S(1)}) custom-call(s32[1]{0:T(128)} %bitcast.spot, f32[184,128]{1,0:T(8,128)S(1)} %get-tuple-element.26.yup, ...), custom_call_target="tpu_custom_call", output_to_operand_aliasing={{2}: (7, {}), {3}: (8, {}), {4}: (9, {})} | custom-call | tf_op jit(solution)/shard_map/levels/pallas_call | solution.py:437
  32.5 21.6 %all_to_all.5 = f32[256,1,128]{2,1,0:T(1,128)S(1)} all-to-all(f32[256,1,128]{2,1,0:T(1,128)S(1)} %bitcast.12), channel_id=1, replica_groups=mesh['gx'=8,'gy'=8,'gz'=4] {'gx','gy','gz'}, dimensions={0} | all-to-all | bytes 262144 | tf_op jit(solution)/shard_map/all_to_all | solution.py:482
  54.1 1.5 %last.1 = (f32[1024,128]{1,0:T(8,128)S(1)}, f32[2,1,5]{2,1,0:T(1,128)}) custom-call(f32[256,128]{1,0:T(8,128)S(1)} %bitcast.11, s32[1]{0:T(128)} %bitcast.spot, f32[1024,128]{1,0:T(8,128)S(1)} %get-tuple-element.36.coef, f32[8,128]{1,0:T(8,128)S(1)} %broadcast_in_dim.2.th), custom_call_target="tpu_custom_call", output_to_operand_aliasing={{0}: (2, {})} | custom-call | tf_op jit(solution)/shard_map/last/pallas_call | solution.py:483
  55.6 0.8 %copy.15 = f32[1,32,32,128]{3,2,1,0:T(8,128)} copy(f32[1,32,32,128]{3,2,1,0:T(8,128)S(1)} %bitcast.7) | data formatting | bytes 1048576
  (2 shorter events, 0.0 us)
Async XLA Ops:
  0.6 11.0 %copy-start = (f32[9,128,128]{2,1,0:T(8,128)S(1)}, f32[9,128,128]{2,1,0:T(8,128)}, u32[]{:S(2)}) copy-start(f32[9,128,128]{2,1,0:T(8,128)} %constant.26.clone.tables) | copy-start | bytes 1769476
  4.1 5.0 %collective-permute-start.1 = (f32[64,128]{1,0:T(8,128)S(1)}, f32[64,128]{1,0:T(8,128)S(1)}, u32[]{:S(2)}, u32[]{:S(2)}) collective-permute-start(f32[64,128]{1,0:T(8,128)S(1)} %ends.1.pz), channel_id=1, source_target_pairs={{1,0},{2,1},{3,2},{0,3},{5,4},{6,5},{7,6},{4,7},{9,8},{10,9},{11,1... | collective-permute-start | bytes 98312 | tf_op jit(solution)/shard_map/ppermute | solution.py:427
  7.7 4.0 %collective-permute-start = (f32[64,128]{1,0:T(8,128)S(1)}, f32[64,128]{1,0:T(8,128)S(1)}, u32[]{:S(2)}, u32[]{:S(2)}) collective-permute-start(f32[64,128]{1,0:T(8,128)S(1)} %ends.1.pz), channel_id=1, source_target_pairs={{0,1},{1,2},{2,3},{3,0},{4,5},{5,6},{6,7},{7,4},{8,9},{9,10},{10,1... | collective-permute-start | bytes 98312 | tf_op jit(solution)/shard_map/ppermute | solution.py:426
  7.7 1.0 %copy-start.1 = (f32[1,32,32,128]{3,2,1,0:T(8,128)S(1)}, f32[1,32,32,128]{3,2,1,0:T(8,128)}, u32[]{:S(2)}) copy-start(f32[1,32,32,128]{3,2,1,0:T(8,128)} %param.4) | copy-start | bytes 1572868
  12.4 7.1 %copy-start.3 = (f32[8,32]{1,0:T(8,128)S(1)}, f32[8,32]{1,0:T(8,128)}, u32[]{:S(2)}) copy-start(f32[8,32]{1,0:T(8,128)} %constant.27.clone.wy) | copy-start | bytes 3076
  12.4 4.7 %collective-permute-start.2 = (f32[160,128]{1,0:T(8,128)S(1)}, f32[160,128]{1,0:T(8,128)S(1)}, u32[]{:S(2)}, u32[]{:S(2)}) collective-permute-start(f32[160,128]{1,0:T(8,128)S(1)} %get-tuple-element.22.up), channel_id=1, source_target_pairs={{0,32},{32,64},{64,96},{96,128},{128,160},{160,192},{192,224},{224... | collective-permute-start | bytes 245768 | tf_op jit(solution)/shard_map/ppermute | solution.py:426
  15.6 3.9 %collective-permute-start.3 = (f32[160,128]{1,0:T(8,128)S(1)}, f32[160,128]{1,0:T(8,128)S(1)}, u32[]{:S(2)}, u32[]{:S(2)}) collective-permute-start(f32[160,128]{1,0:T(8,128)S(1)} %get-tuple-element.23.down), channel_id=1, source_target_pairs={{32,0},{64,32},{96,64},{128,96},{160,128},{192,160},{224,192},{0,2... | collective-permute-start | bytes 245768 | tf_op jit(solution)/shard_map/ppermute | solution.py:427
  19.5 6.1 %copy-start.2 = (f32[1,32,32,128]{3,2,1,0:T(8,128)S(1)}, f32[1,32,32,128]{3,2,1,0:T(8,128)}, u32[]{:S(2)}) copy-start(f32[1,32,32,128]{3,2,1,0:T(8,128)} %param.4) | copy-start | bytes 1572868
  19.9 5.7 %copy-start.4 = (s32[5]{0:T(128)S(1)}, s32[5]{0:T(128)}, u32[]{:S(2)}) copy-start(s32[5]{0:T(128)} %param.5) | copy-start | bytes 64
  19.9 8.6 %collective-permute-start.4 = (f32[184,128]{1,0:T(8,128)S(1)}, f32[184,128]{1,0:T(8,128)S(1)}, u32[]{:S(2)}, u32[]{:S(2)}) collective-permute-start(f32[184,128]{1,0:T(8,128)S(1)} %get-tuple-element.26.yup), channel_id=1, source_target_pairs={{0,4},{4,8},{8,12},{12,16},{16,20},{20,24},{24,28},{28,0},{1,5},{5... | collective-permute-start | bytes 282632 | tf_op jit(solution)/shard_map/ppermute | solution.py:426
  21.5 6.9 %collective-permute-start.5 = (f32[184,128]{1,0:T(8,128)S(1)}, f32[184,128]{1,0:T(8,128)S(1)}, u32[]{:S(2)}, u32[]{:S(2)}) collective-permute-start(f32[184,128]{1,0:T(8,128)S(1)} %get-tuple-element.27.ydown), channel_id=1, source_target_pairs={{4,0},{8,4},{12,8},{16,12},{20,16},{24,20},{28,24},{0,28},{5,1},{9... | collective-permute-start | bytes 282632 | tf_op jit(solution)/shard_map/ppermute | solution.py:427

commit v4 on v3

--- a/solution.py
+++ b/solution.py
@@ -65,7 +65,6 @@
 
 
 def constant_tables():
-    tables = np.zeros((9, LANES, LANES), np.float32)
     left = np.zeros((EXT, EXT))
     right = np.zeros((EXT, EXT))
     left[:, :NEAR] = LAST.T
@@ -74,16 +73,20 @@
     for level in range(NEAR):
         spread[0, level, EXT - (1 << level)] = 1.0
         spread[1, NEAR + level, EXT - (1 << level)] = 1.0
-    tables[0] = np.tile(WZ.T, (1, GROUP))
-    tables[1] = np.kron(np.eye(GROUP), left)
-    tables[2] = np.kron(np.eye(GROUP), right)
+    each = np.eye(GROUP)
+    solve = [np.kron(each, left), np.kron(each, right)]
+    corner = np.zeros((2, LANES, LANES))
+    corner[:, : EXT * EXT, : EXT * EXT] = [np.kron(left, np.eye(EXT)), np.kron(right, np.eye(EXT))]
+    ends = []
     for half in range(2):
-        tables[3 + half, :, : EXT * EXT] = np.kron(W[:, half * GROUP : (half + 1) * GROUP].T, np.eye(EXT))
-    tables[5, : EXT * EXT, : EXT * EXT] = np.kron(left, np.eye(EXT))
-    tables[6, : EXT * EXT, : EXT * EXT] = np.kron(right, np.eye(EXT))
-    tables[7] = np.kron(np.eye(GROUP), spread[0])
-    tables[8] = np.kron(np.eye(GROUP), spread[1])
-    return tables
+        end = np.zeros((LANES, LANES))
+        end[:, : EXT * EXT] = np.kron(W[:, half * GROUP : (half + 1) * GROUP].T, np.eye(EXT))
+        ends += [side @ end for side in solve]
+    tables = np.concatenate(solve + ends + list(corner) + [np.kron(each, part) for part in spread])
+    return np.tile(WZ.T, (1, GROUP)).astype(np.float32), tables.astype(np.float32)
+
+
+SOLVE, ENDS, CORNER, SPREAD = (pl.ds(LANES * i, LANES * n) for i, n in ((0, 2), (2, 4), (6, 2), (8, 2)))
 
 
 def dot(a, b):
@@ -123,14 +126,14 @@
 
 
 def ends_kernel(f, table, pz):
-    turn = pl.program_id(0)
-    rows = pl.ds(turn // 2 * SIDE, SIDE)
+    out = dot(f[...], table[...])
     group = lanes_of(SIDE) // EXT
-    packed = jnp.where(turn % 2 == 0, jnp.zeros((SIDE, LANES), F32), pz[rows, :])
-    for j in range(GROUP // 2):
-        out = dot(f[pl.ds(j * SIDE, SIDE), :], table[...])
-        packed = jnp.where(group == turn % 2 * (GROUP // 2) + j, out, packed)
-    pz[rows, :] = packed
+    for half in range(2):
+        packed = jnp.zeros((SIDE, LANES), F32)
+        for j in range(GROUP):
+            first = (half * GROUP + j) * SIDE
+            packed = jnp.where(group == j, out[first : first + SIDE], packed)
+        pz[pl.ds(half * SIDE, SIDE), :] = packed
 
 
 def faces_kernel(f, fx, fy):
@@ -143,17 +146,11 @@
 
 
 def depth_kernel(pz, before, after, fx, tables, ez, up, down):
-    slot = lanes_of(SIDE) % EXT
-    fxe = None
-    for half in range(2):
-        rows = pl.ds(half * SIDE, SIDE)
-        own = pz[rows, :]
-        full = dot(jnp.where(slot < NEAR, before[rows, :], own), tables[1]) + dot(
-            jnp.where(slot < NEAR, own, after[rows, :]), tables[2]
-        )
-        ez[rows, :] = full
-        part = dot(full, tables[3 + half])
-        fxe = part if fxe is None else fxe + part
+    near = lanes_of(2 * SIDE) % EXT < NEAR
+    own = pz[...]
+    sides = jnp.concatenate([jnp.where(near, before[...], own), jnp.where(near, own, after[...])], axis=1)
+    fxe = dot(jnp.concatenate([sides[:SIDE], sides[SIDE:]], axis=1), tables[ENDS, :])
+    ez[...] = dot(sides, tables[SOLVE, :])
     for g in range(NEAR):
         up[pl.ds(g * SIDE, SIDE), :] = fx[pl.ds(g * SIDE, SIDE), :]
         down[pl.ds(g * SIDE, SIDE), :] = fx[pl.ds((NEAR + g) * SIDE, SIDE), :]
@@ -171,12 +168,11 @@
         for level in range(NEAR):
             xe[pl.ds(level * SIDE + 8 * c, 8), :] = mix(LAST[level], seam_before)
             xe[pl.ds((NEAR + level) * SIDE + 8 * c, 8), :] = mix(FIRST[level], seam_after)
-    slot = lanes_of(SIDE) // EXT
+    near = lanes_of(SIDE) // EXT < NEAR
     rows = pl.ds(NEAR * SIDE, SIDE)
     own = up[rows, :]
-    corner = dot(jnp.where(slot < NEAR, before[rows, :], own), tables[5]) + dot(
-        jnp.where(slot < NEAR, own, after[rows, :]), tables[6]
-    )
+    sides = [jnp.where(near, before[rows, :], own), jnp.where(near, own, after[rows, :])]
+    corner = dot(jnp.concatenate(sides, axis=1), tables[CORNER, :])
     xee[...] = corner
     sums = weighted(EXT, lambda y: xe[pl.ds(y, EXT, stride=SIDE), :])
     for g in range(EXT):
@@ -216,13 +212,12 @@
     return own + ([(SIDE, EXT, 1)] if level < NEAR else [])
 
 
-def lift_lanes(level, go, v, qa, qb, d):
+def lift_lanes(level, go, v, qa, qb, d, pieces):
     step = 1 << level
     rows = [
         (pl.ds(x * PITCH + first, count, stride=stride), count)
         for x in list(range(0, SIDE, step)) + (list(range(SIDE, PITCH)) if level < NEAR - 1 else [])
-        for first, count, stride in chunks(level)
-        if first < SIDE or level < NEAR - 1
+        for first, count, stride in pieces
     ]
 
     @pl.when(go)
@@ -250,19 +245,51 @@
         lift_chunk(ref, lambda i: pl.ds(i * PITCH + first, count, stride=stride), level, masked)
 
 
-def prepare_kernel(f, ez, xe, xee, tables, v, qa, qb):
+def prepare_kernel(spot, f, ez, xe, xee, tables, v, qa, qb, d):
     for x in range(SIDE):
         v[pl.ds(x * PITCH, SIDE), :] = f[pl.ds(x * SIDE, SIDE), :]
     for g in range(EXT):
         v[pl.ds((SIDE + g) * PITCH, SIDE), :] = xe[pl.ds(g * SIDE, SIDE), :]
-    for i in range(3):
-        block = ez[pl.ds(i * SIDE, SIDE), :] if i < 2 else xee[...]
-        parts = [dot(block, tables[7 + k]) for k in range(2)]
-        for j in range(GROUP if i < 2 else EXT):
-            for ref, part in zip((qa, qb), parts):
-                ref[pl.ds((i * GROUP + j) * PITCH, SIDE), :] = roll(part, -EXT * (j + 1))
+    block = jnp.concatenate([ez[...], xee[...]], axis=0)
+    for ref, k in ((qa, 0), (qb, 1)):
+        spread_lanes(ref, 0, SIDE, block, tables, k)
     for ref in (v, qa, qb):
         lift_width(ref, 0, False, chunks(0)[:-1])
+        for first, count, stride in chunks(0):
+
+            def at(i):
+                return pl.ds(first * PITCH + i, count, stride=stride * PITCH)
+
+            even, behind = ref[at(0), :], None
+            for k in range(SIDE // 2 - 1):
+                ahead = ref[at(2 * k + 2), :]
+                detail = ref[at(2 * k + 1), :] - 0.5 * (even + ahead)
+                ref[at(2 * k + 1), :] = detail
+                if k > 0:
+                    ref[at(2 * k), :] = even + 0.25 * (behind + detail)
+                even, behind = ahead, detail
+    lift_lanes(0, spot[0] >= 0, v, qa, qb, d, chunks(0)[1:3])
+
+
+def spread_lanes(ref, first, rows, block, tables, k):
+    part = dot(block, tables[SPREAD, :][LANES * k : LANES * (k + 1)])
+    for x in range(PITCH):
+        group, j = x // GROUP, x % GROUP
+        cells = part[group * rows : (group + 1) * rows]
+        ref[pl.ds(x * PITCH + first, rows), :] = roll(cells, -EXT * (j + 1))
+
+
+def close_height(ref):
+    for first, count, stride in chunks(0):
+
+        def at(i):
+            return pl.ds(first * PITCH + i, count, stride=stride * PITCH)
+
+        last, end = ref[at(SIDE - 2), :], ref[at(SIDE - 1), :]
+        end = end - 0.5 * (last + ref[at(SIDE + NEAR), :])
+        ref[at(SIDE - 1), :] = end
+        ref[at(SIDE - 2), :] = last + 0.25 * (ref[at(SIDE - 3), :] + end)
+        ref[at(0), :] = ref[at(0), :] + 0.25 * (ref[at(SIDE), :] + ref[at(1), :])
 
 
 def levels_kernel(
@@ -278,6 +305,7 @@
             v[pl.ds(8 * c * PITCH + SIDE + level, 8, stride=PITCH), :] = mix(LAST[level], seam_before)
             v[pl.ds(8 * c * PITCH + SIDE + NEAR + level, 8, stride=PITCH), :] = mix(FIRST[level], seam_after)
     row8 = rows_of(EXT)
+    extras = []
     for i in range(3):
         first = NEAR * PITCH + i * EXT
         own = [yup[pl.ds(first + j, 1), :] for j in range(EXT)]
@@ -287,22 +315,30 @@
         for level in range(NEAR):
             extra = jnp.where(row8 == level, mix(LAST[level], seam_before), extra)
             extra = jnp.where(row8 == NEAR + level, mix(FIRST[level], seam_after), extra)
-        parts = [dot(extra, tables[7 + k]) for k in range(2)]
-        for j in range(GROUP if i < 2 else EXT):
-            for ref, part in zip((qa, qb), parts):
-                ref[pl.ds((i * GROUP + j) * PITCH + SIDE, EXT), :] = roll(part, -EXT * (j + 1))
+        extras.append(extra)
+    block = jnp.concatenate(extras, axis=0)
+    for ref, k in ((qa, 0), (qb, 1)):
+        spread_lanes(ref, SIDE, EXT, block, tables, k)
 
     for level in range(NEAR):
+        pieces = chunks(level)
         for ref in (v, qa, qb):
-            lift_width(ref, level, ref is v, chunks(level)[-1:] if level == 0 else chunks(level))
-            for first, count, stride in chunks(level):
+            lift_width(ref, level, ref is v, pieces[-1:] if level == 0 else pieces)
+            if level == 0:
+                close_height(ref)
+                continue
+            for first, count, stride in pieces:
                 lift_chunk(
                     ref,
                     lambda i: pl.ds(first * PITCH + i, count, stride=stride * PITCH),
                     level,
                     ref is v,
                 )
-        lift_lanes(level, go, v, qa, qb, d)
+        if level == 0:
+            pieces = pieces[:1] + pieces[3:]
+        elif level == NEAR - 1:
+            pieces = pieces[:-1]
+        lift_lanes(level, go, v, qa, qb, d, pieces)
 
     energy = [jnp.zeros((8, LANES), F32)] * NEAR
     kept = [jnp.zeros((8, LANES), F32)] * NEAR
@@ -345,66 +381,61 @@
     send[...] = jnp.broadcast_to(jnp.sum(block, axis=0, keepdims=True), send.shape)
 
 
-def last_kernel(got, spot, coef, th, out, stats, grid, *, sizes, counts):
+def last_kernel(spot, got, coef, th, out, stats, grid, *, sizes, counts):
     nx, ny, nz = sizes
     plane = ny * nz
     lane, row = lanes_of(plane), rows_of(plane)
-    turn = pl.program_id(0)
-
-    @pl.when(turn == 0)
-    def _():
-        v = [got[pl.ds(i * plane, plane), :] for i in range(nx)]
-        sums = functools.reduce(lambda a, b: a + b, v)
-        sums = jnp.sum(sums, axis=0, keepdims=True)
-
-        def down(a, shift):
-            return pltpu.roll(a, shift % plane, 0)
-
-        odd = (lane & 16) != 0
-        d = [v[i] - 0.5 * roll(v[i] + v[(i + 1) % nx], 16) for i in range(nx)]
-        v = [jnp.where(odd, d[i], v[i] + 0.25 * roll(d[i] + d[i - 1], -16)) for i in range(nx)]
-        odd = (lane & 8) != 0
-        d = [a - 0.5 * roll(a + down(a, -nz), 8) for a in v]
-        v = [jnp.where(odd, b, a + 0.25 * roll(b + down(b, nz), -8)) for a, b in zip(v, d)]
-        odd = (lane & 1) != 0
-        top, low = (lane & 7) == 7, (lane & 7) == 0
-        far = row % nz == nz - 1
-        near = row % nz == 0
-        result = []
-        for a in v:
-            following = jnp.where(far, down(a, nz - 1), down(a, -1))
-            d = a - 0.5 * (roll(a, 1) + jnp.where(top, roll(following, 7), roll(a, -1)))
-            previous = jnp.where(near, down(d, 1 - nz), down(d, 1))
-            s = a + 0.25 * (jnp.where(low, roll(previous, -7), roll(d, 1)) + roll(d, -1))
-            result.append(jnp.where(odd, d, s))
-        bound = th[pl.ds(LEVELS - 1, 1), :]
-        detail = (lane < 32) & ((lane & 25) != 0)
-        energy = kept = None
-        for i, a in enumerate(result):
-            shrunk = a - jnp.minimum(jnp.maximum(a, -bound), bound)
-            grid[pl.ds(i * plane, plane), :] = jnp.where(detail, shrunk, a)
-            square, size = jnp.where(detail, a * a, 0.0), jnp.where(detail, jnp.abs(shrunk), 0.0)
-            energy = square if energy is None else energy + square
-            kept = size if kept is None else kept + size
-        lane1 = lanes_of(1)
-        for i, (part, base) in enumerate(((energy, 32), (kept, 36))):
-            totals = jnp.where(lane1 == NEAR, jnp.sum(part), roll(sums, -base))
-            scale = jnp.zeros((1, LANES), F32)
-            for level in range(LEVELS):
-                scale = jnp.where(lane1 == level, 1.0 / counts[level], scale)
-            stats[i] = (totals * scale)[:, :LEVELS]
+    v = [got[pl.ds(i * plane, plane), :] for i in range(nx)]
+    sums = functools.reduce(lambda a, b: a + b, v)
+    sums = jnp.sum(sums, axis=0, keepdims=True)
+
+    def down(a, shift):
+        return pltpu.roll(a, shift % plane, 0)
+
+    odd = (lane & 16) != 0
+    d = [v[i] - 0.5 * roll(v[i] + v[(i + 1) % nx], 16) for i in range(nx)]
+    v = [jnp.where(odd, d[i], v[i] + 0.25 * roll(d[i] + d[i - 1], -16)) for i in range(nx)]
+    odd = (lane & 8) != 0
+    d = [a - 0.5 * roll(a + down(a, -nz), 8) for a in v]
+    v = [jnp.where(odd, b, a + 0.25 * roll(b + down(b, nz), -8)) for a, b in zip(v, d)]
+    odd = (lane & 1) != 0
+    top, low = (lane & 7) == 7, (lane & 7) == 0
+    far = row % nz == nz - 1
+    near = row % nz == 0
+    result = []
+    for a in v:
+        following = jnp.where(far, down(a, nz - 1), down(a, -1))
+        d = a - 0.5 * (roll(a, 1) + jnp.where(top, roll(following, 7), roll(a, -1)))
+        previous = jnp.where(near, down(d, 1 - nz), down(d, 1))
+        s = a + 0.25 * (jnp.where(low, roll(previous, -7), roll(d, 1)) + roll(d, -1))
+        result.append(jnp.where(odd, d, s))
+    bound = th[pl.ds(LEVELS - 1, 1), :]
+    detail = (lane < 32) & ((lane & 25) != 0)
+    energy = kept = None
+    for i, a in enumerate(result):
+        shrunk = a - jnp.minimum(jnp.maximum(a, -bound), bound)
+        grid[pl.ds(i * plane, plane), :] = jnp.where(detail, shrunk, a)
+        square, size = jnp.where(detail, a * a, 0.0), jnp.where(detail, jnp.abs(shrunk), 0.0)
+        energy = square if energy is None else energy + square
+        kept = size if kept is None else kept + size
+    lane1 = lanes_of(1)
+    for i, (part, base) in enumerate(((energy, 32), (kept, 36))):
+        totals = jnp.where(lane1 == NEAR, jnp.sum(part), roll(sums, -base))
+        scale = jnp.zeros((1, LANES), F32)
+        for level in range(LEVELS):
+            scale = jnp.where(lane1 == level, 1.0 / counts[level], scale)
+        stats[i] = (totals * scale)[:, :LEVELS]
 
     own = grid[pl.ds(spot[0], 1), :]
     row8, lane8 = rows_of(8), lanes_of(8)
-    block = jnp.where((lane8 < 32) & (lane8 // 8 == 2 * turn + row8) & (row8 < 2), own, 0.0)
+    block = jnp.where((lane8 < 32) & (lane8 // 8 == row8), own, 0.0)
     source, target = rows_of(LANES), lanes_of(LANES)
     pick = jnp.where((target == 16 * (source % 8)) & (source < 32), 1.0, 0.0).astype(F32)
     block = dot(block, pick)
-    out[...] = coef[...]
     start = (lane8[:1] % 16) == 0
-    for b in range(2):
-        at = pl.ds(16 * b, 1)
-        out[at, :] = jnp.where(start, block[b : b + 1, :], coef[at, :])
+    for i in range(4):
+        at = pl.ds((i // 2 * SIDE + i % 2) * 16, 1)
+        out[at, :] = jnp.where(start, block[i : i + 1, :], coef[at, :])
 
 
 def shape(*dims):
@@ -418,7 +449,7 @@
     counts = [7.0 * cells / 8 ** (level + 1) for level in range(LEVELS)]
     f = fields.reshape(SIDE * SIDE, LANES)
     th = jnp.broadcast_to(jnp.pad(jnp.exp2(exponents.astype(F32)), (0, 3))[:, None], (8, LANES))
-    tables = jnp.asarray(constant_tables())
+    table, tables = (jnp.asarray(t) for t in constant_tables())
     wy = jnp.asarray(W.astype(np.float32))
 
     def swap(up, down, axis):
@@ -446,15 +477,9 @@
         )(*scalars, *args)
 
     spot = lax.axis_index(("gx", "gy", "gz")).astype(jnp.int32).reshape(1)
-    whole = lambda *dims: pl.BlockSpec(dims, lambda i: (0,) * len(dims))
     pz = pl.pallas_call(
-        ends_kernel,
-        grid=(4,),
-        in_specs=[pl.BlockSpec((SIDE * SIDE // 4, LANES), lambda i: (i, 0)), whole(LANES, LANES)],
-        out_specs=here,
-        out_shape=pltpu.VMEM((2 * SIDE, LANES), F32),
-        name="ends",
-    )(f, tables[0])
+        ends_kernel, out_specs=here, out_shape=pltpu.VMEM((2 * SIDE, LANES), F32), name="ends"
+    )(f, table)
     before, after = swap(pz, pz, "gz")
     fx, fy = local(faces_kernel, "faces", (EXT * SIDE, EXT * SIDE), f)
     message = (NEAR + 1) * SIDE
@@ -468,7 +493,14 @@
     )
     before, after = swap(yup, ydown, "gy")
     block = PITCH * PITCH
-    v, qa, qb = local(prepare_kernel, "prepare", (block,) * 3, f, ez, xe, xee, tables)
+    v, qa, qb = local(
+        prepare_kernel,
+        "prepare",
+        (block,) * 3,
+        *(f, ez, xe, xee, tables),
+        scalars=(spot,),
+        scratch=(block,),
+    )
     coef, send, *_ = local(
         levels_kernel,
         "levels",
@@ -482,19 +514,14 @@
     got = lax.all_to_all(send.reshape(devices, 1, LANES), ("gx", "gy", "gz"), 0, 0).reshape(devices, LANES)
     out, stats = pl.pallas_call(
         functools.partial(last_kernel, sizes=sizes, counts=counts),
-        grid=(2,),
-        in_specs=[
-            here,
-            pl.BlockSpec(memory_space=pltpu.SMEM),
-            pl.BlockSpec((SIDE, LANES), lambda i: (16 * i, 0)),
-            here,
-        ],
-        out_specs=[pl.BlockSpec((SIDE, LANES), lambda i: (16 * i, 0)), whole(2, 1, LEVELS)],
-        out_shape=(shape(SIDE * SIDE, LANES), shape(2, 1, LEVELS)),
+        in_specs=[pl.BlockSpec(memory_space=pltpu.SMEM), here, here, here],
+        out_specs=[here, here],
+        out_shape=(pltpu.VMEM((SIDE * SIDE, LANES), F32), shape(2, 1, LEVELS)),
         scratch_shapes=[pltpu.VMEM((devices, LANES), F32)],
         input_output_aliases={2: 0},
+        compiler_params=pltpu.CompilerParams(vmem_limit_bytes=8 << 20),
         name="last",
-    )(pinned(got), spot, coef, pinned(th))
+    )(spot, pinned(got), pinned(coef), pinned(th))
     return out.reshape(fields.shape), stats
 
 

time: 56.6 us -> 53.5 us (0.945)
  Pallas kernels: 11.1 us -> 8.95 us
  waiting for transfers between devices: 8.59 us -> 7.62 us
    pallas_call x1, Pallas kernels: 3.46 us -> 1.68 us  [shards(): pl.pallas_call(ends_kernel, out_specs=here, out_shape=pltpu.VMEM((2 * SID...]
    ppermute x3, waiting for transfers between devices: 6.21 us -> 5.23 us  [swap(): before = lax.ppermute(up, axis, [(i, (i + 1) % n) for i in range(n)])]
  transfers between devices with their start and end apart: 6 -> 6, of which waited for: 4 -> 4; matrix products, arithmetic and copies ran while one was open for 0% -> 0% of each run, Pallas kernels for 2% -> 4%
where the time goes in v4:
time: 53.5 us; the launch traced here: 53.4 us
  blocking collectives  21.6 us (40%)
  starting transfers between devices  12.5 us (23%)
  Pallas kernels  8.95 us (17%)
  waiting for transfers between devices  7.62 us (14%)
  local copies, waits for them, and re-layouts  1.93 us (4%)
  between operations  0.7 us (1%)
    all_to_all x1, blocking collectives, shards(): lax.all_to_all(send.reshape(devices, 1, LANES), ('gx', 'gy', 'gz'), 0, 0)  21.6 us
    ppermute x3, starting transfers between devices, swap(): after = lax.ppermute(down, axis, [((i + 1) % n, i) for i in range(n)])  7.63 us
    pallas_call x5, Pallas kernels, local(): pl.pallas_call(kernel, in_specs=[pl.BlockSpec(memory_space=pltpu.SMEM)] *...  5.93 us
    ppermute x3, waiting for transfers between devices, swap(): before = lax.ppermute(up, axis, [(i, (i + 1) % n) for i in range(n)])  5.23 us
    ppermute x3, starting transfers between devices, swap(): before = lax.ppermute(up, axis, [(i, (i + 1) % n) for i in range(n)])  4.89 us
    ppermute x3, waiting for transfers between devices, swap(): after = lax.ppermute(down, axis, [((i + 1) % n, i) for i in range(n)])  2.39 us
    unnamed x11, local copies, waits for them, and re-layouts  1.86 us
    pallas_call x1, Pallas kernels, shards(): pl.pallas_call(ends_kernel, out_specs=here, out_shape=pltpu.VMEM((2 * SID...  1.68 us
  transfers between devices with their start and end apart: 6, of which 4 were waited for; matrix products, arithmetic and copies ran while one was open for 0% of the time, Pallas kernels for 4%

profile of v4, /device:TPU:1, one launch (start us, length us, event | category | flops | bytes accessed | tf_op | source)
XLA Modules:
  0.0 53.4 jit_solution(1568905821790609206)
XLA Ops:
  0.6 0.0 copy-start
  0.6 1.7 %ends.1.pz = f32[64,128]{1,0:T(8,128)S(1)} custom-call(f32[1024,128]{1,0:T(8,128)} %bitcast.8, f32[128,128]{1,0:T(8,128)} %constant.28.clone.table), custom_call_target="tpu_custom_call" | custom-call | tf_op jit(solution)/shard_map/ends/pallas_call | solution.py:480
  2.3 3.6 %collective-permute-start.1 = (f32[64,128]{1,0:T(8,128)S(1)}, f32[64,128]{1,0:T(8,128)S(1)}, u32[]{:S(2)}, u32[]{:S(2)}) collective-permute-start(f32[64,128]{1,0:T(8,128)S(1)} %ends.1.pz), channel_id=1, source_target_pairs={{1,0},{2,1},{3,2},{0,3},{5,4},{6,5},{7,6},{4,7},{9,8},{10,9},{11,1... | collective-permute-start | bytes 98312 | tf_op jit(solution)/shard_map/ppermute | solution.py:458
  6.0 0.0 collective-permute-start
  6.0 0.0 copy-start.1
  6.0 1.0 %copy-done.1 = f32[1,32,32,128]{3,2,1,0:T(8,128)S(1)} copy-done((f32[1,32,32,128]{3,2,1,0:T(8,128)S(1)}, f32[1,32,32,128]{3,2,1,0:T(8,128)}, u32[]{:S(2)}) %copy-start.1) | copy-done | bytes 524312
  7.0 0.4 faces.1
  7.4 0.0 collective-permute-done.1.after
  7.4 2.5 %collective-permute-done.before = f32[64,128]{1,0:T(8,128)S(1)} collective-permute-done((f32[64,128]{1,0:T(8,128)S(1)}, f32[64,128]{1,0:T(8,128)S(1)}, u32[]{:S(2)}, u32[]{:S(2)}) %collective-permute-start) | collective-permute-done | bytes 32800 | tf_op jit(solution)/shard_map/ppermute | solution.py:457
  9.9 0.0 copy-done
  9.9 0.3 depth.1
  10.3 0.0 copy-start.3
  10.3 3.2 %collective-permute-start.2 = (f32[160,128]{1,0:T(8,128)S(1)}, f32[160,128]{1,0:T(8,128)S(1)}, u32[]{:S(2)}, u32[]{:S(2)}) collective-permute-start(f32[160,128]{1,0:T(8,128)S(1)} %get-tuple-element.22.up), channel_id=1, source_target_pairs={{0,32},{32,64},{64,96},{96,128},{128,160},{160,192},{192,224},{224... | collective-permute-start | bytes 245768 | tf_op jit(solution)/shard_map/ppermute | solution.py:457
  13.5 0.0 collective-permute-start.3
  13.5 1.5 %collective-permute-done.2.before = f32[160,128]{1,0:T(8,128)S(1)} collective-permute-done((f32[160,128]{1,0:T(8,128)S(1)}, f32[160,128]{1,0:T(8,128)S(1)}, u32[]{:S(2)}, u32[]{:S(2)}) %collective-permute-start.2) | collective-permute-done | bytes 81952 | tf_op jit(solution)/shard_map/ppermute | solution.py:457
  15.0 2.4 %collective-permute-done.3.after = f32[160,128]{1,0:T(8,128)S(1)} collective-permute-done((f32[160,128]{1,0:T(8,128)S(1)}, f32[160,128]{1,0:T(8,128)S(1)}, u32[]{:S(2)}, u32[]{:S(2)}) %collective-permute-start.3) | collective-permute-done | bytes 81952 | tf_op jit(solution)/shard_map/ppermute | solution.py:458
  17.4 0.0 copy-done.3
  17.4 0.0 copy-start.2
  17.4 0.3 width.1
  17.7 0.0 copy-start.4
  17.7 1.7 %collective-permute-start.4 = (f32[184,128]{1,0:T(8,128)S(1)}, f32[184,128]{1,0:T(8,128)S(1)}, u32[]{:S(2)}, u32[]{:S(2)}) collective-permute-start(f32[184,128]{1,0:T(8,128)S(1)} %get-tuple-element.26.yup), channel_id=1, source_target_pairs={{0,4},{4,8},{8,12},{12,16},{16,20},{20,24},{24,28},{28,0},{1,5},{5... | collective-permute-start | bytes 282632 | tf_op jit(solution)/shard_map/ppermute | solution.py:457
  19.4 4.0 %collective-permute-start.5 = (f32[184,128]{1,0:T(8,128)S(1)}, f32[184,128]{1,0:T(8,128)S(1)}, u32[]{:S(2)}, u32[]{:S(2)}) collective-permute-start(f32[184,128]{1,0:T(8,128)S(1)} %get-tuple-element.27.ydown), channel_id=1, source_target_pairs={{4,0},{8,4},{12,8},{16,12},{20,16},{24,20},{28,24},{0,28},{5,1},{9... | collective-permute-start | bytes 282632 | tf_op jit(solution)/shard_map/ppermute | solution.py:458
  23.4 0.0 copy-done.4
  23.4 0.0 copy-done.2
  23.4 1.6 %prepare.1 = (f32[1600,128]{1,0:T(8,128)S(1)}, f32[1600,128]{1,0:T(8,128)S(1)}, f32[1600,128]{1,0:T(8,128)S(1)}) custom-call(s32[1]{0:T(128)} %bitcast.spot, f32[1024,128]{1,0:T(8,128)S(1)} %bitcast.10, f32[64,128]{1,0:T(8,128)S(1)} %get-tuple-element.25.ez, f32[256,128]{1,0:T(8,128)S(1)} %get-tuple-element.28.xe, f32[32,128]{1,0:T(8,128)S(1)} %get-tuple-element.29.xee, ...), custom_call_target="tpu_custom_call" | custom-call | tf_op jit(solution)/shard_map/prepare/pallas_call | solution.py:468
  25.0 1.2 %collective-permute-done.4.before = f32[184,128]{1,0:T(8,128)S(1)} collective-permute-done((f32[184,128]{1,0:T(8,128)S(1)}, f32[184,128]{1,0:T(8,128)S(1)}, u32[]{:S(2)}, u32[]{:S(2)}) %collective-permute-start.4) | collective-permute-done | bytes 94240 | tf_op jit(solution)/shard_map/ppermute | solution.py:457
  26.3 0.0 collective-permute-done.5.after
  26.3 0.1 broadcast_in_dim.2.th
  26.3 3.2 %levels.1 = (f32[1024,128]{1,0:T(8,128)S(1)}, f32[256,128]{1,0:T(8,128)S(1)}, f32[1600,128]{1,0:T(8,128)S(1)}, f32[1600,128]{1,0:T(8,128)S(1)}, f32[1600,128]{1,0:T(8,128)S(1)}) custom-call(s32[1]{0:T(128)} %bitcast.spot, f32[184,128]{1,0:T(8,128)S(1)} %get-tuple-element.26.yup, ...), custom_call_target="tpu_custom_call", output_to_operand_aliasing={{2}: (7, {}), {3}: (8, {}), {4}: (9, {})} | custom-call | tf_op jit(solution)/shard_map/levels/pallas_call | solution.py:468
  29.6 21.6 %all_to_all.5 = f32[256,1,128]{2,1,0:T(1,128)S(1)} all-to-all(f32[256,1,128]{2,1,0:T(1,128)S(1)} %bitcast.12), channel_id=1, replica_groups=mesh['gx'=8,'gy'=8,'gz'=4] {'gx','gy','gz'}, dimensions={0} | all-to-all | bytes 262144 | tf_op jit(solution)/shard_map/all_to_all | solution.py:514
  51.2 1.3 %last.1 = (f32[1024,128]{1,0:T(8,128)S(1)}, f32[2,1,5]{2,1,0:T(1,128)}) custom-call(s32[1]{0:T(128)} %bitcast.spot, f32[256,128]{1,0:T(8,128)S(1)} %bitcast.11, f32[1024,128]{1,0:T(8,128)S(1)} %get-tuple-element.36.coef, f32[8,128]{1,0:T(8,128)S(1)} %broadcast_in_dim.2.th), custom_call_target="tpu_custom_call", output_to_operand_aliasing={{0}: (2, {})} | custom-call | tf_op jit(solution)/shard_map/last/pallas_call | solution.py:515
  52.6 0.8 %copy.16 = f32[1,32,32,128]{3,2,1,0:T(8,128)} copy(f32[1,32,32,128]{3,2,1,0:T(8,128)S(1)} %bitcast.7) | data formatting | bytes 1048576
  (2 shorter events, 0.0 us)
Async XLA Ops:
  0.6 9.3 %copy-start = (f32[1280,128]{1,0:T(8,128)S(1)}, f32[1280,128]{1,0:T(8,128)}, u32[]{:S(2)}) copy-start(f32[1280,128]{1,0:T(8,128)} %constant.29.clone.tables) | copy-start | bytes 1966084
  2.3 5.1 %collective-permute-start.1 = (f32[64,128]{1,0:T(8,128)S(1)}, f32[64,128]{1,0:T(8,128)S(1)}, u32[]{:S(2)}, u32[]{:S(2)}) collective-permute-start(f32[64,128]{1,0:T(8,128)S(1)} %ends.1.pz), channel_id=1, source_target_pairs={{1,0},{2,1},{3,2},{0,3},{5,4},{6,5},{7,6},{4,7},{9,8},{10,9},{11,1... | collective-permute-start | bytes 98312 | tf_op jit(solution)/shard_map/ppermute | solution.py:458
  6.0 4.0 %collective-permute-start = (f32[64,128]{1,0:T(8,128)S(1)}, f32[64,128]{1,0:T(8,128)S(1)}, u32[]{:S(2)}, u32[]{:S(2)}) collective-permute-start(f32[64,128]{1,0:T(8,128)S(1)} %ends.1.pz), channel_id=1, source_target_pairs={{0,1},{1,2},{2,3},{3,0},{4,5},{5,6},{6,7},{7,4},{8,9},{9,10},{10,1... | collective-permute-start | bytes 98312 | tf_op jit(solution)/shard_map/ppermute | solution.py:457
  6.0 1.0 %copy-start.1 = (f32[1,32,32,128]{3,2,1,0:T(8,128)S(1)}, f32[1,32,32,128]{3,2,1,0:T(8,128)}, u32[]{:S(2)}) copy-start(f32[1,32,32,128]{3,2,1,0:T(8,128)} %param.5) | copy-start | bytes 1572868
  10.3 7.1 %copy-start.3 = (f32[8,32]{1,0:T(8,128)S(1)}, f32[8,32]{1,0:T(8,128)}, u32[]{:S(2)}) copy-start(f32[8,32]{1,0:T(8,128)} %constant.30.clone.wy) | copy-start | bytes 3076
  10.3 4.7 %collective-permute-start.2 = (f32[160,128]{1,0:T(8,128)S(1)}, f32[160,128]{1,0:T(8,128)S(1)}, u32[]{:S(2)}, u32[]{:S(2)}) collective-permute-start(f32[160,128]{1,0:T(8,128)S(1)} %get-tuple-element.22.up), channel_id=1, source_target_pairs={{0,32},{32,64},{64,96},{96,128},{128,160},{160,192},{192,224},{224... | collective-permute-start | bytes 245768 | tf_op jit(solution)/shard_map/ppermute | solution.py:457
  13.5 3.9 %collective-permute-start.3 = (f32[160,128]{1,0:T(8,128)S(1)}, f32[160,128]{1,0:T(8,128)S(1)}, u32[]{:S(2)}, u32[]{:S(2)}) collective-permute-start(f32[160,128]{1,0:T(8,128)S(1)} %get-tuple-element.23.down), channel_id=1, source_target_pairs={{32,0},{64,32},{96,64},{128,96},{160,128},{192,160},{224,192},{0,2... | collective-permute-start | bytes 245768 | tf_op jit(solution)/shard_map/ppermute | solution.py:458
  17.4 6.0 %copy-start.2 = (f32[1,32,32,128]{3,2,1,0:T(8,128)S(1)}, f32[1,32,32,128]{3,2,1,0:T(8,128)}, u32[]{:S(2)}) copy-start(f32[1,32,32,128]{3,2,1,0:T(8,128)} %param.5) | copy-start | bytes 1572868
  17.7 5.7 %copy-start.4 = (s32[5]{0:T(128)S(1)}, s32[5]{0:T(128)}, u32[]{:S(2)}) copy-start(s32[5]{0:T(128)} %param.6) | copy-start | bytes 64
  17.7 8.6 %collective-permute-start.4 = (f32[184,128]{1,0:T(8,128)S(1)}, f32[184,128]{1,0:T(8,128)S(1)}, u32[]{:S(2)}, u32[]{:S(2)}) collective-permute-start(f32[184,128]{1,0:T(8,128)S(1)} %get-tuple-element.26.yup), channel_id=1, source_target_pairs={{0,4},{4,8},{8,12},{12,16},{16,20},{20,24},{24,28},{28,0},{1,5},{5... | collective-permute-start | bytes 282632 | tf_op jit(solution)/shard_map/ppermute | solution.py:457
  19.4 6.9 %collective-permute-start.5 = (f32[184,128]{1,0:T(8,128)S(1)}, f32[184,128]{1,0:T(8,128)S(1)}, u32[]{:S(2)}, u32[]{:S(2)}) collective-permute-start(f32[184,128]{1,0:T(8,128)S(1)} %get-tuple-element.27.ydown), channel_id=1, source_target_pairs={{4,0},{8,4},{12,8},{16,12},{20,16},{24,20},{28,24},{0,28},{5,1},{9... | collective-permute-start | bytes 282632 | tf_op jit(solution)/shard_map/ppermute | solution.py:458

commit v5 on v4

--- a/solution.py
+++ b/solution.py
@@ -212,7 +212,7 @@
     return own + ([(SIDE, EXT, 1)] if level < NEAR else [])
 
 
-def lift_lanes(level, go, v, qa, qb, d, pieces):
+def lift_lanes(level, spot, v, qa, qb, d, pieces):
     step = 1 << level
     rows = [
         (pl.ds(x * PITCH + first, count, stride=stride), count)
@@ -220,7 +220,7 @@
         for first, count, stride in pieces
     ]
 
-    @pl.when(go)
+    @pl.when(spot[0] > -1)
     def _():
         for at, count in rows:
             cells = v[at, :]
@@ -228,7 +228,7 @@
             ahead = roll(jnp.where(lanes_of(count) == LANES - step, qb[at, :], odd), -step)
             d[at, :] = odd - 0.5 * (cells + ahead)
 
-    @pl.when(go)
+    @pl.when(spot[0] > -2)
     def _():
         for at, count in rows:
             lane = lanes_of(count)
@@ -268,7 +268,7 @@
                 if k > 0:
                     ref[at(2 * k), :] = even + 0.25 * (behind + detail)
                 even, behind = ahead, detail
-    lift_lanes(0, spot[0] >= 0, v, qa, qb, d, chunks(0)[1:3])
+    lift_lanes(0, spot, v, qa, qb, d, chunks(0)[1:3])
 
 
 def spread_lanes(ref, first, rows, block, tables, k):
@@ -296,7 +296,6 @@
     spot, yup, ydown, before, after, th, tables, v_in, qa_in, qb_in, coef, send, v, qa, qb, d
 ):
     del v_in, qa_in, qb_in
-    go = spot[0] >= 0
     for c in range(PITCH // 8):
         rows = [pl.ds(g * PITCH + 8 * c, 8) for g in range(NEAR)]
         seam_before = [before[r, :] for r in rows] + [ydown[r, :] for r in rows]
@@ -338,7 +337,7 @@
             pieces = pieces[:1] + pieces[3:]
         elif level == NEAR - 1:
             pieces = pieces[:-1]
-        lift_lanes(level, go, v, qa, qb, d, pieces)
+        lift_lanes(level, spot, v, qa, qb, d, pieces)
 
     energy = [jnp.zeros((8, LANES), F32)] * NEAR
     kept = [jnp.zeros((8, LANES), F32)] * NEAR
@@ -381,7 +380,14 @@
     send[...] = jnp.broadcast_to(jnp.sum(block, axis=0, keepdims=True), send.shape)
 
 
-def last_kernel(spot, got, coef, th, out, stats, grid, *, sizes, counts):
+def last_kernel(spot, got, coef, th, out, stats, grid, planes, sums_out, sem, *, sizes, counts):
+    half = SIDE // 2
+    copies = []
+    for a in range(2):
+        at = pl.ds((a * half + 1) * SIDE, (half - 1) * SIDE)
+        copies.append(pltpu.make_async_copy(coef.at[at], out.at[at], sem.at[a]))
+        copies[a].start()
+        planes[pl.ds(a * SIDE, SIDE), :] = coef[pl.ds(a * half * SIDE, SIDE), :]
     nx, ny, nz = sizes
     plane = ny * nz
     lane, row = lanes_of(plane), rows_of(plane)
@@ -424,7 +430,7 @@
         scale = jnp.zeros((1, LANES), F32)
         for level in range(LEVELS):
             scale = jnp.where(lane1 == level, 1.0 / counts[level], scale)
-        stats[i] = (totals * scale)[:, :LEVELS]
+        sums_out[i] = (totals * scale)[:, :LEVELS]
 
     own = grid[pl.ds(spot[0], 1), :]
     row8, lane8 = rows_of(8), lanes_of(8)
@@ -432,10 +438,18 @@
     source, target = rows_of(LANES), lanes_of(LANES)
     pick = jnp.where((target == 16 * (source % 8)) & (source < 32), 1.0, 0.0).astype(F32)
     block = dot(block, pick)
-    start = (lane8[:1] % 16) == 0
+    start = lane8[:1] % 16 == 0
     for i in range(4):
-        at = pl.ds((i // 2 * SIDE + i % 2) * 16, 1)
-        out[at, :] = jnp.where(start, block[i : i + 1, :], coef[at, :])
+        at = pl.ds(i * half, 1)
+        planes[at, :] = jnp.where(start, block[i : i + 1, :], planes[at, :])
+    for a in range(2):
+        target = out.at[pl.ds(a * half * SIDE, SIDE)]
+        copies.append(pltpu.make_async_copy(planes.at[pl.ds(a * SIDE, SIDE)], target, sem.at[2 + a]))
+    copies.append(pltpu.make_async_copy(sums_out, stats, sem.at[4]))
+    for copy in copies[2:]:
+        copy.start()
+    for copy in copies:
+        copy.wait()
 
 
 def shape(*dims):
@@ -512,13 +526,18 @@
     )
     send, spot, th = lax.optimization_barrier((send, spot, th))
     got = lax.all_to_all(send.reshape(devices, 1, LANES), ("gx", "gy", "gz"), 0, 0).reshape(devices, LANES)
+    there = pl.BlockSpec(memory_space=pltpu.HBM)
     out, stats = pl.pallas_call(
         functools.partial(last_kernel, sizes=sizes, counts=counts),
         in_specs=[pl.BlockSpec(memory_space=pltpu.SMEM), here, here, here],
-        out_specs=[here, here],
-        out_shape=(pltpu.VMEM((SIDE * SIDE, LANES), F32), shape(2, 1, LEVELS)),
-        scratch_shapes=[pltpu.VMEM((devices, LANES), F32)],
-        input_output_aliases={2: 0},
+        out_specs=[there, there],
+        out_shape=(shape(SIDE * SIDE, LANES), shape(2, 1, LEVELS)),
+        scratch_shapes=[
+            pltpu.VMEM((devices, LANES), F32),
+            pltpu.VMEM((2 * SIDE, LANES), F32),
+            pltpu.VMEM((2, 1, LEVELS), F32),
+            pltpu.SemaphoreType.DMA((5,)),
+        ],
         compiler_params=pltpu.CompilerParams(vmem_limit_bytes=8 << 20),
         name="last",
     )(spot, pinned(got), pinned(coef), pinned(th))

time: 53.5 us -> 53.2 us (level)
  local copies, waits for them, and re-layouts: 1.93 us -> 1.14 us
  Pallas kernels: 8.95 us -> 9.58 us
    unnamed x11 -> x10, local copies, waits for them, and re-layouts: 1.86 us -> 1.06 us
where the time goes in v5:
time: 53.2 us; the launch traced here: 53 us
  blocking collectives  21.6 us (41%)
  starting transfers between devices  12.5 us (23%)
  Pallas kernels  9.58 us (18%)
  waiting for transfers between devices  7.45 us (14%)
  local copies, waits for them, and re-layouts  1.14 us (2%)
  between operations  0.7 us (1%)
    all_to_all x1, blocking collectives, shards(): lax.all_to_all(send.reshape(devices, 1, LANES), ('gx', 'gy', 'gz'), 0, 0)  21.6 us
    ppermute x3, starting transfers between devices, swap(): after = lax.ppermute(down, axis, [((i + 1) % n, i) for i in range(n)])  7.63 us
    pallas_call x5, Pallas kernels, local(): pl.pallas_call(kernel, in_specs=[pl.BlockSpec(memory_space=pltpu.SMEM)] *...  6.44 us
    ppermute x3, waiting for transfers between devices, swap(): before = lax.ppermute(up, axis, [(i, (i + 1) % n) for i in range(n)])  5.06 us
    ppermute x3, starting transfers between devices, swap(): before = lax.ppermute(up, axis, [(i, (i + 1) % n) for i in range(n)])  4.89 us
    ppermute x3, waiting for transfers between devices, swap(): after = lax.ppermute(down, axis, [((i + 1) % n, i) for i in range(n)])  2.39 us
    pallas_call x1, Pallas kernels, shards(): pl.pallas_call(ends_kernel, out_specs=here, out_shape=pltpu.VMEM((2 * SID...  1.68 us
    pallas_call x1, Pallas kernels, shards(): pl.pallas_call(functools.partial(last_kernel, sizes=sizes, counts=counts)...  1.46 us
  transfers between devices with their start and end apart: 6, of which 4 were waited for; matrix products, arithmetic and copies ran while one was open for 0% of the time, Pallas kernels for 4%

profile of v5, /device:TPU:1, one launch (start us, length us, event | category | flops | bytes accessed | tf_op | source)
XLA Modules:
  0.0 53.0 jit_solution(10692893921770282780)
XLA Ops:
  0.6 0.0 copy-start
  0.6 1.7 %ends.1.pz = f32[64,128]{1,0:T(8,128)S(1)} custom-call(f32[1024,128]{1,0:T(8,128)} %bitcast.7, f32[128,128]{1,0:T(8,128)} %constant.28.clone.table), custom_call_target="tpu_custom_call" | custom-call | tf_op jit(solution)/shard_map/ends/pallas_call | solution.py:494
  2.3 3.6 %collective-permute-start.1 = (f32[64,128]{1,0:T(8,128)S(1)}, f32[64,128]{1,0:T(8,128)S(1)}, u32[]{:S(2)}, u32[]{:S(2)}) collective-permute-start(f32[64,128]{1,0:T(8,128)S(1)} %ends.1.pz), channel_id=1, source_target_pairs={{1,0},{2,1},{3,2},{0,3},{5,4},{6,5},{7,6},{4,7},{9,8},{10,9},{11,1... | collective-permute-start | bytes 98312 | tf_op jit(solution)/shard_map/ppermute | solution.py:472
  6.0 0.0 collective-permute-start
  6.0 0.0 copy-start.1
  6.0 1.0 %copy-done.1 = f32[1,32,32,128]{3,2,1,0:T(8,128)S(1)} copy-done((f32[1,32,32,128]{3,2,1,0:T(8,128)S(1)}, f32[1,32,32,128]{3,2,1,0:T(8,128)}, u32[]{:S(2)}) %copy-start.1) | copy-done | bytes 524312
  7.0 0.4 faces.1
  7.4 0.0 collective-permute-done.1.after
  7.4 2.5 %collective-permute-done.before = f32[64,128]{1,0:T(8,128)S(1)} collective-permute-done((f32[64,128]{1,0:T(8,128)S(1)}, f32[64,128]{1,0:T(8,128)S(1)}, u32[]{:S(2)}, u32[]{:S(2)}) %collective-permute-start) | collective-permute-done | bytes 32800 | tf_op jit(solution)/shard_map/ppermute | solution.py:471
  9.9 0.0 copy-done
  9.9 0.3 depth.1
  10.3 0.0 copy-start.3
  10.3 3.2 %collective-permute-start.2 = (f32[160,128]{1,0:T(8,128)S(1)}, f32[160,128]{1,0:T(8,128)S(1)}, u32[]{:S(2)}, u32[]{:S(2)}) collective-permute-start(f32[160,128]{1,0:T(8,128)S(1)} %get-tuple-element.22.up), channel_id=1, source_target_pairs={{0,32},{32,64},{64,96},{96,128},{128,160},{160,192},{192,224},{224... | collective-permute-start | bytes 245768 | tf_op jit(solution)/shard_map/ppermute | solution.py:471
  13.5 0.0 collective-permute-start.3
  13.5 1.5 %collective-permute-done.2.before = f32[160,128]{1,0:T(8,128)S(1)} collective-permute-done((f32[160,128]{1,0:T(8,128)S(1)}, f32[160,128]{1,0:T(8,128)S(1)}, u32[]{:S(2)}, u32[]{:S(2)}) %collective-permute-start.2) | collective-permute-done | bytes 81952 | tf_op jit(solution)/shard_map/ppermute | solution.py:471
  15.0 2.4 %collective-permute-done.3.after = f32[160,128]{1,0:T(8,128)S(1)} collective-permute-done((f32[160,128]{1,0:T(8,128)S(1)}, f32[160,128]{1,0:T(8,128)S(1)}, u32[]{:S(2)}, u32[]{:S(2)}) %collective-permute-start.3) | collective-permute-done | bytes 81952 | tf_op jit(solution)/shard_map/ppermute | solution.py:472
  17.4 0.0 copy-done.3
  17.4 0.0 copy-start.2
  17.4 0.3 width.1
  17.7 0.0 copy-start.4
  17.7 1.7 %collective-permute-start.4 = (f32[184,128]{1,0:T(8,128)S(1)}, f32[184,128]{1,0:T(8,128)S(1)}, u32[]{:S(2)}, u32[]{:S(2)}) collective-permute-start(f32[184,128]{1,0:T(8,128)S(1)} %get-tuple-element.26.yup), channel_id=1, source_target_pairs={{0,4},{4,8},{8,12},{12,16},{16,20},{20,24},{24,28},{28,0},{1,5},{5... | collective-permute-start | bytes 282632 | tf_op jit(solution)/shard_map/ppermute | solution.py:471
  19.4 4.0 %collective-permute-start.5 = (f32[184,128]{1,0:T(8,128)S(1)}, f32[184,128]{1,0:T(8,128)S(1)}, u32[]{:S(2)}, u32[]{:S(2)}) collective-permute-start(f32[184,128]{1,0:T(8,128)S(1)} %get-tuple-element.27.ydown), channel_id=1, source_target_pairs={{4,0},{8,4},{12,8},{16,12},{20,16},{24,20},{28,24},{0,28},{5,1},{9... | collective-permute-start | bytes 282632 | tf_op jit(solution)/shard_map/ppermute | solution.py:472
  23.4 0.0 copy-done.4
  23.4 0.0 copy-done.2
  23.4 1.8 %prepare.1 = (f32[1600,128]{1,0:T(8,128)S(1)}, f32[1600,128]{1,0:T(8,128)S(1)}, f32[1600,128]{1,0:T(8,128)S(1)}) custom-call(s32[1]{0:T(128)} %bitcast.spot, f32[1024,128]{1,0:T(8,128)S(1)} %bitcast.9, f32[64,128]{1,0:T(8,128)S(1)} %get-tuple-element.25.ez, f32[256,128]{1,0:T(8,128)S(1)} %get-tuple-element.28.xe, f32[32,128]{1,0:T(8,128)S(1)} %get-tuple-element.29.xee, ...), custom_call_target="tpu_custom_call" | custom-call | tf_op jit(solution)/shard_map/prepare/pallas_call | solution.py:482
  25.2 1.1 %collective-permute-done.4.before = f32[184,128]{1,0:T(8,128)S(1)} collective-permute-done((f32[184,128]{1,0:T(8,128)S(1)}, f32[184,128]{1,0:T(8,128)S(1)}, u32[]{:S(2)}, u32[]{:S(2)}) %collective-permute-start.4) | collective-permute-done | bytes 94240 | tf_op jit(solution)/shard_map/ppermute | solution.py:471
  26.3 0.0 collective-permute-done.5.after
  26.3 0.1 broadcast_in_dim.2.th
  26.3 3.6 %levels.1 = (f32[1024,128]{1,0:T(8,128)S(1)}, f32[256,128]{1,0:T(8,128)S(1)}, f32[1600,128]{1,0:T(8,128)S(1)}, f32[1600,128]{1,0:T(8,128)S(1)}, f32[1600,128]{1,0:T(8,128)S(1)}) custom-call(s32[1]{0:T(128)} %bitcast.spot, f32[184,128]{1,0:T(8,128)S(1)} %get-tuple-element.26.yup, ...), custom_call_target="tpu_custom_call", output_to_operand_aliasing={{2}: (7, {}), {3}: (8, {}), {4}: (9, {})} | custom-call | tf_op jit(solution)/shard_map/levels/pallas_call | solution.py:482
  29.9 21.6 %all_to_all.5 = f32[256,1,128]{2,1,0:T(1,128)S(1)} all-to-all(f32[256,1,128]{2,1,0:T(1,128)S(1)} %bitcast.11), channel_id=1, replica_groups=mesh['gx'=8,'gy'=8,'gz'=4] {'gx','gy','gz'}, dimensions={0} | all-to-all | bytes 262144 | tf_op jit(solution)/shard_map/all_to_all | solution.py:528
  51.6 1.5 %last.1 = (f32[1024,128]{1,0:T(8,128)}, f32[2,1,5]{2,1,0:T(1,128)}) custom-call(s32[1]{0:T(128)} %bitcast.spot, f32[256,128]{1,0:T(8,128)S(1)} %bitcast.10, f32[1024,128]{1,0:T(8,128)S(1)} %get-tuple-element.36.coef, f32[8,128]{1,0:T(8,128)S(1)} %broadcast_in_dim.2.th), custom_call_target="tpu_custom_call" | custom-call | tf_op jit(solution)/shard_map/last/pallas_call | solution.py:530
  (2 shorter events, 0.0 us)
Async XLA Ops:
  0.6 9.3 %copy-start = (f32[1280,128]{1,0:T(8,128)S(1)}, f32[1280,128]{1,0:T(8,128)}, u32[]{:S(2)}) copy-start(f32[1280,128]{1,0:T(8,128)} %constant.29.clone.tables) | copy-start | bytes 1966084
  2.3 5.1 %collective-permute-start.1 = (f32[64,128]{1,0:T(8,128)S(1)}, f32[64,128]{1,0:T(8,128)S(1)}, u32[]{:S(2)}, u32[]{:S(2)}) collective-permute-start(f32[64,128]{1,0:T(8,128)S(1)} %ends.1.pz), channel_id=1, source_target_pairs={{1,0},{2,1},{3,2},{0,3},{5,4},{6,5},{7,6},{4,7},{9,8},{10,9},{11,1... | collective-permute-start | bytes 98312 | tf_op jit(solution)/shard_map/ppermute | solution.py:472
  6.0 4.0 %collective-permute-start = (f32[64,128]{1,0:T(8,128)S(1)}, f32[64,128]{1,0:T(8,128)S(1)}, u32[]{:S(2)}, u32[]{:S(2)}) collective-permute-start(f32[64,128]{1,0:T(8,128)S(1)} %ends.1.pz), channel_id=1, source_target_pairs={{0,1},{1,2},{2,3},{3,0},{4,5},{5,6},{6,7},{7,4},{8,9},{9,10},{10,1... | collective-permute-start | bytes 98312 | tf_op jit(solution)/shard_map/ppermute | solution.py:471
  6.0 1.0 %copy-start.1 = (f32[1,32,32,128]{3,2,1,0:T(8,128)S(1)}, f32[1,32,32,128]{3,2,1,0:T(8,128)}, u32[]{:S(2)}) copy-start(f32[1,32,32,128]{3,2,1,0:T(8,128)} %param.5) | copy-start | bytes 1572868
  10.3 7.1 %copy-start.3 = (f32[8,32]{1,0:T(8,128)S(1)}, f32[8,32]{1,0:T(8,128)}, u32[]{:S(2)}) copy-start(f32[8,32]{1,0:T(8,128)} %constant.30.clone.wy) | copy-start | bytes 3076
  10.3 4.7 %collective-permute-start.2 = (f32[160,128]{1,0:T(8,128)S(1)}, f32[160,128]{1,0:T(8,128)S(1)}, u32[]{:S(2)}, u32[]{:S(2)}) collective-permute-start(f32[160,128]{1,0:T(8,128)S(1)} %get-tuple-element.22.up), channel_id=1, source_target_pairs={{0,32},{32,64},{64,96},{96,128},{128,160},{160,192},{192,224},{224... | collective-permute-start | bytes 245768 | tf_op jit(solution)/shard_map/ppermute | solution.py:471
  13.5 3.9 %collective-permute-start.3 = (f32[160,128]{1,0:T(8,128)S(1)}, f32[160,128]{1,0:T(8,128)S(1)}, u32[]{:S(2)}, u32[]{:S(2)}) collective-permute-start(f32[160,128]{1,0:T(8,128)S(1)} %get-tuple-element.23.down), channel_id=1, source_target_pairs={{32,0},{64,32},{96,64},{128,96},{160,128},{192,160},{224,192},{0,2... | collective-permute-start | bytes 245768 | tf_op jit(solution)/shard_map/ppermute | solution.py:472
  17.4 6.0 %copy-start.2 = (f32[1,32,32,128]{3,2,1,0:T(8,128)S(1)}, f32[1,32,32,128]{3,2,1,0:T(8,128)}, u32[]{:S(2)}) copy-start(f32[1,32,32,128]{3,2,1,0:T(8,128)} %param.5) | copy-start | bytes 1572868
  17.7 5.7 %copy-start.4 = (s32[5]{0:T(128)S(1)}, s32[5]{0:T(128)}, u32[]{:S(2)}) copy-start(s32[5]{0:T(128)} %param.6) | copy-start | bytes 64
  17.7 8.6 %collective-permute-start.4 = (f32[184,128]{1,0:T(8,128)S(1)}, f32[184,128]{1,0:T(8,128)S(1)}, u32[]{:S(2)}, u32[]{:S(2)}) collective-permute-start(f32[184,128]{1,0:T(8,128)S(1)} %get-tuple-element.26.yup), channel_id=1, source_target_pairs={{0,4},{4,8},{8,12},{12,16},{16,20},{20,24},{24,28},{28,0},{1,5},{5... | collective-permute-start | bytes 282632 | tf_op jit(solution)/shard_map/ppermute | solution.py:471
  19.4 6.9 %collective-permute-start.5 = (f32[184,128]{1,0:T(8,128)S(1)}, f32[184,128]{1,0:T(8,128)S(1)}, u32[]{:S(2)}, u32[]{:S(2)}) collective-permute-start(f32[184,128]{1,0:T(8,128)S(1)} %get-tuple-element.27.ydown), channel_id=1, source_target_pairs={{4,0},{8,4},{12,8},{16,12},{20,16},{24,20},{28,24},{0,28},{5,1},{9... | collective-permute-start | bytes 282632 | tf_op jit(solution)/shard_map/ppermute | solution.py:472

commit v6 on v5

--- a/solution.py
+++ b/solution.py
@@ -82,11 +82,12 @@
         end = np.zeros((LANES, LANES))
         end[:, : EXT * EXT] = np.kron(W[:, half * GROUP : (half + 1) * GROUP].T, np.eye(EXT))
         ends += [side @ end for side in solve]
-    tables = np.concatenate(solve + ends + list(corner) + [np.kron(each, part) for part in spread])
-    return np.tile(WZ.T, (1, GROUP)).astype(np.float32), tables.astype(np.float32)
-
-
-SOLVE, ENDS, CORNER, SPREAD = (pl.ds(LANES * i, LANES * n) for i, n in ((0, 2), (2, 4), (6, 2), (8, 2)))
+    tables = np.concatenate(solve + ends + list(corner))
+    spread = np.concatenate([np.kron(each, part) for part in spread], axis=1)
+    return [t.astype(np.float32) for t in (np.tile(WZ.T, (1, GROUP)), tables, spread)]
+
+
+SOLVE, ENDS, CORNER = (pl.ds(LANES * i, LANES * n) for i, n in ((0, 2), (2, 4), (6, 2)))
 
 
 def dot(a, b):
@@ -125,8 +126,11 @@
     return total
 
 
-def ends_kernel(f, table, pz):
-    out = dot(f[...], table[...])
+def ends_kernel(f, table, pz, block, sem):
+    copy = pltpu.make_async_copy(f, block, sem)
+    copy.start()
+    copy.wait()
+    out = dot(block[...], table[...])
     group = lanes_of(SIDE) // EXT
     for half in range(2):
         packed = jnp.zeros((SIDE, LANES), F32)
@@ -212,32 +216,32 @@
     return own + ([(SIDE, EXT, 1)] if level < NEAR else [])
 
 
-def lift_lanes(level, spot, v, qa, qb, d, pieces):
+def lift_lanes(level, rows, v, qa, qb, keep=None):
     step = 1 << level
-    rows = [
+    lane = [lanes_of(count) for _, count in rows]
+    last = [x == LANES - step for x in lane]
+    cells = [v[at, :] for at, _ in rows]
+    odd = [roll(c, -step) for c in cells]
+    ahead = [roll(jnp.where(l, qb[at, :], o), -step) for (at, _), l, o in zip(rows, last, odd)]
+    mid = [o - 0.5 * (c + a) for o, c, a in zip(odd, cells, ahead)]
+    odd = [roll(m, step) for m in mid]
+    behind = [roll(jnp.where(l, qa[at, :], o), step) for (at, _), l, o in zip(rows, last, odd)]
+    for i, (at, _) in enumerate(rows):
+        place = lane[i] & (2 * step - 1)
+        smooth = cells[i] + 0.25 * (mid[i] + behind[i])
+        lifted = jnp.where(place == 0, smooth, jnp.where(place == step, odd[i], cells[i]))
+        mask = keep(i) if keep else None
+        v[at, :] = lifted if mask is None else jnp.where(mask, cells[i], lifted)
+
+
+def lane_rows(level, pieces):
+    step = 1 << level
+    planes = list(range(0, SIDE, step)) + (list(range(SIDE, PITCH)) if level < NEAR - 1 else [])
+    return [
         (pl.ds(x * PITCH + first, count, stride=stride), count)
-        for x in list(range(0, SIDE, step)) + (list(range(SIDE, PITCH)) if level < NEAR - 1 else [])
+        for x in planes
         for first, count, stride in pieces
     ]
-
-    @pl.when(spot[0] > -1)
-    def _():
-        for at, count in rows:
-            cells = v[at, :]
-            odd = roll(cells, -step)
-            ahead = roll(jnp.where(lanes_of(count) == LANES - step, qb[at, :], odd), -step)
-            d[at, :] = odd - 0.5 * (cells + ahead)
-
-    @pl.when(spot[0] > -2)
-    def _():
-        for at, count in rows:
-            lane = lanes_of(count)
-            cells, mid = v[at, :], d[at, :]
-            odd = roll(mid, step)
-            behind = roll(jnp.where(lane == LANES - step, qa[at, :], odd), step)
-            even = cells + 0.25 * (mid + behind)
-            place = lane & (2 * step - 1)
-            v[at, :] = jnp.where(place == 0, even, jnp.where(place == step, odd, cells))
 
 
 def lift_width(ref, level, masked, pieces):
@@ -245,14 +249,13 @@
         lift_chunk(ref, lambda i: pl.ds(i * PITCH + first, count, stride=stride), level, masked)
 
 
-def prepare_kernel(spot, f, ez, xe, xee, tables, v, qa, qb, d):
+def prepare_kernel(f, ez, xe, xee, spread, v, qa, qb):
     for x in range(SIDE):
         v[pl.ds(x * PITCH, SIDE), :] = f[pl.ds(x * SIDE, SIDE), :]
     for g in range(EXT):
         v[pl.ds((SIDE + g) * PITCH, SIDE), :] = xe[pl.ds(g * SIDE, SIDE), :]
     block = jnp.concatenate([ez[...], xee[...]], axis=0)
-    for ref, k in ((qa, 0), (qb, 1)):
-        spread_lanes(ref, 0, SIDE, block, tables, k)
+    spread_lanes(qa, qb, 0, SIDE, block, spread)
     for ref in (v, qa, qb):
         lift_width(ref, 0, False, chunks(0)[:-1])
         for first, count, stride in chunks(0):
@@ -268,15 +271,26 @@
                 if k > 0:
                     ref[at(2 * k), :] = even + 0.25 * (behind + detail)
                 even, behind = ahead, detail
-    lift_lanes(0, spot, v, qa, qb, d, chunks(0)[1:3])
-
-
-def spread_lanes(ref, first, rows, block, tables, k):
-    part = dot(block, tables[SPREAD, :][LANES * k : LANES * (k + 1)])
+    row8 = rows_of(8)
+    waits = [row8 <= 1, None, None, row8 >= 5]
+    lift_lanes(0, lane_rows(0, chunks(0)[:-1]), v, qa, qb, lambda i: waits[i % 4])
+
+
+def spread_lanes(qa, qb, first, rows, block, spread):
+    both = dot(block, spread[...])
     for x in range(PITCH):
         group, j = x // GROUP, x % GROUP
-        cells = part[group * rows : (group + 1) * rows]
-        ref[pl.ds(x * PITCH + first, rows), :] = roll(cells, -EXT * (j + 1))
+        for ref, part in ((qa, both[:, :LANES]), (qb, both[:, LANES:])):
+            cells = part[group * rows : (group + 1) * rows]
+            ref[pl.ds(x * PITCH + first, rows), :] = roll(cells, -EXT * (j + 1))
+
+
+def stretch(v):
+    lane = lanes_of(v.shape[0])
+    for k in (2, 1, 0):
+        spots = [16 * c - 15 * (c % (1 << k)) for c in range(8) if c >> k & 1]
+        v = jnp.where(functools.reduce(jnp.logical_or, [lane == p for p in spots]), roll(v, 15 << k), v)
+    return v
 
 
 def close_height(ref):
@@ -293,7 +307,7 @@
 
 
 def levels_kernel(
-    spot, yup, ydown, before, after, th, tables, v_in, qa_in, qb_in, coef, send, v, qa, qb, d
+    yup, ydown, before, after, th, spread, v_in, qa_in, qb_in, coef, send, v, qa, qb
 ):
     del v_in, qa_in, qb_in
     for c in range(PITCH // 8):
@@ -316,8 +330,7 @@
             extra = jnp.where(row8 == NEAR + level, mix(FIRST[level], seam_after), extra)
         extras.append(extra)
     block = jnp.concatenate(extras, axis=0)
-    for ref, k in ((qa, 0), (qb, 1)):
-        spread_lanes(ref, SIDE, EXT, block, tables, k)
+    spread_lanes(qa, qb, SIDE, EXT, block, spread)
 
     for level in range(NEAR):
         pieces = chunks(level)
@@ -334,10 +347,12 @@
                     ref is v,
                 )
         if level == 0:
-            pieces = pieces[:1] + pieces[3:]
-        elif level == NEAR - 1:
-            pieces = pieces[:-1]
-        lift_lanes(level, spot, v, qa, qb, d, pieces)
+            rows = lane_rows(0, pieces[-1:])
+            for y in (0, 1, SIDE - 3, SIDE - 2, SIDE - 1):
+                rows += [(pl.ds(8 * c * PITCH + y, 8, stride=PITCH), 8) for c in range(PITCH // 8)]
+        else:
+            rows = lane_rows(level, pieces[: len(pieces) - (level == NEAR - 1)])
+        lift_lanes(level, rows, v, qa, qb)
 
     energy = [jnp.zeros((8, LANES), F32)] * NEAR
     kept = [jnp.zeros((8, LANES), F32)] * NEAR
@@ -368,10 +383,9 @@
                 target[level] = target[level] + part
 
     lane8 = lanes_of(8)
-    corners = [v[pl.ds(a * 16 * PITCH + b * 16, 1), :] for a in range(2) for b in range(2)]
     block = jnp.zeros((8, LANES), F32)
-    for i, corner in enumerate(corners):
-        block = jnp.where(row8 == i, corner, block)
+    for i in range(4):
+        block = jnp.where(row8 == i, v[pl.ds((i // 2 * PITCH + i % 2) * 16, 1), :], block)
     source, target = rows_of(LANES), lanes_of(LANES)
     pick = jnp.where((source == 16 * (target % 8)) & (target < 32), 1.0, 0.0).astype(F32)
     block = jnp.where(lane8 // 8 == row8, dot(block, pick), 0.0)
@@ -433,15 +447,10 @@
         sums_out[i] = (totals * scale)[:, :LEVELS]
 
     own = grid[pl.ds(spot[0], 1), :]
-    row8, lane8 = rows_of(8), lanes_of(8)
-    block = jnp.where((lane8 < 32) & (lane8 // 8 == row8), own, 0.0)
-    source, target = rows_of(LANES), lanes_of(LANES)
-    pick = jnp.where((target == 16 * (source % 8)) & (source < 32), 1.0, 0.0).astype(F32)
-    block = dot(block, pick)
-    start = lane8[:1] % 16 == 0
+    start = lanes_of(1) % 16 == 0
     for i in range(4):
         at = pl.ds(i * half, 1)
-        planes[at, :] = jnp.where(start, block[i : i + 1, :], planes[at, :])
+        planes[at, :] = jnp.where(start, stretch(roll(own, -8 * i)), planes[at, :])
     for a in range(2):
         target = out.at[pl.ds(a * half * SIDE, SIDE)]
         copies.append(pltpu.make_async_copy(planes.at[pl.ds(a * SIDE, SIDE)], target, sem.at[2 + a]))
@@ -463,7 +472,7 @@
     counts = [7.0 * cells / 8 ** (level + 1) for level in range(LEVELS)]
     f = fields.reshape(SIDE * SIDE, LANES)
     th = jnp.broadcast_to(jnp.pad(jnp.exp2(exponents.astype(F32)), (0, 3))[:, None], (8, LANES))
-    table, tables = (jnp.asarray(t) for t in constant_tables())
+    table, tables, spread = (jnp.asarray(t) for t in constant_tables())
     wy = jnp.asarray(W.astype(np.float32))
 
     def swap(up, down, axis):
@@ -473,26 +482,32 @@
         return before, after
 
     here = pl.BlockSpec(memory_space=pltpu.VMEM)
+    there = pl.BlockSpec(memory_space=pltpu.HBM)
 
     def pinned(a):
         return pltpu.with_memory_space_constraint(a, pltpu.VMEM)
 
-    def local(kernel, name, outs, *args, scalars=(), scratch=(), aliases={}):
+    def local(kernel, name, outs, *args, aliases={}):
         args = [pinned(a) for a in args]
         return pl.pallas_call(
             kernel,
-            in_specs=[pl.BlockSpec(memory_space=pltpu.SMEM)] * len(scalars) + [here] * len(args),
+            in_specs=[here] * len(args),
             out_specs=[here] * len(outs),
             out_shape=[pltpu.VMEM((rows, LANES), F32) for rows in outs],
-            scratch_shapes=[pltpu.VMEM((rows, LANES), F32) for rows in scratch],
             input_output_aliases=aliases,
             compiler_params=pltpu.CompilerParams(vmem_limit_bytes=8 << 20),
             name=name,
-        )(*scalars, *args)
+        )(*args)
 
     spot = lax.axis_index(("gx", "gy", "gz")).astype(jnp.int32).reshape(1)
     pz = pl.pallas_call(
-        ends_kernel, out_specs=here, out_shape=pltpu.VMEM((2 * SIDE, LANES), F32), name="ends"
+        ends_kernel,
+        in_specs=[there, here],
+        out_specs=here,
+        out_shape=pltpu.VMEM((2 * SIDE, LANES), F32),
+        scratch_shapes=[pltpu.VMEM((SIDE * SIDE, LANES), F32), pltpu.SemaphoreType.DMA(())],
+        compiler_params=pltpu.CompilerParams(vmem_limit_bytes=8 << 20),
+        name="ends",
     )(f, table)
     before, after = swap(pz, pz, "gz")
     fx, fy = local(faces_kernel, "faces", (EXT * SIDE, EXT * SIDE), f)
@@ -511,22 +526,17 @@
         prepare_kernel,
         "prepare",
         (block,) * 3,
-        *(f, ez, xe, xee, tables),
-        scalars=(spot,),
-        scratch=(block,),
+        *(f, ez, xe, xee, spread),
     )
     coef, send, *_ = local(
         levels_kernel,
         "levels",
         (SIDE * SIDE, devices, block, block, block),
-        *(yup, ydown, before, after, th, tables, v, qa, qb),
-        scalars=(spot,),
-        scratch=(block,),
-        aliases={7: 2, 8: 3, 9: 4},
+        *(yup, ydown, before, after, th, spread, v, qa, qb),
+        aliases={6: 2, 7: 3, 8: 4},
     )
     send, spot, th = lax.optimization_barrier((send, spot, th))
     got = lax.all_to_all(send.reshape(devices, 1, LANES), ("gx", "gy", "gz"), 0, 0).reshape(devices, LANES)
-    there = pl.BlockSpec(memory_space=pltpu.HBM)
     out, stats = pl.pallas_call(
         functools.partial(last_kernel, sizes=sizes, counts=counts),
         in_specs=[pl.BlockSpec(memory_space=pltpu.SMEM), here, here, here],

time: 53.2 us -> 52.8 us (level)
  blocking collectives: 21.6 us -> 24 us
  Pallas kernels: 9.58 us -> 7.43 us
  waiting for transfers between devices: 7.45 us -> 5.92 us
  local copies, waits for them, and re-layouts: 1.14 us -> 1.97 us
    all_to_all x1, blocking collectives: 21.6 us -> 24 us  [shards(): lax.all_to_all(send.reshape(devices, 1, LANES), ('gx', 'gy', 'gz'), 0, 0)]
    pallas_call x6, Pallas kernels: 8.12 us -> 5.85 us  [the longest x5 5.23 us: local(): pl.pallas_call(kernel, in_specs=[here] * len(args), out_specs=[here] * le...]
    ppermute x3, starting transfers between devices: 4.89 us -> 6.78 us  [swap(): before = lax.ppermute(up, axis, [(i, (i + 1) % n) for i in range(n)])]
    ppermute x3, waiting for transfers between devices: 5.06 us -> 3.23 us  [swap(): before = lax.ppermute(up, axis, [(i, (i + 1) % n) for i in range(n)])]
    ppermute x3, starting transfers between devices: 7.63 us -> 5.81 us  [swap(): after = lax.ppermute(down, axis, [((i + 1) % n, i) for i in range(n)])]
    unnamed x10 -> x14, local copies, waits for them, and re-layouts: 1.06 us -> 1.9 us
where the time goes in v6:
time: 52.8 us; the launch traced here: 52.6 us
  blocking collectives  24 us (45%)
  starting transfers between devices  12.6 us (24%)
  Pallas kernels  7.43 us (14%)
  waiting for transfers between devices  5.92 us (11%)
  local copies, waits for them, and re-layouts  1.97 us (4%)
  between operations  0.71 us (1%)
    all_to_all x1, blocking collectives, shards(): lax.all_to_all(send.reshape(devices, 1, LANES), ('gx', 'gy', 'gz'), 0, 0)  24 us
    ppermute x3, starting transfers between devices, swap(): before = lax.ppermute(up, axis, [(i, (i + 1) % n) for i in range(n)])  6.78 us
    ppermute x3, starting transfers between devices, swap(): after = lax.ppermute(down, axis, [((i + 1) % n, i) for i in range(n)])  5.81 us
    pallas_call x5, Pallas kernels, local(): pl.pallas_call(kernel, in_specs=[here] * len(args), out_specs=[here] * le...  5.23 us
    ppermute x3, waiting for transfers between devices, swap(): before = lax.ppermute(up, axis, [(i, (i + 1) % n) for i in range(n)])  3.23 us
    ppermute x3, waiting for transfers between devices, swap(): after = lax.ppermute(down, axis, [((i + 1) % n, i) for i in range(n)])  2.7 us
    unnamed x14, local copies, waits for them, and re-layouts  1.9 us
    pallas_call x1, Pallas kernels, shards(): pl.pallas_call(functools.partial(last_kernel, sizes=sizes, counts=counts)...  1.58 us
  transfers between devices with their start and end apart: 6, of which 4 were waited for; matrix products, arithmetic and copies ran while one was open for 0% of the time, Pallas kernels for 4%

profile of v6, /device:TPU:1, one launch (start us, length us, event | category | flops | bytes accessed | tf_op | source)
XLA Modules:
  0.0 52.6 jit_solution(9292221241138460459)
XLA Ops:
  0.6 0.0 copy-start
  0.6 1.0 %copy-done = f32[1,32,32,128]{3,2,1,0:T(8,128)S(1)} copy-done((f32[1,32,32,128]{3,2,1,0:T(8,128)S(1)}, f32[1,32,32,128]{3,2,1,0:T(8,128)}, u32[]{:S(2)}) %copy-start) | copy-done | bytes 524312
  1.7 0.0 copy-start.4
  1.7 0.8 %copy-done.4 = f32[128,128]{1,0:T(8,128)S(1)} copy-done((f32[128,128]{1,0:T(8,128)S(1)}, f32[128,128]{1,0:T(8,128)}, u32[]{:S(2)}) %copy-start.4) | copy-done | bytes 65560
  2.5 0.0 copy-start.2
  2.5 0.6 %ends.1.pz = f32[64,128]{1,0:T(8,128)S(1)} custom-call(f32[1024,128]{1,0:T(8,128)S(1)} %bitcast.7, f32[128,128]{1,0:T(8,128)S(1)} %copy-done.4), custom_call_target="tpu_custom_call" | custom-call | tf_op jit(solution)/shard_map/ends/pallas_call | solution.py:503
  3.1 2.2 %collective-permute-start = (f32[64,128]{1,0:T(8,128)S(1)}, f32[64,128]{1,0:T(8,128)S(1)}, u32[]{:S(2)}, u32[]{:S(2)}) collective-permute-start(f32[64,128]{1,0:T(8,128)S(1)} %ends.1.pz), channel_id=1, source_target_pairs={{0,1},{1,2},{2,3},{3,0},{4,5},{5,6},{6,7},{7,4},{8,9},{9,10},{10,1... | collective-permute-start | bytes 98312 | tf_op jit(solution)/shard_map/ppermute | solution.py:480
  5.3 1.5 %collective-permute-start.1 = (f32[64,128]{1,0:T(8,128)S(1)}, f32[64,128]{1,0:T(8,128)S(1)}, u32[]{:S(2)}, u32[]{:S(2)}) collective-permute-start(f32[64,128]{1,0:T(8,128)S(1)} %ends.1.pz), channel_id=1, source_target_pairs={{1,0},{2,1},{3,2},{0,3},{5,4},{6,5},{7,6},{4,7},{9,8},{10,9},{11,1... | collective-permute-start | bytes 98312 | tf_op jit(solution)/shard_map/ppermute | solution.py:481
  6.9 0.4 faces.1
  7.3 0.8 %collective-permute-done.before = f32[64,128]{1,0:T(8,128)S(1)} collective-permute-done((f32[64,128]{1,0:T(8,128)S(1)}, f32[64,128]{1,0:T(8,128)S(1)}, u32[]{:S(2)}, u32[]{:S(2)}) %collective-permute-start) | collective-permute-done | bytes 32800 | tf_op jit(solution)/shard_map/ppermute | solution.py:480
  8.1 0.0 collective-permute-done.1.after
  8.1 0.0 copy-done.2
  8.1 0.3 depth.1
  8.4 0.0 copy-start.5
  8.4 3.2 %collective-permute-start.2 = (f32[160,128]{1,0:T(8,128)S(1)}, f32[160,128]{1,0:T(8,128)S(1)}, u32[]{:S(2)}, u32[]{:S(2)}) collective-permute-start(f32[160,128]{1,0:T(8,128)S(1)} %get-tuple-element.22.up), channel_id=1, source_target_pairs={{0,32},{32,64},{64,96},{96,128},{128,160},{160,192},{192,224},{224... | collective-permute-start | bytes 245768 | tf_op jit(solution)/shard_map/ppermute | solution.py:480
  11.7 0.3 collective-permute-start.3
  11.9 1.2 %collective-permute-done.2.before = f32[160,128]{1,0:T(8,128)S(1)} collective-permute-done((f32[160,128]{1,0:T(8,128)S(1)}, f32[160,128]{1,0:T(8,128)S(1)}, u32[]{:S(2)}, u32[]{:S(2)}) %collective-permute-start.2) | collective-permute-done | bytes 81952 | tf_op jit(solution)/shard_map/ppermute | solution.py:480
  13.1 2.7 %collective-permute-done.3.after = f32[160,128]{1,0:T(8,128)S(1)} collective-permute-done((f32[160,128]{1,0:T(8,128)S(1)}, f32[160,128]{1,0:T(8,128)S(1)}, u32[]{:S(2)}, u32[]{:S(2)}) %collective-permute-start.3) | collective-permute-done | bytes 81952 | tf_op jit(solution)/shard_map/ppermute | solution.py:481
  15.8 0.0 copy-done.5
  15.8 0.3 width.1
  16.2 1.4 %collective-permute-start.4 = (f32[184,128]{1,0:T(8,128)S(1)}, f32[184,128]{1,0:T(8,128)S(1)}, u32[]{:S(2)}, u32[]{:S(2)}) collective-permute-start(f32[184,128]{1,0:T(8,128)S(1)} %get-tuple-element.26.yup), channel_id=1, source_target_pairs={{0,4},{4,8},{8,12},{12,16},{16,20},{20,24},{24,28},{28,0},{1,5},{5... | collective-permute-start | bytes 282632 | tf_op jit(solution)/shard_map/ppermute | solution.py:480
  17.5 4.0 %collective-permute-start.5 = (f32[184,128]{1,0:T(8,128)S(1)}, f32[184,128]{1,0:T(8,128)S(1)}, u32[]{:S(2)}, u32[]{:S(2)}) collective-permute-start(f32[184,128]{1,0:T(8,128)S(1)} %get-tuple-element.27.ydown), channel_id=1, source_target_pairs={{4,0},{8,4},{12,8},{16,12},{20,16},{24,20},{28,24},{0,28},{5,1},{9... | collective-permute-start | bytes 282632 | tf_op jit(solution)/shard_map/ppermute | solution.py:481
  21.6 0.0 copy-done.6
  21.6 0.0 copy-done.1
  21.6 0.0 copy-done.3
  21.6 1.6 %prepare.1 = (f32[1600,128]{1,0:T(8,128)S(1)}, f32[1600,128]{1,0:T(8,128)S(1)}, f32[1600,128]{1,0:T(8,128)S(1)}) custom-call(f32[1024,128]{1,0:T(8,128)S(1)} %bitcast.9, f32[64,128]{1,0:T(8,128)S(1)} %get-tuple-element.25.ez, f32[256,128]{1,0:T(8,128)S(1)} %get-tuple-element.28.xe, f32[32,128]{1,0:T(8,128)S(1)} %get-tuple-element.29.xee, ...), custom_call_target="tpu_custom_call" | custom-call | tf_op jit(solution)/shard_map/prepare/pallas_call | solution.py:492
  23.2 1.2 %collective-permute-done.4.before = f32[184,128]{1,0:T(8,128)S(1)} collective-permute-done((f32[184,128]{1,0:T(8,128)S(1)}, f32[184,128]{1,0:T(8,128)S(1)}, u32[]{:S(2)}, u32[]{:S(2)}) %collective-permute-start.4) | collective-permute-done | bytes 94240 | tf_op jit(solution)/shard_map/ppermute | solution.py:480
  24.4 0.0 collective-permute-done.5.after
  24.4 0.1 broadcast_in_dim.2.th
  24.5 2.5 %levels.1 = (f32[1024,128]{1,0:T(8,128)S(1)}, f32[256,128]{1,0:T(8,128)S(1)}, f32[1600,128]{1,0:T(8,128)S(1)}, f32[1600,128]{1,0:T(8,128)S(1)}, f32[1600,128]{1,0:T(8,128)S(1)}) custom-call(f32[184,128]{1,0:T(8,128)S(1)} %get-tuple-element.26.yup, ...), custom_call_target="tpu_custom_call", output_to_operand_aliasing={{2}: (6, {}), {3}: (7, {}), {4}: (8, {})} | custom-call | tf_op jit(solution)/shard_map/levels/pallas_call | solution.py:492
  27.0 24.0 %all_to_all.5 = f32[256,1,128]{2,1,0:T(1,128)S(1)} all-to-all(f32[256,1,128]{2,1,0:T(1,128)S(1)} %bitcast.11), channel_id=1, replica_groups=mesh['gx'=8,'gy'=8,'gz'=4] {'gx','gy','gz'}, dimensions={0} | all-to-all | bytes 262144 | tf_op jit(solution)/shard_map/all_to_all | solution.py:539
  51.1 1.6 %last.1 = (f32[1024,128]{1,0:T(8,128)}, f32[2,1,5]{2,1,0:T(1,128)}) custom-call(s32[1]{0:T(128)} %bitcast.1.spot, f32[256,128]{1,0:T(8,128)S(1)} %bitcast.10, f32[1024,128]{1,0:T(8,128)S(1)} %get-tuple-element.36.coef, f32[8,128]{1,0:T(8,128)S(1)} %broadcast_in_dim.2.th), custom_call_target="tpu_custom_call" | custom-call | tf_op jit(solution)/shard_map/last/pallas_call | solution.py:540
  (5 shorter events, 0.0 us)
Async XLA Ops:
  0.6 1.0 %copy-start = (f32[1,32,32,128]{3,2,1,0:T(8,128)S(1)}, f32[1,32,32,128]{3,2,1,0:T(8,128)}, u32[]{:S(2)}) copy-start(f32[1,32,32,128]{3,2,1,0:T(8,128)} %param.6) | copy-start | bytes 1572868
  1.7 0.8 %copy-start.4 = (f32[128,128]{1,0:T(8,128)S(1)}, f32[128,128]{1,0:T(8,128)}, u32[]{:S(2)}) copy-start(f32[128,128]{1,0:T(8,128)} %constant.30.clone.table) | copy-start | bytes 196612
  2.5 5.6 %copy-start.2 = (f32[1024,128]{1,0:T(8,128)S(1)}, f32[1024,128]{1,0:T(8,128)}, u32[]{:S(2)}) copy-start(f32[1024,128]{1,0:T(8,128)} %constant.31.clone.tables) | copy-start | bytes 1572868
  3.1 4.9 %collective-permute-start = (f32[64,128]{1,0:T(8,128)S(1)}, f32[64,128]{1,0:T(8,128)S(1)}, u32[]{:S(2)}, u32[]{:S(2)}) collective-permute-start(f32[64,128]{1,0:T(8,128)S(1)} %ends.1.pz), channel_id=1, source_target_pairs={{0,1},{1,2},{2,3},{3,0},{4,5},{5,6},{6,7},{7,4},{8,9},{9,10},{10,1... | collective-permute-start | bytes 98312 | tf_op jit(solution)/shard_map/ppermute | solution.py:480
  5.3 2.8 %collective-permute-start.1 = (f32[64,128]{1,0:T(8,128)S(1)}, f32[64,128]{1,0:T(8,128)S(1)}, u32[]{:S(2)}, u32[]{:S(2)}) collective-permute-start(f32[64,128]{1,0:T(8,128)S(1)} %ends.1.pz), channel_id=1, source_target_pairs={{1,0},{2,1},{3,2},{0,3},{5,4},{6,5},{7,6},{4,7},{9,8},{10,9},{11,1... | collective-permute-start | bytes 98312 | tf_op jit(solution)/shard_map/ppermute | solution.py:481
  8.4 7.4 %copy-start.5 = (f32[8,32]{1,0:T(8,128)S(1)}, f32[8,32]{1,0:T(8,128)}, u32[]{:S(2)}) copy-start(f32[8,32]{1,0:T(8,128)} %constant.33.clone.wy) | copy-start | bytes 3076
  8.4 4.7 %collective-permute-start.2 = (f32[160,128]{1,0:T(8,128)S(1)}, f32[160,128]{1,0:T(8,128)S(1)}, u32[]{:S(2)}, u32[]{:S(2)}) collective-permute-start(f32[160,128]{1,0:T(8,128)S(1)} %get-tuple-element.22.up), channel_id=1, source_target_pairs={{0,32},{32,64},{64,96},{96,128},{128,160},{160,192},{192,224},{224... | collective-permute-start | bytes 245768 | tf_op jit(solution)/shard_map/ppermute | solution.py:480
  11.7 4.2 %collective-permute-start.3 = (f32[160,128]{1,0:T(8,128)S(1)}, f32[160,128]{1,0:T(8,128)S(1)}, u32[]{:S(2)}, u32[]{:S(2)}) collective-permute-start(f32[160,128]{1,0:T(8,128)S(1)} %get-tuple-element.23.down), channel_id=1, source_target_pairs={{32,0},{64,32},{96,64},{128,96},{160,128},{192,160},{224,192},{0,2... | collective-permute-start | bytes 245768 | tf_op jit(solution)/shard_map/ppermute | solution.py:481
  15.8 5.8 %copy-start.1 = (f32[1,32,32,128]{3,2,1,0:T(8,128)S(1)}, f32[1,32,32,128]{3,2,1,0:T(8,128)}, u32[]{:S(2)}) copy-start(f32[1,32,32,128]{3,2,1,0:T(8,128)} %param.6) | copy-start | bytes 1572868
  15.8 5.8 %copy-start.3 = (f32[128,256]{1,0:T(8,128)S(1)}, f32[128,256]{1,0:T(8,128)}, u32[]{:S(2)}) copy-start(f32[128,256]{1,0:T(8,128)} %constant.32.clone.spread) | copy-start | bytes 393220
  16.2 5.4 %copy-start.6 = (s32[5]{0:T(128)S(1)}, s32[5]{0:T(128)}, u32[]{:S(2)}) copy-start(s32[5]{0:T(128)} %param.7) | copy-start | bytes 64
  16.2 8.3 %collective-permute-start.4 = (f32[184,128]{1,0:T(8,128)S(1)}, f32[184,128]{1,0:T(8,128)S(1)}, u32[]{:S(2)}, u32[]{:S(2)}) collective-permute-start(f32[184,128]{1,0:T(8,128)S(1)} %get-tuple-element.26.yup), channel_id=1, source_target_pairs={{0,4},{4,8},{8,12},{12,16},{16,20},{20,24},{24,28},{28,0},{1,5},{5... | collective-permute-start | bytes 282632 | tf_op jit(solution)/shard_map/ppermute | solution.py:480
  17.5 6.9 %collective-permute-start.5 = (f32[184,128]{1,0:T(8,128)S(1)}, f32[184,128]{1,0:T(8,128)S(1)}, u32[]{:S(2)}, u32[]{:S(2)}) collective-permute-start(f32[184,128]{1,0:T(8,128)S(1)} %get-tuple-element.27.ydown), channel_id=1, source_target_pairs={{4,0},{8,4},{12,8},{16,12},{20,16},{24,20},{28,24},{0,28},{5,1},{9... | collective-permute-start | bytes 282632 | tf_op jit(solution)/shard_map/ppermute | solution.py:481

commit v7 on v6

--- a/solution.py
+++ b/solution.py
@@ -126,11 +126,13 @@
     return total
 
 
-def ends_kernel(f, table, pz, block, sem):
-    copy = pltpu.make_async_copy(f, block, sem)
-    copy.start()
-    copy.wait()
-    out = dot(block[...], table[...])
+def ends_kernel(f, table, pz, block, weights, sem):
+    copies = [pltpu.make_async_copy(f, block, sem.at[0]), pltpu.make_async_copy(table, weights, sem.at[1])]
+    for copy in copies:
+        copy.start()
+    for copy in copies:
+        copy.wait()
+    out = dot(block[...], weights[...])
     group = lanes_of(SIDE) // EXT
     for half in range(2):
         packed = jnp.zeros((SIDE, LANES), F32)
@@ -500,15 +502,15 @@
         )(*args)
 
     spot = lax.axis_index(("gx", "gy", "gz")).astype(jnp.int32).reshape(1)
-    pz = pl.pallas_call(
+    pz, f = pl.pallas_call(
         ends_kernel,
-        in_specs=[there, here],
-        out_specs=here,
-        out_shape=pltpu.VMEM((2 * SIDE, LANES), F32),
-        scratch_shapes=[pltpu.VMEM((SIDE * SIDE, LANES), F32), pltpu.SemaphoreType.DMA(())],
+        in_specs=[there] * 2,
+        out_specs=[here] * 2,
+        out_shape=[pltpu.VMEM((2 * SIDE, LANES), F32), pltpu.VMEM((SIDE * SIDE, LANES), F32)],
+        scratch_shapes=[pltpu.VMEM((LANES, LANES), F32), pltpu.SemaphoreType.DMA((2,))],
         compiler_params=pltpu.CompilerParams(vmem_limit_bytes=8 << 20),
         name="ends",
-    )(f, table)
+    )(*(pltpu.with_memory_space_constraint(a, pltpu.HBM) for a in (f, table)))
     before, after = swap(pz, pz, "gz")
     fx, fy = local(faces_kernel, "faces", (EXT * SIDE, EXT * SIDE), f)
     message = (NEAR + 1) * SIDE

time: 52.8 us -> 51.9 us (0.983)
  local copies, waits for them, and re-layouts: 1.97 us -> 0.1 us
  Pallas kernels: 7.43 us -> 8.51 us
    unnamed x14 -> x8, local copies, waits for them, and re-layouts: 1.9 us -> 0.02 us
    pallas_call x1, Pallas kernels: 0.62 us -> 1.69 us  [shards(): pl.pallas_call(ends_kernel, in_specs=[there] * 2, out_specs=[here] * 2, o...]
where the time goes in v7:
time: 51.9 us; the launch traced here: 51.8 us
  blocking collectives  24 us (46%)
  starting transfers between devices  12.6 us (24%)
  Pallas kernels  8.51 us (16%)
  waiting for transfers between devices  5.94 us (11%)
  between operations  0.7 us (1%)
    all_to_all x1, blocking collectives, shards(): lax.all_to_all(send.reshape(devices, 1, LANES), ('gx', 'gy', 'gz'), 0, 0)  24 us
    ppermute x3, starting transfers between devices, swap(): before = lax.ppermute(up, axis, [(i, (i + 1) % n) for i in range(n)])  6.78 us
    ppermute x3, starting transfers between devices, swap(): after = lax.ppermute(down, axis, [((i + 1) % n, i) for i in range(n)])  5.81 us
    pallas_call x5, Pallas kernels, local(): pl.pallas_call(kernel, in_specs=[here] * len(args), out_specs=[here] * le...  5.24 us
    ppermute x3, waiting for transfers between devices, swap(): before = lax.ppermute(up, axis, [(i, (i + 1) % n) for i in range(n)])  3.24 us
    ppermute x3, waiting for transfers between devices, swap(): after = lax.ppermute(down, axis, [((i + 1) % n, i) for i in range(n)])  2.7 us
    pallas_call x1, Pallas kernels, shards(): pl.pallas_call(ends_kernel, in_specs=[there] * 2, out_specs=[here] * 2, o...  1.69 us
    pallas_call x1, Pallas kernels, shards(): pl.pallas_call(functools.partial(last_kernel, sizes=sizes, counts=counts)...  1.58 us
  transfers between devices with their start and end apart: 6, of which 4 were waited for; matrix products, arithmetic and copies ran while one was open for 0% of the time, Pallas kernels for 4%

profile of v7, /device:TPU:1, one launch (start us, length us, event | category | flops | bytes accessed | tf_op | source)
XLA Modules:
  0.0 51.8 jit_solution(12077125671134915580)
XLA Ops:
  0.6 0.0 copy-start
  0.6 1.7 %ends.1 = (f32[64,128]{1,0:T(8,128)S(1)}, f32[1024,128]{1,0:T(8,128)S(1)}) custom-call(f32[1024,128]{1,0:T(8,128)} %bitcast.9, f32[128,128]{1,0:T(8,128)} %constant.30.clone.table), custom_call_target="tpu_custom_call" | custom-call | tf_op jit(solution)/shard_map/ends/pallas_call | solution.py:505
  2.3 2.2 %collective-permute-start = (f32[64,128]{1,0:T(8,128)S(1)}, f32[64,128]{1,0:T(8,128)S(1)}, u32[]{:S(2)}, u32[]{:S(2)}) collective-permute-start(f32[64,128]{1,0:T(8,128)S(1)} %get-tuple-element.23.pz), channel_id=1, source_target_pairs={{0,1},{1,2},{2,3},{3,0},{4,5},{5,6},{6,7},{7,4},{8,9},{9,10},{10,1... | collective-permute-start | bytes 98312 | tf_op jit(solution)/shard_map/ppermute | solution.py:482
  4.5 1.5 %collective-permute-start.1 = (f32[64,128]{1,0:T(8,128)S(1)}, f32[64,128]{1,0:T(8,128)S(1)}, u32[]{:S(2)}, u32[]{:S(2)}) collective-permute-start(f32[64,128]{1,0:T(8,128)S(1)} %get-tuple-element.23.pz), channel_id=1, source_target_pairs={{1,0},{2,1},{3,2},{0,3},{5,4},{6,5},{7,6},{4,7},{9,8},{10,9},{11,1... | collective-permute-start | bytes 98312 | tf_op jit(solution)/shard_map/ppermute | solution.py:483
  6.1 0.4 faces.1
  6.5 0.8 %collective-permute-done.before = f32[64,128]{1,0:T(8,128)S(1)} collective-permute-done((f32[64,128]{1,0:T(8,128)S(1)}, f32[64,128]{1,0:T(8,128)S(1)}, u32[]{:S(2)}, u32[]{:S(2)}) %collective-permute-start) | collective-permute-done | bytes 32800 | tf_op jit(solution)/shard_map/ppermute | solution.py:482
  7.3 0.0 collective-permute-done.1.after
  7.3 0.0 copy-done
  7.3 0.3 depth.1
  7.6 0.0 copy-start.2
  7.6 3.2 %collective-permute-start.2 = (f32[160,128]{1,0:T(8,128)S(1)}, f32[160,128]{1,0:T(8,128)S(1)}, u32[]{:S(2)}, u32[]{:S(2)}) collective-permute-start(f32[160,128]{1,0:T(8,128)S(1)} %get-tuple-element.26.up), channel_id=1, source_target_pairs={{0,32},{32,64},{64,96},{96,128},{128,160},{160,192},{192,224},{224... | collective-permute-start | bytes 245768 | tf_op jit(solution)/shard_map/ppermute | solution.py:482
  10.9 0.3 collective-permute-start.3
  11.1 1.2 %collective-permute-done.2.before = f32[160,128]{1,0:T(8,128)S(1)} collective-permute-done((f32[160,128]{1,0:T(8,128)S(1)}, f32[160,128]{1,0:T(8,128)S(1)}, u32[]{:S(2)}, u32[]{:S(2)}) %collective-permute-start.2) | collective-permute-done | bytes 81952 | tf_op jit(solution)/shard_map/ppermute | solution.py:482
  12.3 2.7 %collective-permute-done.3.after = f32[160,128]{1,0:T(8,128)S(1)} collective-permute-done((f32[160,128]{1,0:T(8,128)S(1)}, f32[160,128]{1,0:T(8,128)S(1)}, u32[]{:S(2)}, u32[]{:S(2)}) %collective-permute-start.3) | collective-permute-done | bytes 81952 | tf_op jit(solution)/shard_map/ppermute | solution.py:483
  15.0 0.0 copy-done.2
  15.0 0.0 copy-start.1
  15.0 0.3 width.1
  15.4 0.0 copy-start.3
  15.4 1.4 %collective-permute-start.4 = (f32[184,128]{1,0:T(8,128)S(1)}, f32[184,128]{1,0:T(8,128)S(1)}, u32[]{:S(2)}, u32[]{:S(2)}) collective-permute-start(f32[184,128]{1,0:T(8,128)S(1)} %get-tuple-element.30.yup), channel_id=1, source_target_pairs={{0,4},{4,8},{8,12},{12,16},{16,20},{20,24},{24,28},{28,0},{1,5},{5... | collective-permute-start | bytes 282632 | tf_op jit(solution)/shard_map/ppermute | solution.py:482
  16.7 4.0 %collective-permute-start.5 = (f32[184,128]{1,0:T(8,128)S(1)}, f32[184,128]{1,0:T(8,128)S(1)}, u32[]{:S(2)}, u32[]{:S(2)}) collective-permute-start(f32[184,128]{1,0:T(8,128)S(1)} %get-tuple-element.31.ydown), channel_id=1, source_target_pairs={{4,0},{8,4},{12,8},{16,12},{20,16},{24,20},{28,24},{0,28},{5,1},{9... | collective-permute-start | bytes 282632 | tf_op jit(solution)/shard_map/ppermute | solution.py:483
  20.7 0.0 copy-done.3
  20.8 0.0 copy-done.1
  20.8 1.6 %prepare.1 = (f32[1600,128]{1,0:T(8,128)S(1)}, f32[1600,128]{1,0:T(8,128)S(1)}, f32[1600,128]{1,0:T(8,128)S(1)}) custom-call(f32[1024,128]{1,0:T(8,128)S(1)} %get-tuple-element.24.f, f32[64,128]{1,0:T(8,128)S(1)} %get-tuple-element.29.ez, f32[256,128]{1,0:T(8,128)S(1)} %get-tuple-element.32.xe, f32[32,128]{1,0:T(8,128)S(1)} %get-tuple-element.33.xee, ...), custom_call_target="tpu_custom_call" | custom-call | tf_op jit(solution)/shard_map/prepare/pallas_call | solution.py:494
  22.4 1.2 %collective-permute-done.4.before = f32[184,128]{1,0:T(8,128)S(1)} collective-permute-done((f32[184,128]{1,0:T(8,128)S(1)}, f32[184,128]{1,0:T(8,128)S(1)}, u32[]{:S(2)}, u32[]{:S(2)}) %collective-permute-start.4) | collective-permute-done | bytes 94240 | tf_op jit(solution)/shard_map/ppermute | solution.py:482
  23.6 0.0 collective-permute-done.5.after
  23.7 0.1 broadcast_in_dim.2.th
  23.7 2.5 %levels.1 = (f32[1024,128]{1,0:T(8,128)S(1)}, f32[256,128]{1,0:T(8,128)S(1)}, f32[1600,128]{1,0:T(8,128)S(1)}, f32[1600,128]{1,0:T(8,128)S(1)}, f32[1600,128]{1,0:T(8,128)S(1)}) custom-call(f32[184,128]{1,0:T(8,128)S(1)} %get-tuple-element.30.yup, ...), custom_call_target="tpu_custom_call", output_to_operand_aliasing={{2}: (6, {}), {3}: (7, {}), {4}: (8, {})} | custom-call | tf_op jit(solution)/shard_map/levels/pallas_call | solution.py:494
  26.3 24.0 %all_to_all.5 = f32[256,1,128]{2,1,0:T(1,128)S(1)} all-to-all(f32[256,1,128]{2,1,0:T(1,128)S(1)} %bitcast.8), channel_id=1, replica_groups=mesh['gx'=8,'gy'=8,'gz'=4] {'gx','gy','gz'}, dimensions={0} | all-to-all | bytes 262144 | tf_op jit(solution)/shard_map/all_to_all | solution.py:541
  50.2 1.6 %last.1 = (f32[1024,128]{1,0:T(8,128)}, f32[2,1,5]{2,1,0:T(1,128)}) custom-call(s32[1]{0:T(128)} %bitcast.1.spot, f32[256,128]{1,0:T(8,128)S(1)} %bitcast.7, f32[1024,128]{1,0:T(8,128)S(1)} %get-tuple-element.40.coef, f32[8,128]{1,0:T(8,128)S(1)} %broadcast_in_dim.2.th), custom_call_target="tpu_custom_call" | custom-call | tf_op jit(solution)/shard_map/last/pallas_call | solution.py:542
  (2 shorter events, 0.0 us)
Async XLA Ops:
  0.6 6.7 %copy-start = (f32[1024,128]{1,0:T(8,128)S(1)}, f32[1024,128]{1,0:T(8,128)}, u32[]{:S(2)}) copy-start(f32[1024,128]{1,0:T(8,128)} %constant.31.clone.tables) | copy-start | bytes 1572868
  2.3 4.9 %collective-permute-start = (f32[64,128]{1,0:T(8,128)S(1)}, f32[64,128]{1,0:T(8,128)S(1)}, u32[]{:S(2)}, u32[]{:S(2)}) collective-permute-start(f32[64,128]{1,0:T(8,128)S(1)} %get-tuple-element.23.pz), channel_id=1, source_target_pairs={{0,1},{1,2},{2,3},{3,0},{4,5},{5,6},{6,7},{7,4},{8,9},{9,10},{10,1... | collective-permute-start | bytes 98312 | tf_op jit(solution)/shard_map/ppermute | solution.py:482
  4.5 2.8 %collective-permute-start.1 = (f32[64,128]{1,0:T(8,128)S(1)}, f32[64,128]{1,0:T(8,128)S(1)}, u32[]{:S(2)}, u32[]{:S(2)}) collective-permute-start(f32[64,128]{1,0:T(8,128)S(1)} %get-tuple-element.23.pz), channel_id=1, source_target_pairs={{1,0},{2,1},{3,2},{0,3},{5,4},{6,5},{7,6},{4,7},{9,8},{10,9},{11,1... | collective-permute-start | bytes 98312 | tf_op jit(solution)/shard_map/ppermute | solution.py:483
  7.6 7.4 %copy-start.2 = (f32[8,32]{1,0:T(8,128)S(1)}, f32[8,32]{1,0:T(8,128)}, u32[]{:S(2)}) copy-start(f32[8,32]{1,0:T(8,128)} %constant.33.clone.wy) | copy-start | bytes 3076
  7.6 4.7 %collective-permute-start.2 = (f32[160,128]{1,0:T(8,128)S(1)}, f32[160,128]{1,0:T(8,128)S(1)}, u32[]{:S(2)}, u32[]{:S(2)}) collective-permute-start(f32[160,128]{1,0:T(8,128)S(1)} %get-tuple-element.26.up), channel_id=1, source_target_pairs={{0,32},{32,64},{64,96},{96,128},{128,160},{160,192},{192,224},{224... | collective-permute-start | bytes 245768 | tf_op jit(solution)/shard_map/ppermute | solution.py:482
  10.9 4.2 %collective-permute-start.3 = (f32[160,128]{1,0:T(8,128)S(1)}, f32[160,128]{1,0:T(8,128)S(1)}, u32[]{:S(2)}, u32[]{:S(2)}) collective-permute-start(f32[160,128]{1,0:T(8,128)S(1)} %get-tuple-element.27.down), channel_id=1, source_target_pairs={{32,0},{64,32},{96,64},{128,96},{160,128},{192,160},{224,192},{0,2... | collective-permute-start | bytes 245768 | tf_op jit(solution)/shard_map/ppermute | solution.py:483
  15.0 5.8 %copy-start.1 = (f32[128,256]{1,0:T(8,128)S(1)}, f32[128,256]{1,0:T(8,128)}, u32[]{:S(2)}) copy-start(f32[128,256]{1,0:T(8,128)} %constant.32.clone.spread) | copy-start | bytes 393220
  15.4 5.4 %copy-start.3 = (s32[5]{0:T(128)S(1)}, s32[5]{0:T(128)}, u32[]{:S(2)}) copy-start(s32[5]{0:T(128)} %param.7) | copy-start | bytes 64
  15.4 8.3 %collective-permute-start.4 = (f32[184,128]{1,0:T(8,128)S(1)}, f32[184,128]{1,0:T(8,128)S(1)}, u32[]{:S(2)}, u32[]{:S(2)}) collective-permute-start(f32[184,128]{1,0:T(8,128)S(1)} %get-tuple-element.30.yup), channel_id=1, source_target_pairs={{0,4},{4,8},{8,12},{12,16},{16,20},{20,24},{24,28},{28,0},{1,5},{5... | collective-permute-start | bytes 282632 | tf_op jit(solution)/shard_map/ppermute | solution.py:482
  16.7 6.9 %collective-permute-start.5 = (f32[184,128]{1,0:T(8,128)S(1)}, f32[184,128]{1,0:T(8,128)S(1)}, u32[]{:S(2)}, u32[]{:S(2)}) collective-permute-start(f32[184,128]{1,0:T(8,128)S(1)} %get-tuple-element.31.ydown), channel_id=1, source_target_pairs={{4,0},{8,4},{12,8},{16,12},{20,16},{24,20},{28,24},{0,28},{5,1},{9... | collective-permute-start | bytes 282632 | tf_op jit(solution)/shard_map/ppermute | solution.py:483

commit v8 on v7

--- a/solution.py
+++ b/solution.py
@@ -440,14 +440,6 @@
         square, size = jnp.where(detail, a * a, 0.0), jnp.where(detail, jnp.abs(shrunk), 0.0)
         energy = square if energy is None else energy + square
         kept = size if kept is None else kept + size
-    lane1 = lanes_of(1)
-    for i, (part, base) in enumerate(((energy, 32), (kept, 36))):
-        totals = jnp.where(lane1 == NEAR, jnp.sum(part), roll(sums, -base))
-        scale = jnp.zeros((1, LANES), F32)
-        for level in range(LEVELS):
-            scale = jnp.where(lane1 == level, 1.0 / counts[level], scale)
-        sums_out[i] = (totals * scale)[:, :LEVELS]
-
     own = grid[pl.ds(spot[0], 1), :]
     start = lanes_of(1) % 16 == 0
     for i in range(4):
@@ -456,9 +448,16 @@
     for a in range(2):
         target = out.at[pl.ds(a * half * SIDE, SIDE)]
         copies.append(pltpu.make_async_copy(planes.at[pl.ds(a * SIDE, SIDE)], target, sem.at[2 + a]))
+        copies[2 + a].start()
+    lane1 = lanes_of(1)
+    for i, (part, base) in enumerate(((energy, 32), (kept, 36))):
+        totals = jnp.where(lane1 == NEAR, jnp.sum(part), roll(sums, -base))
+        scale = jnp.zeros((1, LANES), F32)
+        for level in range(LEVELS):
+            scale = jnp.where(lane1 == level, 1.0 / counts[level], scale)
+        sums_out[i] = (totals * scale)[:, :LEVELS]
     copies.append(pltpu.make_async_copy(sums_out, stats, sem.at[4]))
-    for copy in copies[2:]:
-        copy.start()
+    copies[4].start()
     for copy in copies:
         copy.wait()
 

time: 51.9 us -> 51.9 us (level)
  no operation moved by 1% of the time
where the time goes in v8:
time: 51.9 us; the launch traced here: 51.8 us
  blocking collectives  24 us (46%)
  starting transfers between devices  12.6 us (24%)
  Pallas kernels  8.51 us (16%)
  waiting for transfers between devices  5.94 us (11%)
  between operations  0.7 us (1%)
    all_to_all x1, blocking collectives, shards(): lax.all_to_all(send.reshape(devices, 1, LANES), ('gx', 'gy', 'gz'), 0, 0)  24 us
    ppermute x3, starting transfers between devices, swap(): before = lax.ppermute(up, axis, [(i, (i + 1) % n) for i in range(n)])  6.78 us
    ppermute x3, starting transfers between devices, swap(): after = lax.ppermute(down, axis, [((i + 1) % n, i) for i in range(n)])  5.81 us
    pallas_call x5, Pallas kernels, local(): pl.pallas_call(kernel, in_specs=[here] * len(args), out_specs=[here] * le...  5.24 us
    ppermute x3, waiting for transfers between devices, swap(): before = lax.ppermute(up, axis, [(i, (i + 1) % n) for i in range(n)])  3.24 us
    ppermute x3, waiting for transfers between devices, swap(): after = lax.ppermute(down, axis, [((i + 1) % n, i) for i in range(n)])  2.7 us
    pallas_call x1, Pallas kernels, shards(): pl.pallas_call(ends_kernel, in_specs=[there] * 2, out_specs=[here] * 2, o...  1.69 us
    pallas_call x1, Pallas kernels, shards(): pl.pallas_call(functools.partial(last_kernel, sizes=sizes, counts=counts)...  1.58 us
  transfers between devices with their start and end apart: 6, of which 4 were waited for; matrix products, arithmetic and copies ran while one was open for 0% of the time, Pallas kernels for 4%

profile of v8, /device:TPU:1, one launch (start us, length us, event | category | flops | bytes accessed | tf_op | source)
XLA Modules:
  0.0 51.8 jit_solution(12077125671134915580)
XLA Ops:
  0.6 0.0 copy-start
  0.6 1.7 %ends.1 = (f32[64,128]{1,0:T(8,128)S(1)}, f32[1024,128]{1,0:T(8,128)S(1)}) custom-call(f32[1024,128]{1,0:T(8,128)} %bitcast.9, f32[128,128]{1,0:T(8,128)} %constant.30.clone.table), custom_call_target="tpu_custom_call" | custom-call | tf_op jit(solution)/shard_map/ends/pallas_call | solution.py:504
  2.3 2.2 %collective-permute-start = (f32[64,128]{1,0:T(8,128)S(1)}, f32[64,128]{1,0:T(8,128)S(1)}, u32[]{:S(2)}, u32[]{:S(2)}) collective-permute-start(f32[64,128]{1,0:T(8,128)S(1)} %get-tuple-element.23.pz), channel_id=1, source_target_pairs={{0,1},{1,2},{2,3},{3,0},{4,5},{5,6},{6,7},{7,4},{8,9},{9,10},{10,1... | collective-permute-start | bytes 98312 | tf_op jit(solution)/shard_map/ppermute | solution.py:481
  4.5 1.5 %collective-permute-start.1 = (f32[64,128]{1,0:T(8,128)S(1)}, f32[64,128]{1,0:T(8,128)S(1)}, u32[]{:S(2)}, u32[]{:S(2)}) collective-permute-start(f32[64,128]{1,0:T(8,128)S(1)} %get-tuple-element.23.pz), channel_id=1, source_target_pairs={{1,0},{2,1},{3,2},{0,3},{5,4},{6,5},{7,6},{4,7},{9,8},{10,9},{11,1... | collective-permute-start | bytes 98312 | tf_op jit(solution)/shard_map/ppermute | solution.py:482
  6.1 0.4 faces.1
  6.5 0.8 %collective-permute-done.before = f32[64,128]{1,0:T(8,128)S(1)} collective-permute-done((f32[64,128]{1,0:T(8,128)S(1)}, f32[64,128]{1,0:T(8,128)S(1)}, u32[]{:S(2)}, u32[]{:S(2)}) %collective-permute-start) | collective-permute-done | bytes 32800 | tf_op jit(solution)/shard_map/ppermute | solution.py:481
  7.3 0.0 collective-permute-done.1.after
  7.3 0.0 copy-done
  7.3 0.3 depth.1
  7.6 0.0 copy-start.2
  7.6 3.2 %collective-permute-start.2 = (f32[160,128]{1,0:T(8,128)S(1)}, f32[160,128]{1,0:T(8,128)S(1)}, u32[]{:S(2)}, u32[]{:S(2)}) collective-permute-start(f32[160,128]{1,0:T(8,128)S(1)} %get-tuple-element.26.up), channel_id=1, source_target_pairs={{0,32},{32,64},{64,96},{96,128},{128,160},{160,192},{192,224},{224... | collective-permute-start | bytes 245768 | tf_op jit(solution)/shard_map/ppermute | solution.py:481
  10.9 0.3 collective-permute-start.3
  11.1 1.2 %collective-permute-done.2.before = f32[160,128]{1,0:T(8,128)S(1)} collective-permute-done((f32[160,128]{1,0:T(8,128)S(1)}, f32[160,128]{1,0:T(8,128)S(1)}, u32[]{:S(2)}, u32[]{:S(2)}) %collective-permute-start.2) | collective-permute-done | bytes 81952 | tf_op jit(solution)/shard_map/ppermute | solution.py:481
  12.3 2.7 %collective-permute-done.3.after = f32[160,128]{1,0:T(8,128)S(1)} collective-permute-done((f32[160,128]{1,0:T(8,128)S(1)}, f32[160,128]{1,0:T(8,128)S(1)}, u32[]{:S(2)}, u32[]{:S(2)}) %collective-permute-start.3) | collective-permute-done | bytes 81952 | tf_op jit(solution)/shard_map/ppermute | solution.py:482
  15.0 0.0 copy-done.2
  15.0 0.0 copy-start.1
  15.0 0.3 width.1
  15.4 0.0 copy-start.3
  15.4 1.4 %collective-permute-start.4 = (f32[184,128]{1,0:T(8,128)S(1)}, f32[184,128]{1,0:T(8,128)S(1)}, u32[]{:S(2)}, u32[]{:S(2)}) collective-permute-start(f32[184,128]{1,0:T(8,128)S(1)} %get-tuple-element.30.yup), channel_id=1, source_target_pairs={{0,4},{4,8},{8,12},{12,16},{16,20},{20,24},{24,28},{28,0},{1,5},{5... | collective-permute-start | bytes 282632 | tf_op jit(solution)/shard_map/ppermute | solution.py:481
  16.7 4.0 %collective-permute-start.5 = (f32[184,128]{1,0:T(8,128)S(1)}, f32[184,128]{1,0:T(8,128)S(1)}, u32[]{:S(2)}, u32[]{:S(2)}) collective-permute-start(f32[184,128]{1,0:T(8,128)S(1)} %get-tuple-element.31.ydown), channel_id=1, source_target_pairs={{4,0},{8,4},{12,8},{16,12},{20,16},{24,20},{28,24},{0,28},{5,1},{9... | collective-permute-start | bytes 282632 | tf_op jit(solution)/shard_map/ppermute | solution.py:482
  20.7 0.0 copy-done.3
  20.8 0.0 copy-done.1
  20.8 1.6 %prepare.1 = (f32[1600,128]{1,0:T(8,128)S(1)}, f32[1600,128]{1,0:T(8,128)S(1)}, f32[1600,128]{1,0:T(8,128)S(1)}) custom-call(f32[1024,128]{1,0:T(8,128)S(1)} %get-tuple-element.24.f, f32[64,128]{1,0:T(8,128)S(1)} %get-tuple-element.29.ez, f32[256,128]{1,0:T(8,128)S(1)} %get-tuple-element.32.xe, f32[32,128]{1,0:T(8,128)S(1)} %get-tuple-element.33.xee, ...), custom_call_target="tpu_custom_call" | custom-call | tf_op jit(solution)/shard_map/prepare/pallas_call | solution.py:493
  22.4 1.2 %collective-permute-done.4.before = f32[184,128]{1,0:T(8,128)S(1)} collective-permute-done((f32[184,128]{1,0:T(8,128)S(1)}, f32[184,128]{1,0:T(8,128)S(1)}, u32[]{:S(2)}, u32[]{:S(2)}) %collective-permute-start.4) | collective-permute-done | bytes 94240 | tf_op jit(solution)/shard_map/ppermute | solution.py:481
  23.6 0.0 collective-permute-done.5.after
  23.7 0.1 broadcast_in_dim.2.th
  23.7 2.5 %levels.1 = (f32[1024,128]{1,0:T(8,128)S(1)}, f32[256,128]{1,0:T(8,128)S(1)}, f32[1600,128]{1,0:T(8,128)S(1)}, f32[1600,128]{1,0:T(8,128)S(1)}, f32[1600,128]{1,0:T(8,128)S(1)}) custom-call(f32[184,128]{1,0:T(8,128)S(1)} %get-tuple-element.30.yup, ...), custom_call_target="tpu_custom_call", output_to_operand_aliasing={{2}: (6, {}), {3}: (7, {}), {4}: (8, {})} | custom-call | tf_op jit(solution)/shard_map/levels/pallas_call | solution.py:493
  26.3 24.0 %all_to_all.5 = f32[256,1,128]{2,1,0:T(1,128)S(1)} all-to-all(f32[256,1,128]{2,1,0:T(1,128)S(1)} %bitcast.8), channel_id=1, replica_groups=mesh['gx'=8,'gy'=8,'gz'=4] {'gx','gy','gz'}, dimensions={0} | all-to-all | bytes 262144 | tf_op jit(solution)/shard_map/all_to_all | solution.py:540
  50.2 1.6 %last.1 = (f32[1024,128]{1,0:T(8,128)}, f32[2,1,5]{2,1,0:T(1,128)}) custom-call(s32[1]{0:T(128)} %bitcast.1.spot, f32[256,128]{1,0:T(8,128)S(1)} %bitcast.7, f32[1024,128]{1,0:T(8,128)S(1)} %get-tuple-element.40.coef, f32[8,128]{1,0:T(8,128)S(1)} %broadcast_in_dim.2.th), custom_call_target="tpu_custom_call" | custom-call | tf_op jit(solution)/shard_map/last/pallas_call | solution.py:541
  (2 shorter events, 0.0 us)
Async XLA Ops:
  0.6 6.7 %copy-start = (f32[1024,128]{1,0:T(8,128)S(1)}, f32[1024,128]{1,0:T(8,128)}, u32[]{:S(2)}) copy-start(f32[1024,128]{1,0:T(8,128)} %constant.31.clone.tables) | copy-start | bytes 1572868
  2.3 4.9 %collective-permute-start = (f32[64,128]{1,0:T(8,128)S(1)}, f32[64,128]{1,0:T(8,128)S(1)}, u32[]{:S(2)}, u32[]{:S(2)}) collective-permute-start(f32[64,128]{1,0:T(8,128)S(1)} %get-tuple-element.23.pz), channel_id=1, source_target_pairs={{0,1},{1,2},{2,3},{3,0},{4,5},{5,6},{6,7},{7,4},{8,9},{9,10},{10,1... | collective-permute-start | bytes 98312 | tf_op jit(solution)/shard_map/ppermute | solution.py:481
  4.5 2.8 %collective-permute-start.1 = (f32[64,128]{1,0:T(8,128)S(1)}, f32[64,128]{1,0:T(8,128)S(1)}, u32[]{:S(2)}, u32[]{:S(2)}) collective-permute-start(f32[64,128]{1,0:T(8,128)S(1)} %get-tuple-element.23.pz), channel_id=1, source_target_pairs={{1,0},{2,1},{3,2},{0,3},{5,4},{6,5},{7,6},{4,7},{9,8},{10,9},{11,1... | collective-permute-start | bytes 98312 | tf_op jit(solution)/shard_map/ppermute | solution.py:482
  7.6 7.4 %copy-start.2 = (f32[8,32]{1,0:T(8,128)S(1)}, f32[8,32]{1,0:T(8,128)}, u32[]{:S(2)}) copy-start(f32[8,32]{1,0:T(8,128)} %constant.33.clone.wy) | copy-start | bytes 3076
  7.6 4.7 %collective-permute-start.2 = (f32[160,128]{1,0:T(8,128)S(1)}, f32[160,128]{1,0:T(8,128)S(1)}, u32[]{:S(2)}, u32[]{:S(2)}) collective-permute-start(f32[160,128]{1,0:T(8,128)S(1)} %get-tuple-element.26.up), channel_id=1, source_target_pairs={{0,32},{32,64},{64,96},{96,128},{128,160},{160,192},{192,224},{224... | collective-permute-start | bytes 245768 | tf_op jit(solution)/shard_map/ppermute | solution.py:481
  10.9 4.2 %collective-permute-start.3 = (f32[160,128]{1,0:T(8,128)S(1)}, f32[160,128]{1,0:T(8,128)S(1)}, u32[]{:S(2)}, u32[]{:S(2)}) collective-permute-start(f32[160,128]{1,0:T(8,128)S(1)} %get-tuple-element.27.down), channel_id=1, source_target_pairs={{32,0},{64,32},{96,64},{128,96},{160,128},{192,160},{224,192},{0,2... | collective-permute-start | bytes 245768 | tf_op jit(solution)/shard_map/ppermute | solution.py:482
  15.0 5.8 %copy-start.1 = (f32[128,256]{1,0:T(8,128)S(1)}, f32[128,256]{1,0:T(8,128)}, u32[]{:S(2)}) copy-start(f32[128,256]{1,0:T(8,128)} %constant.32.clone.spread) | copy-start | bytes 393220
  15.4 5.4 %copy-start.3 = (s32[5]{0:T(128)S(1)}, s32[5]{0:T(128)}, u32[]{:S(2)}) copy-start(s32[5]{0:T(128)} %param.7) | copy-start | bytes 64
  15.4 8.3 %collective-permute-start.4 = (f32[184,128]{1,0:T(8,128)S(1)}, f32[184,128]{1,0:T(8,128)S(1)}, u32[]{:S(2)}, u32[]{:S(2)}) collective-permute-start(f32[184,128]{1,0:T(8,128)S(1)} %get-tuple-element.30.yup), channel_id=1, source_target_pairs={{0,4},{4,8},{8,12},{12,16},{16,20},{20,24},{24,28},{28,0},{1,5},{5... | collective-permute-start | bytes 282632 | tf_op jit(solution)/shard_map/ppermute | solution.py:481
  16.7 6.9 %collective-permute-start.5 = (f32[184,128]{1,0:T(8,128)S(1)}, f32[184,128]{1,0:T(8,128)S(1)}, u32[]{:S(2)}, u32[]{:S(2)}) collective-permute-start(f32[184,128]{1,0:T(8,128)S(1)} %get-tuple-element.31.ydown), channel_id=1, source_target_pairs={{4,0},{8,4},{12,8},{16,12},{20,16},{24,20},{28,24},{0,28},{5,1},{9... | collective-permute-start | bytes 282632 | tf_op jit(solution)/shard_map/ppermute | solution.py:482

commit v9 on v8

--- a/solution.py
+++ b/solution.py
@@ -424,13 +424,17 @@
     top, low = (lane & 7) == 7, (lane & 7) == 0
     far = row % nz == nz - 1
     near = row % nz == 0
-    result = []
-    for a in v:
-        following = jnp.where(far, down(a, nz - 1), down(a, -1))
-        d = a - 0.5 * (roll(a, 1) + jnp.where(top, roll(following, 7), roll(a, -1)))
-        previous = jnp.where(near, down(d, 1 - nz), down(d, 1))
-        s = a + 0.25 * (jnp.where(low, roll(previous, -7), roll(d, 1)) + roll(d, -1))
-        result.append(jnp.where(odd, d, s))
+    left = [roll(a, 1) for a in v]
+    right = [roll(a, -1) for a in v]
+    wrap = [roll(jnp.where(far, down(a, nz - 1), down(a, -1)), 7) for a in v]
+    d = [a - 0.5 * (x + jnp.where(top, w, y)) for a, x, y, w in zip(v, left, right, wrap)]
+    right = [roll(a, -1) for a in d]
+    left = [roll(a, 1) for a in d]
+    wrap = [roll(jnp.where(near, down(a, 1 - nz), down(a, 1)), -7) for a in d]
+    result = [
+        jnp.where(odd, b, a + 0.25 * (jnp.where(low, w, x) + y))
+        for a, b, x, y, w in zip(v, d, left, right, wrap)
+    ]
     bound = th[pl.ds(LEVELS - 1, 1), :]
     detail = (lane < 32) & ((lane & 25) != 0)
     energy = kept = None

time: 51.9 us -> 51.9 us (level)
  no operation moved by 1% of the time
where the time goes in v9:
time: 51.9 us; the launch traced here: 51.8 us
  blocking collectives  24 us (46%)
  starting transfers between devices  12.6 us (24%)
  Pallas kernels  8.51 us (16%)
  waiting for transfers between devices  5.94 us (11%)
  between operations  0.7 us (1%)
    all_to_all x1, blocking collectives, shards(): lax.all_to_all(send.reshape(devices, 1, LANES), ('gx', 'gy', 'gz'), 0, 0)  24 us
    ppermute x3, starting transfers between devices, swap(): before = lax.ppermute(up, axis, [(i, (i + 1) % n) for i in range(n)])  6.78 us
    ppermute x3, starting transfers between devices, swap(): after = lax.ppermute(down, axis, [((i + 1) % n, i) for i in range(n)])  5.81 us
    pallas_call x5, Pallas kernels, local(): pl.pallas_call(kernel, in_specs=[here] * len(args), out_specs=[here] * le...  5.24 us
    ppermute x3, waiting for transfers between devices, swap(): before = lax.ppermute(up, axis, [(i, (i + 1) % n) for i in range(n)])  3.24 us
    ppermute x3, waiting for transfers between devices, swap(): after = lax.ppermute(down, axis, [((i + 1) % n, i) for i in range(n)])  2.7 us
    pallas_call x1, Pallas kernels, shards(): pl.pallas_call(ends_kernel, in_specs=[there] * 2, out_specs=[here] * 2, o...  1.69 us
    pallas_call x1, Pallas kernels, shards(): pl.pallas_call(functools.partial(last_kernel, sizes=sizes, counts=counts)...  1.58 us
  transfers between devices with their start and end apart: 6, of which 4 were waited for; matrix products, arithmetic and copies ran while one was open for 0% of the time, Pallas kernels for 4%

profile of v9, /device:TPU:1, one launch (start us, length us, event | category | flops | bytes accessed | tf_op | source)
XLA Modules:
  0.0 51.8 jit_solution(15679502205034857306)
XLA Ops:
  0.6 0.0 copy-start
  0.6 1.7 %ends.1 = (f32[64,128]{1,0:T(8,128)S(1)}, f32[1024,128]{1,0:T(8,128)S(1)}) custom-call(f32[1024,128]{1,0:T(8,128)} %bitcast.9, f32[128,128]{1,0:T(8,128)} %constant.30.clone.table), custom_call_target="tpu_custom_call" | custom-call | tf_op jit(solution)/shard_map/ends/pallas_call | solution.py:508
  2.3 2.2 %collective-permute-start = (f32[64,128]{1,0:T(8,128)S(1)}, f32[64,128]{1,0:T(8,128)S(1)}, u32[]{:S(2)}, u32[]{:S(2)}) collective-permute-start(f32[64,128]{1,0:T(8,128)S(1)} %get-tuple-element.23.pz), channel_id=1, source_target_pairs={{0,1},{1,2},{2,3},{3,0},{4,5},{5,6},{6,7},{7,4},{8,9},{9,10},{10,1... | collective-permute-start | bytes 98312 | tf_op jit(solution)/shard_map/ppermute | solution.py:485
  4.5 1.5 %collective-permute-start.1 = (f32[64,128]{1,0:T(8,128)S(1)}, f32[64,128]{1,0:T(8,128)S(1)}, u32[]{:S(2)}, u32[]{:S(2)}) collective-permute-start(f32[64,128]{1,0:T(8,128)S(1)} %get-tuple-element.23.pz), channel_id=1, source_target_pairs={{1,0},{2,1},{3,2},{0,3},{5,4},{6,5},{7,6},{4,7},{9,8},{10,9},{11,1... | collective-permute-start | bytes 98312 | tf_op jit(solution)/shard_map/ppermute | solution.py:486
  6.1 0.4 faces.1
  6.5 0.8 %collective-permute-done.before = f32[64,128]{1,0:T(8,128)S(1)} collective-permute-done((f32[64,128]{1,0:T(8,128)S(1)}, f32[64,128]{1,0:T(8,128)S(1)}, u32[]{:S(2)}, u32[]{:S(2)}) %collective-permute-start) | collective-permute-done | bytes 32800 | tf_op jit(solution)/shard_map/ppermute | solution.py:485
  7.3 0.0 collective-permute-done.1.after
  7.3 0.0 copy-done
  7.3 0.3 depth.1
  7.6 0.0 copy-start.2
  7.6 3.2 %collective-permute-start.2 = (f32[160,128]{1,0:T(8,128)S(1)}, f32[160,128]{1,0:T(8,128)S(1)}, u32[]{:S(2)}, u32[]{:S(2)}) collective-permute-start(f32[160,128]{1,0:T(8,128)S(1)} %get-tuple-element.26.up), channel_id=1, source_target_pairs={{0,32},{32,64},{64,96},{96,128},{128,160},{160,192},{192,224},{224... | collective-permute-start | bytes 245768 | tf_op jit(solution)/shard_map/ppermute | solution.py:485
  10.9 0.3 collective-permute-start.3
  11.1 1.2 %collective-permute-done.2.before = f32[160,128]{1,0:T(8,128)S(1)} collective-permute-done((f32[160,128]{1,0:T(8,128)S(1)}, f32[160,128]{1,0:T(8,128)S(1)}, u32[]{:S(2)}, u32[]{:S(2)}) %collective-permute-start.2) | collective-permute-done | bytes 81952 | tf_op jit(solution)/shard_map/ppermute | solution.py:485
  12.3 2.7 %collective-permute-done.3.after = f32[160,128]{1,0:T(8,128)S(1)} collective-permute-done((f32[160,128]{1,0:T(8,128)S(1)}, f32[160,128]{1,0:T(8,128)S(1)}, u32[]{:S(2)}, u32[]{:S(2)}) %collective-permute-start.3) | collective-permute-done | bytes 81952 | tf_op jit(solution)/shard_map/ppermute | solution.py:486
  15.0 0.0 copy-done.2
  15.0 0.0 copy-start.1
  15.0 0.3 width.1
  15.4 0.0 copy-start.3
  15.4 1.4 %collective-permute-start.4 = (f32[184,128]{1,0:T(8,128)S(1)}, f32[184,128]{1,0:T(8,128)S(1)}, u32[]{:S(2)}, u32[]{:S(2)}) collective-permute-start(f32[184,128]{1,0:T(8,128)S(1)} %get-tuple-element.30.yup), channel_id=1, source_target_pairs={{0,4},{4,8},{8,12},{12,16},{16,20},{20,24},{24,28},{28,0},{1,5},{5... | collective-permute-start | bytes 282632 | tf_op jit(solution)/shard_map/ppermute | solution.py:485
  16.7 4.0 %collective-permute-start.5 = (f32[184,128]{1,0:T(8,128)S(1)}, f32[184,128]{1,0:T(8,128)S(1)}, u32[]{:S(2)}, u32[]{:S(2)}) collective-permute-start(f32[184,128]{1,0:T(8,128)S(1)} %get-tuple-element.31.ydown), channel_id=1, source_target_pairs={{4,0},{8,4},{12,8},{16,12},{20,16},{24,20},{28,24},{0,28},{5,1},{9... | collective-permute-start | bytes 282632 | tf_op jit(solution)/shard_map/ppermute | solution.py:486
  20.7 0.0 copy-done.3
  20.8 0.0 copy-done.1
  20.8 1.6 %prepare.1 = (f32[1600,128]{1,0:T(8,128)S(1)}, f32[1600,128]{1,0:T(8,128)S(1)}, f32[1600,128]{1,0:T(8,128)S(1)}) custom-call(f32[1024,128]{1,0:T(8,128)S(1)} %get-tuple-element.24.f, f32[64,128]{1,0:T(8,128)S(1)} %get-tuple-element.29.ez, f32[256,128]{1,0:T(8,128)S(1)} %get-tuple-element.32.xe, f32[32,128]{1,0:T(8,128)S(1)} %get-tuple-element.33.xee, ...), custom_call_target="tpu_custom_call" | custom-call | tf_op jit(solution)/shard_map/prepare/pallas_call | solution.py:497
  22.4 1.2 %collective-permute-done.4.before = f32[184,128]{1,0:T(8,128)S(1)} collective-permute-done((f32[184,128]{1,0:T(8,128)S(1)}, f32[184,128]{1,0:T(8,128)S(1)}, u32[]{:S(2)}, u32[]{:S(2)}) %collective-permute-start.4) | collective-permute-done | bytes 94240 | tf_op jit(solution)/shard_map/ppermute | solution.py:485
  23.6 0.0 collective-permute-done.5.after
  23.7 0.1 broadcast_in_dim.2.th
  23.7 2.5 %levels.1 = (f32[1024,128]{1,0:T(8,128)S(1)}, f32[256,128]{1,0:T(8,128)S(1)}, f32[1600,128]{1,0:T(8,128)S(1)}, f32[1600,128]{1,0:T(8,128)S(1)}, f32[1600,128]{1,0:T(8,128)S(1)}) custom-call(f32[184,128]{1,0:T(8,128)S(1)} %get-tuple-element.30.yup, ...), custom_call_target="tpu_custom_call", output_to_operand_aliasing={{2}: (6, {}), {3}: (7, {}), {4}: (8, {})} | custom-call | tf_op jit(solution)/shard_map/levels/pallas_call | solution.py:497
  26.3 24.0 %all_to_all.5 = f32[256,1,128]{2,1,0:T(1,128)S(1)} all-to-all(f32[256,1,128]{2,1,0:T(1,128)S(1)} %bitcast.8), channel_id=1, replica_groups=mesh['gx'=8,'gy'=8,'gz'=4] {'gx','gy','gz'}, dimensions={0} | all-to-all | bytes 262144 | tf_op jit(solution)/shard_map/all_to_all | solution.py:544
  50.2 1.6 %last.1 = (f32[1024,128]{1,0:T(8,128)}, f32[2,1,5]{2,1,0:T(1,128)}) custom-call(s32[1]{0:T(128)} %bitcast.1.spot, f32[256,128]{1,0:T(8,128)S(1)} %bitcast.7, f32[1024,128]{1,0:T(8,128)S(1)} %get-tuple-element.40.coef, f32[8,128]{1,0:T(8,128)S(1)} %broadcast_in_dim.2.th), custom_call_target="tpu_custom_call" | custom-call | tf_op jit(solution)/shard_map/last/pallas_call | solution.py:545
  (2 shorter events, 0.0 us)
Async XLA Ops:
  0.6 6.7 %copy-start = (f32[1024,128]{1,0:T(8,128)S(1)}, f32[1024,128]{1,0:T(8,128)}, u32[]{:S(2)}) copy-start(f32[1024,128]{1,0:T(8,128)} %constant.31.clone.tables) | copy-start | bytes 1572868
  2.3 4.9 %collective-permute-start = (f32[64,128]{1,0:T(8,128)S(1)}, f32[64,128]{1,0:T(8,128)S(1)}, u32[]{:S(2)}, u32[]{:S(2)}) collective-permute-start(f32[64,128]{1,0:T(8,128)S(1)} %get-tuple-element.23.pz), channel_id=1, source_target_pairs={{0,1},{1,2},{2,3},{3,0},{4,5},{5,6},{6,7},{7,4},{8,9},{9,10},{10,1... | collective-permute-start | bytes 98312 | tf_op jit(solution)/shard_map/ppermute | solution.py:485
  4.5 2.8 %collective-permute-start.1 = (f32[64,128]{1,0:T(8,128)S(1)}, f32[64,128]{1,0:T(8,128)S(1)}, u32[]{:S(2)}, u32[]{:S(2)}) collective-permute-start(f32[64,128]{1,0:T(8,128)S(1)} %get-tuple-element.23.pz), channel_id=1, source_target_pairs={{1,0},{2,1},{3,2},{0,3},{5,4},{6,5},{7,6},{4,7},{9,8},{10,9},{11,1... | collective-permute-start | bytes 98312 | tf_op jit(solution)/shard_map/ppermute | solution.py:486
  7.6 7.4 %copy-start.2 = (f32[8,32]{1,0:T(8,128)S(1)}, f32[8,32]{1,0:T(8,128)}, u32[]{:S(2)}) copy-start(f32[8,32]{1,0:T(8,128)} %constant.33.clone.wy) | copy-start | bytes 3076
  7.6 4.7 %collective-permute-start.2 = (f32[160,128]{1,0:T(8,128)S(1)}, f32[160,128]{1,0:T(8,128)S(1)}, u32[]{:S(2)}, u32[]{:S(2)}) collective-permute-start(f32[160,128]{1,0:T(8,128)S(1)} %get-tuple-element.26.up), channel_id=1, source_target_pairs={{0,32},{32,64},{64,96},{96,128},{128,160},{160,192},{192,224},{224... | collective-permute-start | bytes 245768 | tf_op jit(solution)/shard_map/ppermute | solution.py:485
  10.9 4.2 %collective-permute-start.3 = (f32[160,128]{1,0:T(8,128)S(1)}, f32[160,128]{1,0:T(8,128)S(1)}, u32[]{:S(2)}, u32[]{:S(2)}) collective-permute-start(f32[160,128]{1,0:T(8,128)S(1)} %get-tuple-element.27.down), channel_id=1, source_target_pairs={{32,0},{64,32},{96,64},{128,96},{160,128},{192,160},{224,192},{0,2... | collective-permute-start | bytes 245768 | tf_op jit(solution)/shard_map/ppermute | solution.py:486
  15.0 5.8 %copy-start.1 = (f32[128,256]{1,0:T(8,128)S(1)}, f32[128,256]{1,0:T(8,128)}, u32[]{:S(2)}) copy-start(f32[128,256]{1,0:T(8,128)} %constant.32.clone.spread) | copy-start | bytes 393220
  15.4 5.4 %copy-start.3 = (s32[5]{0:T(128)S(1)}, s32[5]{0:T(128)}, u32[]{:S(2)}) copy-start(s32[5]{0:T(128)} %param.7) | copy-start | bytes 64
  15.4 8.3 %collective-permute-start.4 = (f32[184,128]{1,0:T(8,128)S(1)}, f32[184,128]{1,0:T(8,128)S(1)}, u32[]{:S(2)}, u32[]{:S(2)}) collective-permute-start(f32[184,128]{1,0:T(8,128)S(1)} %get-tuple-element.30.yup), channel_id=1, source_target_pairs={{0,4},{4,8},{8,12},{12,16},{16,20},{20,24},{24,28},{28,0},{1,5},{5... | collective-permute-start | bytes 282632 | tf_op jit(solution)/shard_map/ppermute | solution.py:485
  16.7 6.9 %collective-permute-start.5 = (f32[184,128]{1,0:T(8,128)S(1)}, f32[184,128]{1,0:T(8,128)S(1)}, u32[]{:S(2)}, u32[]{:S(2)}) collective-permute-start(f32[184,128]{1,0:T(8,128)S(1)} %get-tuple-element.31.ydown), channel_id=1, source_target_pairs={{4,0},{8,4},{12,8},{16,12},{20,16},{24,20},{28,24},{0,28},{5,1},{9... | collective-permute-start | bytes 282632 | tf_op jit(solution)/shard_map/ppermute | solution.py:486

commit v10 on v7

--- a/solution.py
+++ b/solution.py
@@ -238,7 +238,7 @@
 
 def lane_rows(level, pieces):
     step = 1 << level
-    planes = list(range(0, SIDE, step)) + (list(range(SIDE, PITCH)) if level < NEAR - 1 else [])
+    planes = list(range(0, SIDE, step)) + [SIDE + g for g in range(EXT) if g % NEAR > level]
     return [
         (pl.ds(x * PITCH + first, count, stride=stride), count)
         for x in planes

time: 51.9 us -> 51.9 us (level)
  no operation moved by 1% of the time
where the time goes in v10:
time: 51.9 us; the launch traced here: 51.8 us
  blocking collectives  24 us (46%)
  starting transfers between devices  12.6 us (24%)
  Pallas kernels  8.48 us (16%)
  waiting for transfers between devices  5.96 us (11%)
  between operations  0.7 us (1%)
    all_to_all x1, blocking collectives, shards(): lax.all_to_all(send.reshape(devices, 1, LANES), ('gx', 'gy', 'gz'), 0, 0)  24 us
    ppermute x3, starting transfers between devices, swap(): before = lax.ppermute(up, axis, [(i, (i + 1) % n) for i in range(n)])  6.78 us
    ppermute x3, starting transfers between devices, swap(): after = lax.ppermute(down, axis, [((i + 1) % n, i) for i in range(n)])  5.81 us
    pallas_call x5, Pallas kernels, local(): pl.pallas_call(kernel, in_specs=[here] * len(args), out_specs=[here] * le...  5.2 us
    ppermute x3, waiting for transfers between devices, swap(): before = lax.ppermute(up, axis, [(i, (i + 1) % n) for i in range(n)])  3.26 us
    ppermute x3, waiting for transfers between devices, swap(): after = lax.ppermute(down, axis, [((i + 1) % n, i) for i in range(n)])  2.7 us
    pallas_call x1, Pallas kernels, shards(): pl.pallas_call(ends_kernel, in_specs=[there] * 2, out_specs=[here] * 2, o...  1.69 us
    pallas_call x1, Pallas kernels, shards(): pl.pallas_call(functools.partial(last_kernel, sizes=sizes, counts=counts)...  1.58 us
  transfers between devices with their start and end apart: 6, of which 4 were waited for; matrix products, arithmetic and copies ran while one was open for 0% of the time, Pallas kernels for 4%

profile of v10, /device:TPU:1, one launch (start us, length us, event | category | flops | bytes accessed | tf_op | source)
XLA Modules:
  0.0 51.8 jit_solution(17182348818528682358)
XLA Ops:
  0.6 0.0 copy-start
  0.6 1.7 %ends.1 = (f32[64,128]{1,0:T(8,128)S(1)}, f32[1024,128]{1,0:T(8,128)S(1)}) custom-call(f32[1024,128]{1,0:T(8,128)} %bitcast.9, f32[128,128]{1,0:T(8,128)} %constant.30.clone.table), custom_call_target="tpu_custom_call" | custom-call | tf_op jit(solution)/shard_map/ends/pallas_call | solution.py:505
  2.3 2.2 %collective-permute-start = (f32[64,128]{1,0:T(8,128)S(1)}, f32[64,128]{1,0:T(8,128)S(1)}, u32[]{:S(2)}, u32[]{:S(2)}) collective-permute-start(f32[64,128]{1,0:T(8,128)S(1)} %get-tuple-element.23.pz), channel_id=1, source_target_pairs={{0,1},{1,2},{2,3},{3,0},{4,5},{5,6},{6,7},{7,4},{8,9},{9,10},{10,1... | collective-permute-start | bytes 98312 | tf_op jit(solution)/shard_map/ppermute | solution.py:482
  4.5 1.5 %collective-permute-start.1 = (f32[64,128]{1,0:T(8,128)S(1)}, f32[64,128]{1,0:T(8,128)S(1)}, u32[]{:S(2)}, u32[]{:S(2)}) collective-permute-start(f32[64,128]{1,0:T(8,128)S(1)} %get-tuple-element.23.pz), channel_id=1, source_target_pairs={{1,0},{2,1},{3,2},{0,3},{5,4},{6,5},{7,6},{4,7},{9,8},{10,9},{11,1... | collective-permute-start | bytes 98312 | tf_op jit(solution)/shard_map/ppermute | solution.py:483
  6.1 0.4 faces.1
  6.5 0.8 %collective-permute-done.before = f32[64,128]{1,0:T(8,128)S(1)} collective-permute-done((f32[64,128]{1,0:T(8,128)S(1)}, f32[64,128]{1,0:T(8,128)S(1)}, u32[]{:S(2)}, u32[]{:S(2)}) %collective-permute-start) | collective-permute-done | bytes 32800 | tf_op jit(solution)/shard_map/ppermute | solution.py:482
  7.3 0.0 collective-permute-done.1.after
  7.3 0.0 copy-done
  7.3 0.3 depth.1
  7.6 0.0 copy-start.2
  7.6 3.2 %collective-permute-start.2 = (f32[160,128]{1,0:T(8,128)S(1)}, f32[160,128]{1,0:T(8,128)S(1)}, u32[]{:S(2)}, u32[]{:S(2)}) collective-permute-start(f32[160,128]{1,0:T(8,128)S(1)} %get-tuple-element.26.up), channel_id=1, source_target_pairs={{0,32},{32,64},{64,96},{96,128},{128,160},{160,192},{192,224},{224... | collective-permute-start | bytes 245768 | tf_op jit(solution)/shard_map/ppermute | solution.py:482
  10.9 0.3 collective-permute-start.3
  11.1 1.2 %collective-permute-done.2.before = f32[160,128]{1,0:T(8,128)S(1)} collective-permute-done((f32[160,128]{1,0:T(8,128)S(1)}, f32[160,128]{1,0:T(8,128)S(1)}, u32[]{:S(2)}, u32[]{:S(2)}) %collective-permute-start.2) | collective-permute-done | bytes 81952 | tf_op jit(solution)/shard_map/ppermute | solution.py:482
  12.3 2.7 %collective-permute-done.3.after = f32[160,128]{1,0:T(8,128)S(1)} collective-permute-done((f32[160,128]{1,0:T(8,128)S(1)}, f32[160,128]{1,0:T(8,128)S(1)}, u32[]{:S(2)}, u32[]{:S(2)}) %collective-permute-start.3) | collective-permute-done | bytes 81952 | tf_op jit(solution)/shard_map/ppermute | solution.py:483
  15.0 0.0 copy-done.2
  15.0 0.0 copy-start.1
  15.0 0.3 width.1
  15.4 0.0 copy-start.3
  15.4 1.4 %collective-permute-start.4 = (f32[184,128]{1,0:T(8,128)S(1)}, f32[184,128]{1,0:T(8,128)S(1)}, u32[]{:S(2)}, u32[]{:S(2)}) collective-permute-start(f32[184,128]{1,0:T(8,128)S(1)} %get-tuple-element.30.yup), channel_id=1, source_target_pairs={{0,4},{4,8},{8,12},{12,16},{16,20},{20,24},{24,28},{28,0},{1,5},{5... | collective-permute-start | bytes 282632 | tf_op jit(solution)/shard_map/ppermute | solution.py:482
  16.7 4.0 %collective-permute-start.5 = (f32[184,128]{1,0:T(8,128)S(1)}, f32[184,128]{1,0:T(8,128)S(1)}, u32[]{:S(2)}, u32[]{:S(2)}) collective-permute-start(f32[184,128]{1,0:T(8,128)S(1)} %get-tuple-element.31.ydown), channel_id=1, source_target_pairs={{4,0},{8,4},{12,8},{16,12},{20,16},{24,20},{28,24},{0,28},{5,1},{9... | collective-permute-start | bytes 282632 | tf_op jit(solution)/shard_map/ppermute | solution.py:483
  20.7 0.0 copy-done.3
  20.8 0.0 copy-done.1
  20.8 1.6 %prepare.1 = (f32[1600,128]{1,0:T(8,128)S(1)}, f32[1600,128]{1,0:T(8,128)S(1)}, f32[1600,128]{1,0:T(8,128)S(1)}) custom-call(f32[1024,128]{1,0:T(8,128)S(1)} %get-tuple-element.24.f, f32[64,128]{1,0:T(8,128)S(1)} %get-tuple-element.29.ez, f32[256,128]{1,0:T(8,128)S(1)} %get-tuple-element.32.xe, f32[32,128]{1,0:T(8,128)S(1)} %get-tuple-element.33.xee, ...), custom_call_target="tpu_custom_call" | custom-call | tf_op jit(solution)/shard_map/prepare/pallas_call | solution.py:494
  22.4 1.3 %collective-permute-done.4.before = f32[184,128]{1,0:T(8,128)S(1)} collective-permute-done((f32[184,128]{1,0:T(8,128)S(1)}, f32[184,128]{1,0:T(8,128)S(1)}, u32[]{:S(2)}, u32[]{:S(2)}) %collective-permute-start.4) | collective-permute-done | bytes 94240 | tf_op jit(solution)/shard_map/ppermute | solution.py:482
  23.6 0.0 collective-permute-done.5.after
  23.7 0.1 broadcast_in_dim.2.th
  23.7 2.5 %levels.1 = (f32[1024,128]{1,0:T(8,128)S(1)}, f32[256,128]{1,0:T(8,128)S(1)}, f32[1600,128]{1,0:T(8,128)S(1)}, f32[1600,128]{1,0:T(8,128)S(1)}, f32[1600,128]{1,0:T(8,128)S(1)}) custom-call(f32[184,128]{1,0:T(8,128)S(1)} %get-tuple-element.30.yup, ...), custom_call_target="tpu_custom_call", output_to_operand_aliasing={{2}: (6, {}), {3}: (7, {}), {4}: (8, {})} | custom-call | tf_op jit(solution)/shard_map/levels/pallas_call | solution.py:494
  26.2 24.0 %all_to_all.5 = f32[256,1,128]{2,1,0:T(1,128)S(1)} all-to-all(f32[256,1,128]{2,1,0:T(1,128)S(1)} %bitcast.8), channel_id=1, replica_groups=mesh['gx'=8,'gy'=8,'gz'=4] {'gx','gy','gz'}, dimensions={0} | all-to-all | bytes 262144 | tf_op jit(solution)/shard_map/all_to_all | solution.py:541
  50.2 1.6 %last.1 = (f32[1024,128]{1,0:T(8,128)}, f32[2,1,5]{2,1,0:T(1,128)}) custom-call(s32[1]{0:T(128)} %bitcast.1.spot, f32[256,128]{1,0:T(8,128)S(1)} %bitcast.7, f32[1024,128]{1,0:T(8,128)S(1)} %get-tuple-element.40.coef, f32[8,128]{1,0:T(8,128)S(1)} %broadcast_in_dim.2.th), custom_call_target="tpu_custom_call" | custom-call | tf_op jit(solution)/shard_map/last/pallas_call | solution.py:542
  (2 shorter events, 0.0 us)
Async XLA Ops:
  0.6 6.7 %copy-start = (f32[1024,128]{1,0:T(8,128)S(1)}, f32[1024,128]{1,0:T(8,128)}, u32[]{:S(2)}) copy-start(f32[1024,128]{1,0:T(8,128)} %constant.31.clone.tables) | copy-start | bytes 1572868
  2.3 4.9 %collective-permute-start = (f32[64,128]{1,0:T(8,128)S(1)}, f32[64,128]{1,0:T(8,128)S(1)}, u32[]{:S(2)}, u32[]{:S(2)}) collective-permute-start(f32[64,128]{1,0:T(8,128)S(1)} %get-tuple-element.23.pz), channel_id=1, source_target_pairs={{0,1},{1,2},{2,3},{3,0},{4,5},{5,6},{6,7},{7,4},{8,9},{9,10},{10,1... | collective-permute-start | bytes 98312 | tf_op jit(solution)/shard_map/ppermute | solution.py:482
  4.5 2.8 %collective-permute-start.1 = (f32[64,128]{1,0:T(8,128)S(1)}, f32[64,128]{1,0:T(8,128)S(1)}, u32[]{:S(2)}, u32[]{:S(2)}) collective-permute-start(f32[64,128]{1,0:T(8,128)S(1)} %get-tuple-element.23.pz), channel_id=1, source_target_pairs={{1,0},{2,1},{3,2},{0,3},{5,4},{6,5},{7,6},{4,7},{9,8},{10,9},{11,1... | collective-permute-start | bytes 98312 | tf_op jit(solution)/shard_map/ppermute | solution.py:483
  7.6 7.4 %copy-start.2 = (f32[8,32]{1,0:T(8,128)S(1)}, f32[8,32]{1,0:T(8,128)}, u32[]{:S(2)}) copy-start(f32[8,32]{1,0:T(8,128)} %constant.33.clone.wy) | copy-start | bytes 3076
  7.6 4.7 %collective-permute-start.2 = (f32[160,128]{1,0:T(8,128)S(1)}, f32[160,128]{1,0:T(8,128)S(1)}, u32[]{:S(2)}, u32[]{:S(2)}) collective-permute-start(f32[160,128]{1,0:T(8,128)S(1)} %get-tuple-element.26.up), channel_id=1, source_target_pairs={{0,32},{32,64},{64,96},{96,128},{128,160},{160,192},{192,224},{224... | collective-permute-start | bytes 245768 | tf_op jit(solution)/shard_map/ppermute | solution.py:482
  10.9 4.2 %collective-permute-start.3 = (f32[160,128]{1,0:T(8,128)S(1)}, f32[160,128]{1,0:T(8,128)S(1)}, u32[]{:S(2)}, u32[]{:S(2)}) collective-permute-start(f32[160,128]{1,0:T(8,128)S(1)} %get-tuple-element.27.down), channel_id=1, source_target_pairs={{32,0},{64,32},{96,64},{128,96},{160,128},{192,160},{224,192},{0,2... | collective-permute-start | bytes 245768 | tf_op jit(solution)/shard_map/ppermute | solution.py:483
  15.0 5.8 %copy-start.1 = (f32[128,256]{1,0:T(8,128)S(1)}, f32[128,256]{1,0:T(8,128)}, u32[]{:S(2)}) copy-start(f32[128,256]{1,0:T(8,128)} %constant.32.clone.spread) | copy-start | bytes 393220
  15.4 5.4 %copy-start.3 = (s32[5]{0:T(128)S(1)}, s32[5]{0:T(128)}, u32[]{:S(2)}) copy-start(s32[5]{0:T(128)} %param.7) | copy-start | bytes 64
  15.4 8.3 %collective-permute-start.4 = (f32[184,128]{1,0:T(8,128)S(1)}, f32[184,128]{1,0:T(8,128)S(1)}, u32[]{:S(2)}, u32[]{:S(2)}) collective-permute-start(f32[184,128]{1,0:T(8,128)S(1)} %get-tuple-element.30.yup), channel_id=1, source_target_pairs={{0,4},{4,8},{8,12},{12,16},{16,20},{20,24},{24,28},{28,0},{1,5},{5... | collective-permute-start | bytes 282632 | tf_op jit(solution)/shard_map/ppermute | solution.py:482
  16.7 6.9 %collective-permute-start.5 = (f32[184,128]{1,0:T(8,128)S(1)}, f32[184,128]{1,0:T(8,128)S(1)}, u32[]{:S(2)}, u32[]{:S(2)}) collective-permute-start(f32[184,128]{1,0:T(8,128)S(1)} %get-tuple-element.31.ydown), channel_id=1, source_target_pairs={{4,0},{8,4},{12,8},{16,12},{20,16},{24,20},{28,24},{0,28},{5,1},{9... | collective-permute-start | bytes 282632 | tf_op jit(solution)/shard_map/ppermute | solution.py:483
